TPU v7x, 32 devices: a whole 2x2x4 slice. The times are simulated.
32 devices in a mesh: dp: 4 (over y, core), expert: 8 (over z, x).
Axes of the slice: x: 2, y: 2, z: 4, core: 2. Of those that a mesh axis runs over, the one named last changes fastest.
Arguments:
- inputs: bfloat16 [4096, 1536], P(('dp', 'expert')), may hold values from -6 to 6
- segment_ids: int32 [32, 128], P(('dp', 'expert')), may hold values from 0 to 3, never falling along the last dimension, each value on 1 to 64 neighbouring positions
- routes: int32 [4096, 8], P(('dp', 'expert')), may hold values from 0 to 39, all different within a row; in each aligned block of 128 rows (0 to 127, 128 to 255, ...) at most 28 rows name the same one
- expert_blocks: int32 [40], replicated, may hold values from 6 to 7, as said below
- norm1_gain: bfloat16 [1536], P('dp'), may hold values from 0.5 to 1.5
- q_weight: bfloat16 [1536, 1536], P('dp')
- k_weight: bfloat16 [1536, 512], P('dp')
- value_matrix: bfloat16 [1536, 512], P('dp'), may hold values from -0.15625 to 0.15625
- o_weight: bfloat16 [1536, 1536], P('dp'), may hold values from -3 to 3
- norm2_gain: bfloat16 [1536], P('dp'), may hold values from 0.5 to 1.5
- router_weight: bfloat16 [1536, 40], P('dp')
- expert_gate_up: bfloat16 [40, 1536, 1024], P('expert'), may hold values from -0.3125 to 0.3125
- expert_down: bfloat16 [40, 512, 1536], P('expert'), may hold values from -3 to 3
- out_grad: bfloat16 [4096, 1536], P(('dp', 'expert')), may hold values from -6 to 6
Outputs:
- output: bfloat16 [4096, 1536], P(('dp', 'expert'))
- grad_inputs: float32 [4096, 1536], P(('dp', 'expert'))
- grad_norm1_gain: float32 [1536], P('dp')
- grad_q_weight: float32 [1536, 1536], P('dp')
- grad_k_weight: float32 [1536, 512], P('dp')
- grad_v_weight: float32 [1536, 512], P('dp')
- grad_o_weight: float32 [1536, 1536], P('dp')
- grad_norm2_gain: float32 [1536], P('dp')
- grad_router_weight: float32 [1536, 40], P('dp')
- grad_expert_gate_up: float32 [40, 1536, 1024], P('expert', 'dp')
- grad_expert_down: float32 [40, 512, 1536], P('expert', None, 'dp')
Inputs may be any that keep to these rules, and one draw needn't show every extreme that they name: `segment_ids`: in each sequence the ids never fall and take every value; a document spans 1 to 64 positions, and in every sequence one document spans exactly 64. The 8 routes of a token name different experts. Among the 128 tokens of one sequence no expert is named more than 28 times, and in some sequences one is named exactly 28 times. `expert_blocks`: both values occur.
All inputs are finite; a program needn't handle non-finite values.
Results may differ from a plain program's by a relative error of at most 0.015.
The roundings to bfloat16 on the way count: a program that leaves them out, or rounds other values in their place, can miss the bound.
Values may be sent and summed in bfloat16 or wider, within the bound.
A program may use at most 256 MiB of HBM per device.

v0:
```python
import jax
import jax.numpy as jnp
from jax import lax
from jax.sharding import PartitionSpec as P

QUERY_HEADS = 24
KEY_VALUE_HEADS = 8
HEAD_DIMENSION = 64
EXPERT_COUNT = 40
BLK = 4
CAP = 28


NORM_EPSILON = 1e-06
SCORE_SCALE = 0.015625
RESIDUAL_SCALE = 0.22
ROPE_BASE = 10000.0
MASKED_SCORE = -1e30


def rope_tables(sequence_length, head_size):
    positions = jnp.arange(sequence_length, dtype=jnp.float32)
    frequency = ROPE_BASE ** (-(jnp.arange(head_size // 2, dtype=jnp.float32) * 2.0) / head_size)
    angles = positions[:, None] * frequency[None, :]
    return (jnp.cos(angles)[:, None, :], jnp.sin(angles)[:, None, :])


def apply_rotary(tensor, cosine_lookup, sine_lookup):
    half_size = tensor.shape[-1] // 2
    front_half = tensor[..., :half_size]
    back_half = tensor[..., half_size:]
    return jnp.concatenate(
        [
            front_half * cosine_lookup - back_half * sine_lookup,
            back_half * cosine_lookup + front_half * sine_lookup,
        ],
        axis=-1,
    )


def inverse_rotary(tensor, cosine_lookup, sine_lookup):
    half_size = tensor.shape[-1] // 2
    front_half = tensor[..., :half_size]
    back_half = tensor[..., half_size:]
    return jnp.concatenate(
        [
            front_half * cosine_lookup + back_half * sine_lookup,
            back_half * cosine_lookup - front_half * sine_lookup,
        ],
        axis=-1,
    )


def norm_stats(values):
    norm_scale = lax.rsqrt(jnp.mean(values * values, axis=-1, keepdims=True) + NORM_EPSILON)
    return (values * norm_scale, norm_scale)


def norm_back(grad_out, normed, norm_scale, gain_values):
    grad_hat = grad_out * gain_values
    grad_in = norm_scale * (grad_hat - normed * jnp.mean(grad_hat * normed, axis=-1, keepdims=True))
    return (grad_in, jnp.sum(grad_out * normed, axis=0))


def masked_scores(query_rows, rows_of_keys, segments, block_start):
    rows_here = query_rows.shape[0]
    scores = (
        jnp.einsum("qhgd,khd->hgqk", query_rows, rows_of_keys, preferred_element_type=jnp.float32)
        * SCORE_SCALE
    )
    row_pos = block_start + jnp.arange(rows_here, dtype=jnp.int32)
    col_pos = jnp.arange(rows_of_keys.shape[0], dtype=jnp.int32)
    allowed = (col_pos[None, :] <= row_pos[:, None]) & (segments[:, None] == segments[None, :])
    return jnp.where(allowed, scores, MASKED_SCORE)


def route_rows(seq_routes, expert_blocks):
    flat_routes = seq_routes.reshape(-1)
    onehot_table = (
        flat_routes[:, None] == jnp.arange(EXPERT_COUNT, dtype=jnp.int32)[None, :]
    ).astype(jnp.int32)
    row_rank = jnp.sum((jnp.cumsum(onehot_table, axis=0) - onehot_table) * onehot_table, axis=1)
    row_limit = jnp.sum(onehot_table * expert_blocks[None, :], axis=1) * BLK
    return (flat_routes, onehot_table, row_rank, row_rank < row_limit)


def on_device(
    inputs,
    segment_ids,
    routes,
    expert_blocks,
    norm1_gain,
    q_weight,
    k_weight,
    value_matrix,
    o_weight,
    norm2_gain,
    router_weight,
    expert_gate_up,
    expert_down,
    out_grad,
):
    (
        gain_one,
        weight_q,
        key_projection_weight,
        value_projection_weight,
        output_projection_weight,
        gain_two,
        weight_router,
    ) = (
        lax.all_gather(norm1_gain, "dp", axis=0, tiled=True),
        lax.all_gather(q_weight, "dp", axis=0, tiled=True),
        lax.all_gather(k_weight, "dp", axis=0, tiled=True),
        lax.all_gather(value_matrix, "dp", axis=0, tiled=True),
        lax.all_gather(o_weight, "dp", axis=0, tiled=True),
        lax.all_gather(norm2_gain, "dp", axis=0, tiled=True),
        lax.all_gather(router_weight, "dp", axis=0, tiled=True),
    )
    sequence_length, model_width = inputs.shape
    top_count = routes.shape[1]
    head_groups = QUERY_HEADS // KEY_VALUE_HEADS
    hidden_size = expert_down.shape[1]
    expert_slots = expert_gate_up.shape[0]
    owners = lax.axis_size("expert")
    segments = segment_ids[0]
    rows_per_block = min(512, sequence_length)
    count_of_blocks = sequence_length // rows_per_block
    block_starts = jnp.arange(count_of_blocks, dtype=jnp.int32) * rows_per_block
    input_float = inputs.astype(jnp.float32)
    gain_first = gain_one.astype(jnp.float32)
    gain_second = gain_two.astype(jnp.float32)
    normed_one, scale_one = norm_stats(input_float)
    input_before_norm = (normed_one * gain_first).astype(jnp.bfloat16)
    cosine_lookup, sine_lookup = rope_tables(sequence_length, HEAD_DIMENSION)
    query_rows = apply_rotary(
        jnp.dot(input_before_norm, weight_q, preferred_element_type=jnp.float32).reshape(
            sequence_length, QUERY_HEADS, HEAD_DIMENSION
        ),
        cosine_lookup,
        sine_lookup,
    ).astype(jnp.bfloat16)
    rows_of_keys = apply_rotary(
        jnp.dot(
            input_before_norm, key_projection_weight, preferred_element_type=jnp.float32
        ).reshape(sequence_length, KEY_VALUE_HEADS, HEAD_DIMENSION),
        cosine_lookup,
        sine_lookup,
    ).astype(jnp.bfloat16)
    rows_of_values = (
        jnp.dot(input_before_norm, value_projection_weight, preferred_element_type=jnp.float32)
        .reshape(sequence_length, KEY_VALUE_HEADS, HEAD_DIMENSION)
        .astype(jnp.bfloat16)
    )
    blocks_of_queries = query_rows.reshape(
        count_of_blocks, rows_per_block, KEY_VALUE_HEADS, head_groups, HEAD_DIMENSION
    )

    def attend_block(pieces):
        query_block, block_start = pieces
        scores = masked_scores(query_block, rows_of_keys, segments, block_start)
        row_max = jnp.max(scores, axis=-1, keepdims=True)
        log_total = row_max + jnp.log(jnp.sum(jnp.exp(scores - row_max), axis=-1, keepdims=True))
        probs = jnp.exp(scores - log_total).astype(jnp.bfloat16)
        attended_block = jnp.einsum(
            "hgqk,khd->qhgd", probs, rows_of_values, preferred_element_type=jnp.float32
        ).astype(jnp.bfloat16)
        return (attended_block, log_total)

    attended, log_totals = lax.map(attend_block, (blocks_of_queries, block_starts))
    attended_flat = attended.reshape(sequence_length, QUERY_HEADS * HEAD_DIMENSION)
    hidden = input_float + RESIDUAL_SCALE * jnp.dot(
        attended_flat, output_projection_weight, preferred_element_type=jnp.float32
    )
    normed_two, scale_two = norm_stats(hidden)
    norm_hidden = (normed_two * gain_second).astype(jnp.bfloat16)
    router_probs = jax.nn.softmax(
        jnp.dot(norm_hidden, weight_router, preferred_element_type=jnp.float32), axis=-1
    )
    flat_routes, onehot_table, row_rank, retained = route_rows(routes, expert_blocks)
    table_three = onehot_table.reshape(sequence_length, top_count, EXPERT_COUNT).astype(jnp.float32)
    gate_prob = jnp.sum(table_three * router_probs[:, None, :], axis=2)
    keep_three = retained.reshape(sequence_length, top_count)
    mixing = jnp.where(keep_three, gate_prob, 0.0)
    total_rows = owners * expert_slots * CAP
    target = jnp.where(
        retained,
        (flat_routes % owners * expert_slots + flat_routes // owners) * CAP + row_rank,
        total_rows,
    )
    safe_slot = jnp.minimum(target, total_rows - 1)
    source_rows = jnp.repeat(norm_hidden, top_count, axis=0)
    send_rows = (
        jnp.zeros((total_rows, model_width), jnp.bfloat16)
        .at[target]
        .set(source_rows, mode="drop")
        .reshape(owners, expert_slots, CAP, model_width)
    )
    received = lax.all_to_all(send_rows, "expert", split_axis=0, concat_axis=0, tiled=True)
    gate_up = jnp.einsum(
        "jscd,sdf->jscf", received, expert_gate_up, preferred_element_type=jnp.float32
    )
    gate_part = gate_up[..., :hidden_size]
    up_part = gate_up[..., hidden_size:]
    inner_act = (jax.nn.silu(gate_part) * up_part).astype(jnp.bfloat16)
    produced = jnp.einsum(
        "jsch,shd->jscd", inner_act, expert_down, preferred_element_type=jnp.float32
    ).astype(jnp.bfloat16)
    returned = lax.all_to_all(produced, "expert", split_axis=0, concat_axis=0, tiled=True)
    out_rows = (
        returned.reshape(total_rows, model_width)[safe_slot]
        .reshape(sequence_length, top_count, model_width)
        .astype(jnp.float32)
    )
    mixture = jnp.sum(mixing[..., None] * out_rows, axis=1)
    output = (hidden + RESIDUAL_SCALE * mixture).astype(jnp.bfloat16)
    grad_y = out_grad.astype(jnp.float32)
    grad_mix = RESIDUAL_SCALE * grad_y
    grad_gate = jnp.where(keep_three, jnp.sum(grad_mix[:, None, :] * out_rows, axis=2), 0.0)
    grad_rows = (
        (mixing[..., None] * grad_mix[:, None, :])
        .astype(jnp.bfloat16)
        .reshape(sequence_length * top_count, model_width)
    )
    grad_send = (
        jnp.zeros((total_rows, model_width), jnp.bfloat16)
        .at[target]
        .set(grad_rows, mode="drop")
        .reshape(owners, expert_slots, CAP, model_width)
    )
    grad_received = lax.all_to_all(grad_send, "expert", split_axis=0, concat_axis=0, tiled=True)
    grad_inner = jnp.einsum(
        "jscd,shd->jsch", grad_received, expert_down, preferred_element_type=jnp.float32
    )
    grad_down = jnp.einsum(
        "jsch,jscd->shd", inner_act, grad_received, preferred_element_type=jnp.float32
    )
    squash = jax.nn.sigmoid(gate_part)
    grad_gate_part = grad_inner * up_part * squash * (1.0 + gate_part * (1.0 - squash))
    grad_up_part = grad_inner * (gate_part * squash)
    grad_gu = jnp.concatenate([grad_gate_part, grad_up_part], axis=-1).astype(jnp.bfloat16)
    grad_gate_up = jnp.einsum(
        "jscd,jscf->sdf", received, grad_gu, preferred_element_type=jnp.float32
    )
    grad_xrows = jnp.einsum(
        "jscf,sdf->jscd", grad_gu, expert_gate_up, preferred_element_type=jnp.float32
    ).astype(jnp.bfloat16)
    back_rows = lax.all_to_all(grad_xrows, "expert", split_axis=0, concat_axis=0, tiled=True)
    grad_gate_up_shard, grad_down_shard = (
        lax.psum_scatter(grad_gate_up, "dp", scatter_dimension=1, tiled=True),
        lax.psum_scatter(grad_down, "dp", scatter_dimension=2, tiled=True),
    )
    rows_back = (
        back_rows.reshape(total_rows, model_width)[safe_slot]
        .reshape(sequence_length, top_count, model_width)
        .astype(jnp.float32)
    )
    grad_from_rows = jnp.sum(jnp.where(keep_three[..., None], rows_back, 0.0), axis=1)
    grad_probs = jnp.sum(table_three * grad_gate[..., None], axis=1)
    grad_logits = router_probs * (
        grad_probs - jnp.sum(router_probs * grad_probs, axis=1, keepdims=True)
    )
    router_float = weight_router.astype(jnp.float32)
    grad_norm_hidden = grad_from_rows + jnp.einsum(
        "te,de->td", grad_logits, router_float, precision=lax.Precision.HIGHEST
    )
    grad_router = jnp.einsum(
        "td,te->de", norm_hidden.astype(jnp.float32), grad_logits, precision=lax.Precision.HIGHEST
    )
    grad_hidden_part, grad_gain_two = norm_back(
        grad_norm_hidden, normed_two, scale_two, gain_second
    )
    grad_hidden = grad_y + grad_hidden_part
    branch_gradient = (RESIDUAL_SCALE * grad_hidden).astype(jnp.bfloat16)
    grad_wo = jnp.einsum(
        "tf,td->fd", attended_flat, branch_gradient, preferred_element_type=jnp.float32
    )
    attended_gradient = jnp.einsum(
        "td,fd->tf", branch_gradient, output_projection_weight, preferred_element_type=jnp.float32
    ).astype(jnp.bfloat16)
    block_gradients = attended_gradient.reshape(
        count_of_blocks, rows_per_block, KEY_VALUE_HEADS, head_groups, HEAD_DIMENSION
    )

    def attend_back(totals, pieces):
        key_gradients, value_gradients = totals
        query_block, block_start, attended_block, grad_block, log_total = pieces
        scores = masked_scores(query_block, rows_of_keys, segments, block_start)
        soft_weights = jnp.exp(scores - log_total)
        probs = soft_weights.astype(jnp.bfloat16)
        value_gradients = value_gradients + jnp.einsum(
            "hgqk,qhgd->khd", probs, grad_block, preferred_element_type=jnp.float32
        )
        grad_weights = jnp.einsum(
            "qhgd,khd->hgqk", grad_block, rows_of_values, preferred_element_type=jnp.float32
        )
        row_delta = jnp.einsum(
            "qhgd,qhgd->hgq", grad_block, attended_block, preferred_element_type=jnp.float32
        )[..., None]
        grad_scores = (soft_weights * (grad_weights - row_delta) * SCORE_SCALE).astype(jnp.bfloat16)
        grad_query = jnp.einsum(
            "hgqk,khd->qhgd", grad_scores, rows_of_keys, preferred_element_type=jnp.float32
        )
        key_gradients = key_gradients + jnp.einsum(
            "hgqk,qhgd->khd", grad_scores, query_block, preferred_element_type=jnp.float32
        )
        return ((key_gradients, value_gradients), grad_query)

    empty_key_rows = jnp.zeros((sequence_length, KEY_VALUE_HEADS, HEAD_DIMENSION), jnp.float32)
    (key_gradients, value_gradients), grad_query_blocks = lax.scan(
        attend_back,
        (empty_key_rows, empty_key_rows),
        (blocks_of_queries, block_starts, attended, block_gradients, log_totals),
    )
    grad_q_low = (
        inverse_rotary(
            grad_query_blocks.reshape(sequence_length, QUERY_HEADS, HEAD_DIMENSION),
            cosine_lookup,
            sine_lookup,
        )
        .astype(jnp.bfloat16)
        .reshape(sequence_length, QUERY_HEADS * HEAD_DIMENSION)
    )
    key_gradient_narrow = (
        inverse_rotary(key_gradients, cosine_lookup, sine_lookup)
        .astype(jnp.bfloat16)
        .reshape(sequence_length, KEY_VALUE_HEADS * HEAD_DIMENSION)
    )
    value_gradient_narrow = value_gradients.astype(jnp.bfloat16).reshape(
        sequence_length, KEY_VALUE_HEADS * HEAD_DIMENSION
    )
    grad_wq = jnp.einsum(
        "td,tf->df", input_before_norm, grad_q_low, preferred_element_type=jnp.float32
    )
    grad_wk = jnp.einsum(
        "td,tf->df", input_before_norm, key_gradient_narrow, preferred_element_type=jnp.float32
    )
    grad_wv = jnp.einsum(
        "td,tf->df", input_before_norm, value_gradient_narrow, preferred_element_type=jnp.float32
    )
    grad_norm_input = jnp.einsum(
        "tf,df->td", grad_q_low, weight_q, preferred_element_type=jnp.float32
    )
    grad_norm_input = grad_norm_input + jnp.einsum(
        "tf,df->td", key_gradient_narrow, key_projection_weight, preferred_element_type=jnp.float32
    )
    grad_norm_input = grad_norm_input + jnp.einsum(
        "tf,df->td",
        value_gradient_narrow,
        value_projection_weight,
        preferred_element_type=jnp.float32,
    )
    grad_in_part, grad_gain_one = norm_back(grad_norm_input, normed_one, scale_one, gain_first)
    grad_inputs = grad_hidden + grad_in_part
    summed = lax.psum(
        (grad_gain_one, grad_wq, grad_wk, grad_wv, grad_wo, grad_gain_two, grad_router), "expert"
    )
    total_one, total_q, total_k, total_v, total_o, total_two, total_router = summed
    shards = (
        lax.psum_scatter(total_one, "dp", scatter_dimension=0, tiled=True),
        lax.psum_scatter(total_q, "dp", scatter_dimension=0, tiled=True),
        lax.psum_scatter(total_k, "dp", scatter_dimension=0, tiled=True),
        lax.psum_scatter(total_v, "dp", scatter_dimension=0, tiled=True),
        lax.psum_scatter(total_o, "dp", scatter_dimension=0, tiled=True),
        lax.psum_scatter(total_two, "dp", scatter_dimension=0, tiled=True),
        lax.psum_scatter(total_router, "dp", scatter_dimension=0, tiled=True),
    )
    final_one, final_q, final_k, final_v, final_o, final_two, final_router = shards
    return (
        output,
        grad_inputs,
        final_one,
        final_q,
        final_k,
        final_v,
        final_o,
        final_two,
        final_router,
        grad_gate_up_shard,
        grad_down_shard,
    )


def solution(mesh):
    placed = (
        P(("dp", "expert"), None),
        P(("dp", "expert"), None),
        P(("dp", "expert"), None),
        P(),
        P("dp"),
        P("dp", None),
        P("dp", None),
        P("dp", None),
        P("dp", None),
        P("dp"),
        P("dp", None),
        P("expert", None, None),
        P("expert", None, None),
        P(("dp", "expert"), None),
    )
    return jax.shard_map(
        on_device,
        mesh=mesh,
        in_specs=placed,
        out_specs=(
            P(("dp", "expert"), None),
            P(("dp", "expert"), None),
            P("dp"),
            P("dp", None),
            P("dp", None),
            P("dp", None),
            P("dp", None),
            P("dp"),
            P("dp", None),
            P("expert", "dp", None),
            P("expert", None, "dp"),
        ),
        check_vma=False,
    )
```

profile of v0, /device:TPU:0, one launch (start us, length us, event | category | flops | bytes accessed | tf_op | source)
XLA Modules:
  0.0 1387.4 jit_solution(12779607783628203115)
XLA Ops:
  22.2 11.3 reduce-window.6
  36.6 16.6 %all-gather.9.cloned.1.call-done = bf16[1536,512]{1,0:T(8,128)(2,1)} async-done(((bf16[384,512]{1,0:T(8,128)(2,1)}), bf16[1536,512]{1,0:T(8,128)(2,1)}) %all-gather.9.cloned.1.call-update) | async-done | bytes 1572880 | tf_op jit(solution)/shard_map/all_gather | solution.py:114
  55.5 36.8 %all-gather.11.cloned.1.call-done = bf16[1536,1536]{1,0:T(8,128)(2,1)} async-done(((bf16[384,1536]{1,0:T(8,128)(2,1)}), bf16[1536,1536]{1,0:T(8,128)(2,1)}) %all-gather.11.cloned.1.call-update) | async-done | bytes 4718608 | tf_op jit(solution)/shard_map/all_gather | solution.py:113
  98.8 32.4 %all-gather.13.cloned.1.call-done = bf16[1536,1536]{1,0:T(8,128)(2,1)} async-done(((bf16[384,1536]{1,0:T(8,128)(2,1)}), bf16[1536,1536]{1,0:T(8,128)(2,1)}) %all-gather.13.cloned.1.call-update) | async-done | bytes 4718608 | tf_op jit(solution)/shard_map/all_gather | solution.py:116
  151.0 16.5 %all_gather.27 = bf16[1536,40]{0,1:T(8,128)(2,1)S(1)} all-gather(bf16[384,40]{0,1:T(8,128)(2,1)S(1)} %copy-done.50), channel_id=1, replica_groups=mesh['dp'=4,'expert'=8] {'dp'}, dimensions={0}, use_global_device_ids=true | all-gather | bytes 153600 | tf_op jit(solution)/shard_map/all_gather | solution.py:118
  169.1 7.2 scatter_custom_fusion.1
  179.5 59.6 %all-to-all-done = bf16[8,5,28,1536]{3,2,1,0:T(8,128)(2,1)} async-done(((bf16[8,5,28,1536]{3,2,1,0:T(8,128)(2,1)}), bf16[8,5,28,1536]{3,2,1,0:T(8,128)(2,1)}, u32[]{:S(2)}, u32[]{:S(2)}) %all-to-all-start) | async-done | bytes 3440672 | tf_op jit(solution)/shard_map/all_to_all | solution.py:199
  243.6 13.3 fusion.40
  256.9 73.9 %all-to-all-done.2 = bf16[8,5,28,1536]{3,2,1,0:T(8,128)(2,1)} async-done(((bf16[8,5,28,1536]{3,2,1,0:T(8,128)(2,1)}), bf16[8,5,28,1536]{3,2,1,0:T(8,128)(2,1)}, u32[]{:S(2)}, u32[]{:S(2)}) %all-to-all-start.2) | async-done | bytes 3440672 | tf_op jit(solution)/shard_map/all_to_all | solution.py:231
  330.8 9.9 fusion.35
  340.7 9.1 fusion.22
  364.6 79.1 %all-to-all-done.3 = bf16[8,5,28,1536]{3,2,1,0:T(8,128)(2,1)} async-done(((bf16[8,5,28,1536]{3,2,1,0:T(8,128)(2,1)}), bf16[8,5,28,1536]{3,2,1,0:T(8,128)(2,1)}, u32[]{:S(2)}, u32[]{:S(2)}) %all-to-all-start.3) | async-done | bytes 3440672 | tf_op jit(solution)/shard_map/all_to_all | solution.py:248
  465.5 69.6 %all-to-all-done.1 = bf16[8,5,28,1536]{3,2,1,0:T(8,128)(2,1)} async-done(((bf16[8,5,28,1536]{3,2,1,0:T(8,128)(2,1)}), bf16[8,5,28,1536]{3,2,1,0:T(8,128)(2,1)}, u32[]{:S(2)}, u32[]{:S(2)}) %all-to-all-start.1) | async-done | bytes 3440672 | tf_op jit(solution)/shard_map/all_to_all | solution.py:209
  580.5 16.7 %reduce-scatter.16.cloned.1.call-done = f32[384,512]{1,0:T(8,128)} async-done(((f32[1536,512]{1,0:T(8,128)}), f32[384,512]{1,0:T(8,128)}) %reduce-scatter.16.cloned.1.call-update) | async-done | bytes 786448 | tf_op jit(solution)/shard_map/reduce_scatter | solution.py:363
  597.2 40.9 %reduce-scatter.14.cloned.1.call-done = f32[384,512]{1,0:T(8,128)} async-done(((f32[1536,512]{1,0:T(8,128)}), f32[384,512]{1,0:T(8,128)}) %reduce-scatter.14.cloned.1.call-update) | async-done | bytes 786448 | tf_op jit(solution)/shard_map/reduce_scatter | solution.py:362
  638.1 80.6 %reduce-scatter.18.cloned.1.call-done = f32[384,1536]{1,0:T(8,128)} async-done(((f32[1536,1536]{1,0:T(8,128)}), f32[384,1536]{1,0:T(8,128)}) %reduce-scatter.18.cloned.1.call-update) | async-done | bytes 2359312 | tf_op jit(solution)/shard_map/reduce_scatter | solution.py:364
  718.6 80.6 %reduce-scatter.12.cloned.1.call-done = f32[384,1536]{1,0:T(8,128)} async-done(((f32[1536,1536]{1,0:T(8,128)}), f32[384,1536]{1,0:T(8,128)}) %reduce-scatter.12.cloned.1.call-update) | async-done | bytes 2359312 | tf_op jit(solution)/shard_map/reduce_scatter | solution.py:361
  800.5 10.0 convolution_bitcast_fusion.1
  811.8 17.6 %convolution_bitcast_fusion = f32[5,1536,1024]{2,1,0:T(8,128)} fusion(bf16[8,5,28,1536]{3,2,1,0:T(8,128)(2,1)} %all-to-all-done, bf16[8,5,28,512]{3,2,0,1:T(8,128)(2,1)} %get-tuple-element.87, bf16[8,5,28,512]{3,2,0,1:T(8,128)(2,1)S(1)} %copy-done.59), kind=kOutput, calls=%fused_computation.4 | convolution fusion | flops 3527802880 | bytes 37191680 | tf_op jit(solution)/shard_map/jscd,jscf->sdf/dot_general | solution.py:242
  837.5 10.9 all-reduce.4
  849.7 41.9 %all-reduce.2 = (f32[384]{0:T(512)}, f32[384]{0:T(512)}, f32[384,40]{0,1:T(8,128)}) all-reduce(f32[384]{0:T(512)S(1)} %dynamic-slice.3, f32[384]{0:T(512)S(1)} %dynamic-slice.5, f32[384,40]{0,1:T(8,128)} %reduce-scatter.20.cloned.1.call-done), channel_id=1, replica_groups=mesh['dp'=4,'expert'=8] {'expert'}, use_global_device_ids=true, to_apply=%region_21.22 | all-reduce | flops 16128 | bytes 129024 | tf_op jit(solution)/shard_map/psum | solution.py:355
  891.6 146.6 %all-reduce.7.cloned.1.call-done = (f32[384,1536]{1,0:T(8,128)}, f32[384,512]{1,0:T(8,128)}, f32[384,512]{1,0:T(8,128)}, f32[384,1536]{1,0:T(8,128)}) async-done(((f32[384,1536]{1,0:T(8,128)}, f32[384,512]{1,0:T(8,128)}, f32[384,512]{1,0:T(8,128)}, f32[384,1536]{1,0:T(8,128)}), (f32[384,1536]{1,0:T(8,128)}, f32[384,512]{1,0:T(8,128)}, f32[384,512]{1,0:T(8,128)}, ...) | async-done | bytes 6291472 | tf_op jit(solution)/shard_map/psum | solution.py:355
  1038.3 118.8 %reduce-scatter.10.cloned.1.call-done = f32[5,512,384]{2,1,0:T(8,128)} async-done(((f32[5,512,1536]{2,1,0:T(8,128)}), f32[5,512,384]{2,1,0:T(8,128)}) %reduce-scatter.10.cloned.1.call-update) | async-done | bytes 3932176 | tf_op jit(solution)/shard_map/reduce_scatter | solution.py:251
  1157.0 216.7 %reduce-scatter.8.cloned.1.call-done = f32[5,384,1024]{2,1,0:T(8,128)} async-done(((f32[5,1536,1024]{2,1,0:T(8,128)}), f32[5,384,1024]{2,1,0:T(8,128)}) %reduce-scatter.8.cloned.1.call-update) | async-done | bytes 7864336 | tf_op jit(solution)/shard_map/reduce_scatter | solution.py:250
  (251 shorter events, 154.8 us)
Async XLA Ops:
  7.2 27.4 %all-gather.7.cloned.1.call-start = ((), (), s32[]{:S(2)}) async-start(), calls=%async_computation.11 | async-start | bytes 1966080 | tf_op jit(solution)/shard_map/all_gather | solution.py:115
  8.0 45.3 %all-gather.9.cloned.1.call-start = ((), (), s32[]{:S(2)}) async-start(), calls=%async_computation.12 | async-start | bytes 1966080 | tf_op jit(solution)/shard_map/all_gather | solution.py:114
  8.7 83.6 %all-gather.11.cloned.1.call-start = ((), (), s32[]{:S(2)}) async-start(), calls=%async_computation.13 | async-start | bytes 5898240 | tf_op jit(solution)/shard_map/all_gather | solution.py:113
  9.5 121.7 %all-gather.13.cloned.1.call-start = ((), (), s32[]{:S(2)}) async-start(), calls=%async_computation.14 | async-start | bytes 5898240 | tf_op jit(solution)/shard_map/all_gather | solution.py:116
  34.3 62.3 %copy-start.47 = (f32[128]{0:T(128)}, f32[128]{0:T(128)S(1)}, u32[]{:S(2)}) copy-start(f32[128]{0:T(128)S(1)} %add_rsqrt_fusion.1) | copy-start | bytes 1540
  34.6 62.0 %copy-start.31 = (f32[128,32]{0,1:T(8,128)}, f32[128,32]{0,1:T(8,128)S(1)}, u32[]{:S(2)}) copy-start(f32[128,32]{0,1:T(8,128)S(1)} %get-tuple-element.99) | copy-start | bytes 49156
  34.6 62.0 %copy-start.34 = (f32[128,32]{0,1:T(8,128)}, f32[128,32]{0,1:T(8,128)S(1)}, u32[]{:S(2)}) copy-start(f32[128,32]{0,1:T(8,128)S(1)} %get-tuple-element.100) | copy-start | bytes 49156
  36.6 61.0 %copy-start.22 = (bf16[128,512]{0,1:T(8,128)(2,1)}, bf16[128,512]{0,1:T(8,128)(2,1)S(1)}, u32[]{:S(2)}) copy-start(bf16[128,512]{0,1:T(8,128)(2,1)S(1)} %copy.106) | copy-start | bytes 393220
  55.5 41.3 %copy-start.42 = (bf16[128,8,32]{0,2,1:T(8,128)(2,1)}, bf16[128,8,32]{0,2,1:T(8,128)(2,1)S(1)}, u32[]{:S(2)}) copy-start(bf16[128,8,32]{0,2,1:T(8,128)(2,1)S(1)} %get-tuple-element.97) | copy-start | bytes 196612
  55.5 41.3 %copy-start.44 = (bf16[128,8,32]{0,2,1:T(8,128)(2,1)}, bf16[128,8,32]{0,2,1:T(8,128)(2,1)S(1)}, u32[]{:S(2)}) copy-start(bf16[128,8,32]{0,2,1:T(8,128)(2,1)S(1)} %get-tuple-element.98) | copy-start | bytes 196612
  145.4 93.7 %all-to-all-start = ((bf16[8,5,28,1536]{3,2,1,0:T(8,128)(2,1)}), bf16[8,5,28,1536]{3,2,1,0:T(8,128)(2,1)}, u32[]{:S(2)}, u32[]{:S(2)}) async-start(bf16[8,5,28,1536]{3,2,1,0:T(8,128)(2,1)} %reshape.423), calls=%async_computation | async-start | bytes 7864320 | tf_op jit(solution)/shard_map/all_to_all | solution.py:199
  168.9 380.9 %copy-start.37 = (f32[128,40]{0,1:T(8,128)}, f32[128,40]{0,1:T(8,128)S(1)}, u32[]{:S(2)}) copy-start(f32[128,40]{0,1:T(8,128)S(1)} %fusion.74) | copy-start | bytes 61444
  239.1 91.7 %all-to-all-start.2 = ((bf16[8,5,28,1536]{3,2,1,0:T(8,128)(2,1)}), bf16[8,5,28,1536]{3,2,1,0:T(8,128)(2,1)}, u32[]{:S(2)}, u32[]{:S(2)}) async-start(bf16[8,5,28,1536]{3,2,1,0:T(8,128)(2,1)} %reshape.425), calls=%async_computation.2 | async-start | bytes 7864320 | tf_op jit(solution)/shard_map/all_to_all | solution.py:231
  352.2 91.5 %all-to-all-start.3 = ((bf16[8,5,28,1536]{3,2,1,0:T(8,128)(2,1)}), bf16[8,5,28,1536]{3,2,1,0:T(8,128)(2,1)}, u32[]{:S(2)}, u32[]{:S(2)}) async-start(bf16[8,5,28,1536]{3,2,1,0:T(8,128)(2,1)} %copy.121), calls=%async_computation.3 | async-start | bytes 7864320 | tf_op jit(solution)/shard_map/all_to_all | solution.py:248
  443.7 91.5 %all-to-all-start.1 = ((bf16[8,5,28,1536]{3,2,1,0:T(8,128)(2,1)}), bf16[8,5,28,1536]{3,2,1,0:T(8,128)(2,1)}, u32[]{:S(2)}, u32[]{:S(2)}) async-start(bf16[8,5,28,1536]{3,2,1,0:T(8,128)(2,1)} %copy.118), calls=%async_computation.1 | async-start | bytes 7864320 | tf_op jit(solution)/shard_map/all_to_all | solution.py:209
  448.2 149.0 %reduce-scatter.16.cloned.1.call-start = ((), (), s32[]{:S(2)}) async-start(), calls=%async_computation.19 | async-start | bytes 3932160 | tf_op jit(solution)/shard_map/reduce_scatter | solution.py:363
  561.0 77.0 %reduce-scatter.14.cloned.1.call-start = ((), (), s32[]{:S(2)}) async-start(), calls=%async_computation.18 | async-start | bytes 3932160 | tf_op jit(solution)/shard_map/reduce_scatter | solution.py:362
  566.5 152.1 %reduce-scatter.18.cloned.1.call-start = ((), (), s32[]{:S(2)}) async-start(), calls=%async_computation.20 | async-start | bytes 11796480 | tf_op jit(solution)/shard_map/reduce_scatter | solution.py:364
  571.7 227.5 %reduce-scatter.12.cloned.1.call-start = ((), (), s32[]{:S(2)}) async-start(), calls=%async_computation.17 | async-start | bytes 11796480 | tf_op jit(solution)/shard_map/reduce_scatter | solution.py:361
  578.5 271.3 %reduce-scatter.20.cloned.1.call-start = ((), (), s32[]{:S(2)}) async-start(), calls=%async_computation.21 | async-start | bytes 307200 | tf_op jit(solution)/shard_map/reduce_scatter | solution.py:366
  580.4 457.8 %all-reduce.7.cloned.1.call-start = ((), (), s32[]{:S(2)}) async-start(), calls=%async_computation.22 | async-start | bytes 12582912 | tf_op jit(solution)/shard_map/psum | solution.py:355
  799.2 357.8 %reduce-scatter.10.cloned.1.call-start = ((), (), s32[]{:S(2)}) async-start(), calls=%async_computation.16 | async-start | bytes 19660800 | tf_op jit(solution)/shard_map/reduce_scatter | solution.py:251
  810.5 563.3 %reduce-scatter.8.cloned.1.call-start = ((), (), s32[]{:S(2)}) async-start(), calls=%async_computation.15 | async-start | bytes 39321600 | tf_op jit(solution)/shard_map/reduce_scatter | solution.py:250
  1038.3 338.9 %copy-start.26 = (f32[384,512]{1,0:T(8,128)S(1)}, f32[384,512]{1,0:T(8,128)}, u32[]{:S(2)}) copy-start(f32[384,512]{1,0:T(8,128)} %get-tuple-element.113) | copy-start | bytes 2359300
  (52 other events, 301.4 us)
Sparse Core Ops, SparseCore 0:
  9.6 22.3 all-gather.6
  33.6 19.6 all-gather.8
  54.8 37.4 all-gather.10
  93.7 37.4 all-gather.12
  561.1 35.9 reduce-scatter.15
  600.1 37.8 reduce-scatter.13
  640.6 77.9 reduce-scatter.17
  721.2 77.9 reduce-scatter.11
  802.2 19.9 reduce-scatter.19
  826.5 211.6 all-reduce.6
  1041.4 115.5 reduce-scatter.9
  1160.1 213.6 reduce-scatter.7
where the time goes:
time: 1400 us; the launch traced here: 1390 us
  waiting for transfers between devices  1070 us (76%)
  matrix products  109 us (8%)
  blocking collectives  81 us (6%)
  local copies, waits for them, and re-layouts  55.2 us (4%)
  other arithmetic  34.4 us (2%)
  starting transfers between devices  20.3 us (1%)
  between operations  16 us (1%)
    reduce_scatter x1, waiting for transfers between devices, on_device(): lax.psum_scatter(grad_gate_up, 'dp', scatter_dimension=1, tiled=True)  217 us
    psum x1, waiting for transfers between devices, on_device(): lax.psum((grad_gain_one, grad_wq, grad_wk, grad_wv, grad_wo, grad_gain_tw...  147 us
    reduce_scatter x1, waiting for transfers between devices, on_device(): lax.psum_scatter(grad_down, 'dp', scatter_dimension=2, tiled=True)  119 us
    reduce_scatter x1, waiting for transfers between devices, on_device(): lax.psum_scatter(total_q, 'dp', scatter_dimension=0, tiled=True)  80.6 us
    reduce_scatter x1, waiting for transfers between devices, on_device(): lax.psum_scatter(total_o, 'dp', scatter_dimension=0, tiled=True)  80.6 us
    all_to_all x1, waiting for transfers between devices, on_device(): lax.all_to_all(grad_xrows, 'expert', split_axis=0, concat_axis=0, tiled=T...  79.1 us
    all_to_all x1, waiting for transfers between devices, on_device(): lax.all_to_all(grad_send, 'expert', split_axis=0, concat_axis=0, tiled=True)  73.9 us
    all_to_all x1, waiting for transfers between devices, on_device(): lax.all_to_all(produced, 'expert', split_axis=0, concat_axis=0, tiled=True)  69.6 us
  transfers between devices with their start and end apart: 16, of which 14 were waited for; matrix products, arithmetic and copies ran while one was open for 9% of the time, Pallas kernels for 0%

commit v1 on v0

v1 whole, which is shorter than its diff:
```python
import functools
import math

import jax
import jax.numpy as jnp
import numpy as np
from jax import lax
from jax.experimental import pallas as pl
from jax.experimental.pallas import tpu as pltpu
from jax.sharding import PartitionSpec as P

QUERY_HEADS = 24
KEY_VALUE_HEADS = 8
HEAD_DIMENSION = 64
EXPERT_COUNT = 40
BLK = 4
SLOT_ROWS = 32
SLOT_STRIDE = 8

NORM_EPSILON = 1e-06
SCORE_SCALE = 0.015625
RESIDUAL_SCALE = 0.22
ROPE_BASE = 10000.0
MASKED_SCORE = -1e30

MESH = pl.DeviceIdType.MESH
F32, BF16 = jnp.float32, jnp.bfloat16
MEBI = 1024 * 1024
VMEM_MOST = 67_043_328


class Grid:
    def __init__(self, axis, A, B):
        self.axis, self.A, self.B = axis, A, B
        self.me = lax.axis_index(axis)
        self.a, self.b = self.me // B, self.me % B

    def at(self, a, b):
        return a * self.B + b

    def dev(self, a, b):
        return {self.axis: self.at(a, b)}

    def here(self):
        return {self.axis: self.me}

    def near(self):
        found = []
        if self.A > 1:
            found += [
                (self.a > 0, self.dev(self.a - 1, self.b)),
                (self.a < self.A - 1, self.dev(self.a + 1, self.b)),
            ]
        if self.B > 1:
            found += [
                (self.b > 0, self.dev(self.a, self.b - 1)),
                (self.b < self.B - 1, self.dev(self.a, self.b + 1)),
            ]
        return found

    def all(self):
        n = self.A * self.B
        return [(self.me >= 0, {self.axis: (self.me + r) % n}) for r in range(1, n)]

    def next(self, kind, way):
        step = 1 if way == 0 else -1
        if kind == "a":
            return self.ahead("a", way, 1), self.dev(self.a + step, self.b)
        return self.ahead("b", way, 1), self.dev(self.a, self.b + step)

    def behind(self, kind, way, far):
        at, size = (self.a, self.A) if kind == "a" else (self.b, self.B)
        return (at - far >= 0) if way == 0 else (at + far <= size - 1)

    def ahead(self, kind, way, far):
        return self.behind(kind, 1 - way, far)


def greet(peers):
    barrier = pltpu.get_barrier_semaphore()
    for there, device in peers:

        @pl.when(there)
        def _():
            pl.semaphore_signal(barrier, inc=1, device_id=device, device_id_type=MESH)

    pl.semaphore_wait(barrier, sum(jnp.where(there, 1, 0) for there, _ in peers))


def remote(src, dst, send, recv, device):
    return pltpu.make_async_remote_copy(
        src_ref=src, dst_ref=dst, send_sem=send, recv_sem=recv, device_id=device, device_id_type=MESH
    )


def run(*steps):
    steps = list(steps)
    while steps:
        left = []
        for step in steps:
            try:
                next(step)
                left.append(step)
            except StopIteration:
                pass
        steps = left


def line_sems(A, B):
    dma = pltpu.SemaphoreType.DMA
    return [dma((2, A)), dma((2, A)), dma((2, A, B)), dma((2, A, B))]


def gather(g, own, out, sems):
    send_a, recv_a, send_b, recv_b = sems
    A, B = g.A, g.B
    row = lambda way, k: g.a - k if way == 0 else g.a + k
    col = lambda way, k: g.b - k if way == 0 else g.b + k
    rows = [(0, 0)] + [(way, k) for k in range(1, A) for way in (0, 1)]

    def along_a(way, k, src, do):
        if k < A - 1:
            there, device = g.next("a", way)
            i = g.at(row(way, k), g.b)

            @pl.when(there)
            def _():
                do(remote(src, out.at[i], send_a.at[way, k], recv_a.at[way, k + 1], device))

    def along_b(way, j, a, i, src, do):
        if j < B - 1:
            there, device = g.next("b", way)

            @pl.when(there)
            def _():
                do(remote(src, out.at[i], send_b.at[way, a, j], recv_b.at[way, a, j + 1], device))

    def start(copy):
        copy.start()

    def sent(copy):
        copy.wait_send()

    for way in (0, 1):
        along_a(way, 0, own, start)
    for way in (0, 1):
        along_b(way, 0, g.a, g.me, own, start)
    yield
    for k in range(1, A):
        for way in (0, 1):
            i = g.at(row(way, k), g.b)

            @pl.when(g.behind("a", way, k))
            def _():
                remote(out.at[i], out.at[i], send_a.at[way, k], recv_a.at[way, k], g.here()).wait_recv()
                along_a(way, k, out.at[i], start)
                for w in (0, 1):
                    along_b(w, 0, row(way, k), i, out.at[i], start)

            yield
    for j in range(1, B):
        for way, k in rows:
            for w in (0, 1):
                i = g.at(row(way, k), col(w, j))

                @pl.when(g.behind("a", way, k) & g.behind("b", w, j))
                def _():
                    a = row(way, k)
                    remote(out.at[i], out.at[i], send_b.at[w, a, j], recv_b.at[w, a, j], g.here()).wait_recv()
                    along_b(w, j, a, i, out.at[i], start)

            yield
    for way, k in rows:
        for w in (0, 1) if k == 0 else (way,):

            @pl.when(g.behind("a", w, k))
            def _():
                along_a(w, k, own, sent)

        @pl.when(g.behind("a", way, k))
        def _():
            for w in (0, 1):
                for j in range(B - 1):

                    @pl.when(g.behind("b", w, j))
                    def _():
                        along_b(w, j, row(way, k), g.me, own, sent)


def sum_slots(A, B, block, dtype=BF16):
    return [
        pltpu.VMEM((2, A) + block, dtype),
        pltpu.VMEM((2, A) + block, dtype),
        pltpu.VMEM((2, A, B - 1) + block, dtype),
        pltpu.VMEM((2, A, B - 2) + block if B > 2 else (8, 128), dtype),
    ]


def reduce(g, part, finish, sems, slots):
    send_a, recv_a, send_b, recv_b = sems
    land_a, out_a, land_b, out_b = slots
    A, B = g.A, g.B
    row = lambda way, k: g.a + k if way == 0 else g.a - k
    col = lambda way, k: g.b + k if way == 0 else g.b - k
    rows = [(way, k) for k in range(A - 1, 0, -1) for way in (0, 1)] + [(0, 0)]
    here = g.here()
    first = lambda kind, way: jnp.logical_not(g.behind(kind, way, 1))

    for way, k in rows:

        @pl.when(g.ahead("a", way, k))
        def _():
            a = row(way, k)
            for j in range(B - 1, 0, -1):
                for w in (0, 1):

                    @pl.when(g.ahead("b", w, j) & first("b", w))
                    def _():
                        remote(
                            part(g.at(a, col(w, j))),
                            land_b.at[w, a, j - 1],
                            send_b.at[w, a, j],
                            recv_b.at[w, a, j - 1],
                            g.next("b", w)[1],
                        ).start()

    yield
    for way, k in rows:

        @pl.when(g.ahead("a", way, k))
        def _():
            a = row(way, k)
            for j in range(B - 2, 0, -1):
                for w in (0, 1):

                    @pl.when(g.ahead("b", w, j) & g.behind("b", w, 1))
                    def _():
                        remote(land_b.at[w, a, j], land_b.at[w, a, j], send_b.at[w, a, j], recv_b.at[w, a, j], here).wait_recv()
                        out_b[w, a, j - 1] = (
                            part(g.at(a, col(w, j)))[...].astype(F32) + land_b[w, a, j].astype(F32)
                        ).astype(out_b.dtype)
                        remote(
                            out_b.at[w, a, j - 1],
                            land_b.at[w, a, j - 1],
                            send_b.at[w, a, j],
                            recv_b.at[w, a, j - 1],
                            g.next("b", w)[1],
                        ).start()

            for w in (0, 1):
                if B > 1:

                    @pl.when(g.behind("b", w, 1))
                    def _():
                        remote(land_b.at[w, a, 0], land_b.at[w, a, 0], send_b.at[w, a, 0], recv_b.at[w, a, 0], here).wait_recv()

            def near():
                total = part(g.at(a, g.b))[...].astype(F32)
                if B == 2:
                    return total + land_b[1 - g.b, a, 0].astype(F32)
                for w in (0, 1):
                    if B > 1:
                        total = total + jnp.where(g.behind("b", w, 1), land_b[w, a, 0].astype(F32), 0.0)
                return total

            if k > 0:

                @pl.when(g.behind("a", way, 1))
                def _():
                    if k < A - 1:
                        remote(land_a.at[way, k], land_a.at[way, k], send_a.at[way, k], recv_a.at[way, k], here).wait_recv()
                        out_a[way, k] = (near() + land_a[way, k].astype(F32)).astype(out_a.dtype)

                @pl.when(first("a", way))
                def _():
                    out_a[way, k] = near().astype(out_a.dtype)

                remote(
                    out_a.at[way, k], land_a.at[way, k - 1], send_a.at[way, k], recv_a.at[way, k - 1], g.next("a", way)[1]
                ).start()
            else:
                for w in (0, 1):
                    if A > 1:

                        @pl.when(g.behind("a", w, 1))
                        def _():
                            remote(land_a.at[w, 0], land_a.at[w, 0], send_a.at[w, 0], recv_a.at[w, 0], here).wait_recv()

                total = near()
                if A == 2:
                    total = total + land_a[1 - g.a, 0].astype(F32)
                else:
                    for w in (0, 1):
                        if A > 1:
                            total = total + jnp.where(g.behind("a", w, 1), land_a[w, 0].astype(F32), 0.0)
                finish(total)

        yield
    for way, k in rows:

        @pl.when(g.ahead("a", way, k))
        def _():
            a = row(way, k)
            for j in range(B - 1, 0, -1):
                for w in (0, 1):

                    @pl.when(g.ahead("b", w, j))
                    def _():
                        remote(part(g.me), land_b.at[w, a, j - 1], send_b.at[w, a, j], recv_b.at[w, a, j - 1], here).wait_send()

            if k > 0:
                remote(out_a.at[way, k], land_a.at[way, k - 1], send_a.at[way, k], recv_a.at[way, k - 1], here).wait_send()


def reduce_gather(g, part, out, kept, sems, slots):
    def finish(total):
        kept[...] = total.astype(kept.dtype)

    yield from reduce(g, part, finish, sems[:4], slots)
    out[g.me] = kept[...]
    yield from gather(g, kept, out, sems[4:])


def exchange_sems(n):
    return [pltpu.SemaphoreType.DMA((n,)), pltpu.SemaphoreType.DMA((n,))]


def exchange(g, part, out, sems):
    send, recv = sems
    n = g.A * g.B
    copies = []
    for r in range(1, n):
        to = (g.me + r) % n
        copies.append(remote(part.at[to], out.at[g.me], send.at[r], recv.at[r], {g.axis: to}))
        copies[-1].start()
    out[g.me] = part[g.me]
    yield
    for r in range(1, n):
        origin = (g.me + n - r) % n
        remote(part.at[origin], out.at[origin], send.at[r], recv.at[r], g.here()).wait_recv()
    yield
    for copy in copies:
        copy.wait_send()


def call(body, name, outs, ins, scratch=(), cid=None, us=10.0, **grid):
    whole = pl.BlockSpec(memory_space=pltpu.VMEM)
    params = dict(vmem_limit_bytes=VMEM_MOST)
    if cid is not None:
        params |= dict(collective_id=cid, has_side_effects=True)
    return pl.pallas_call(
        body,
        out_shape=[jax.ShapeDtypeStruct(shape, dtype) for shape, dtype in outs],
        in_specs=grid.pop("in_specs", [whole] * len(ins)),
        out_specs=grid.pop("out_specs", [whole] * len(outs)),
        scratch_shapes=list(scratch),
        compiler_params=pltpu.CompilerParams(**params),
        cost_estimate=pl.CostEstimate(flops=0, transcendentals=0, bytes_accessed=int(us * 3e6)),
        name=name,
        **grid,
    )(*ins)


def taker(refs):
    refs = list(refs)

    def take(n=None):
        if n is None:
            return refs.pop(0)
        return [refs.pop(0) for _ in range(n)]

    return take


def dot(left, right, contract=((1,), (0,))):
    return lax.dot_general(left, right, (contract, ((), ())), preferred_element_type=F32)


def halves(values):
    high = values.astype(BF16)
    return high, (values - high.astype(F32)).astype(BF16)


def norm_scale(values):
    return lax.rsqrt(jnp.mean(values * values, axis=-1, keepdims=True) + NORM_EPSILON)


def norm_back(grad, normed, scale, gain):
    grad_hat = grad * gain
    return scale * (grad_hat - normed * jnp.mean(grad_hat * normed, axis=-1, keepdims=True))


def rotary(values, cosine, sine, back=False):
    width, half = values.shape[1], HEAD_DIMENSION // 2
    later = pltpu.roll(values, width - half, 1)
    earlier = pltpu.roll(values, half, 1)
    front = lax.broadcasted_iota(jnp.int32, values.shape, 1) % HEAD_DIMENSION < half
    other = jnp.where(front, -later, earlier)
    return values * cosine - other * sine if back else values * cosine + other * sine


def allowed_pairs(segment_row):
    size = segment_row.shape[1]
    across = jnp.broadcast_to(segment_row, (size, size))
    rows = lax.broadcasted_iota(jnp.int32, (size, size), 0)
    cols = lax.broadcasted_iota(jnp.int32, (size, size), 1)
    return (cols <= rows) & (across == across.T)


def attention_weights(stacked, keys, allowed):
    scores = dot(stacked, keys, ((1,), (1,))) * SCORE_SCALE
    scores = jnp.where(allowed, scores, MASKED_SCORE)
    row_max = jnp.max(scores, axis=-1, keepdims=True)
    log_total = row_max + jnp.log(jnp.sum(jnp.exp(scores - row_max), axis=-1, keepdims=True))
    return jnp.exp(scores - log_total)


class Heads:
    def __init__(self, ranks):
        self.q, self.kv = QUERY_HEADS // ranks, KEY_VALUE_HEADS // ranks
        self.group = QUERY_HEADS // KEY_VALUE_HEADS
        self.q_cols, self.kv_cols = self.q * HEAD_DIMENSION, self.kv * HEAD_DIMENSION
        self.cols = -(-(self.q_cols + 2 * self.kv_cols) // 128) * 128

    def stack(self, rows, kv):
        first = kv * self.group
        return jnp.concatenate([self.head(rows, first + i) for i in range(self.group)], axis=0)

    def head(self, rows, i):
        return rows[:, i * HEAD_DIMENSION : (i + 1) * HEAD_DIMENSION]

    def key(self, rows, kv):
        return self.head(rows, self.q + kv)

    def value(self, rows, kv):
        return self.head(rows, self.q + self.kv + kv)


def rope_tables(length, heads):
    frequency = np.float32(ROPE_BASE) ** (-(np.arange(HEAD_DIMENSION // 2, dtype=np.float32) * 2.0) / HEAD_DIMENSION)
    angles = np.arange(length, dtype=np.float32)[:, None] * frequency.astype(np.float32)[None, :]
    cosine, sine = (np.tile(f(angles.astype(np.float64)).astype(np.float32), (1, 2)) for f in (np.cos, np.sin))
    turned = heads.q + heads.kv
    rest = heads.cols - turned * HEAD_DIMENSION
    cosine = np.concatenate([np.tile(cosine, (1, turned)), np.ones((length, rest), np.float32)], axis=1)
    sine = np.concatenate([np.tile(sine, (1, turned)), np.zeros((length, rest), np.float32)], axis=1)
    return cosine, sine


def gain_row(misc_ref, ranks, which):
    return jnp.concatenate([misc_ref[i, which : which + 1, :] for i in range(ranks)], axis=1)


def attention_forward(ranks, heads, length, x_ref, w_ref, o_ref, misc_ref, cos_ref, sin_ref, part_ref, qkv_ref, att_ref, scale_ref):
    width = x_ref.shape[2]
    gain = gain_row(misc_ref, ranks, 0)
    weights = w_ref[...].reshape(width, heads.cols)

    def one(b, carry):
        x = x_ref[b].astype(F32)
        scale = norm_scale(x)
        scale_ref[b] = jnp.broadcast_to(scale, (length, 128))
        normed = (x * scale * gain).astype(BF16)
        qkv_ref[b] = rotary(dot(normed, weights), cos_ref[...], sin_ref[...]).astype(BF16)
        qkv = qkv_ref[b]
        allowed = allowed_pairs(misc_ref[b, 8:9, :length])
        allowed = jnp.concatenate([allowed] * heads.group, axis=0)
        outs = []
        for kv in range(heads.kv):
            probs = attention_weights(heads.stack(qkv, kv), heads.key(qkv, kv), allowed).astype(BF16)
            mixed = dot(probs, heads.value(qkv, kv)).astype(BF16)
            outs += [mixed[i * length : (i + 1) * length] for i in range(heads.group)]
        att_ref[b] = jnp.concatenate(outs, axis=1)
        part_ref[b] = dot(att_ref[b], o_ref[...]).astype(BF16)
        return carry

    lax.fori_loop(0, ranks, one, 0)


def route_tables(n_expert, slots, routes, blocks):
    tokens = routes.shape[0]
    column = lax.broadcasted_iota(jnp.int32, (1, 128), 1)
    owner, slot = column // SLOT_STRIDE, column % SLOT_STRIDE
    expert = slot * n_expert + owner
    real = (owner < n_expert) & (slot < slots) & (expert < EXPERT_COUNT)
    expert = jnp.where(real, expert, -1)
    named = jnp.zeros((tokens, 128), F32)
    for k in range(routes.shape[1]):
        named = named + jnp.where(routes[:, k : k + 1] == expert, 1.0, 0.0)
    rows = lax.broadcasted_iota(jnp.int32, (tokens, tokens), 0)
    cols = lax.broadcasted_iota(jnp.int32, (tokens, tokens), 1)
    earlier = jnp.where(cols < rows, 1.0, 0.0).astype(BF16)
    rank = dot(earlier, named.astype(BF16))
    kept = (named > 0.0) & (rank < (blocks * BLK).astype(F32))
    return real, kept, jnp.where(kept, rank, -1.0)


def route_forward(ranks, n_expert, slots, x_ref, branch_ref, misc_ref, router_ref, routes_ref, blocks_ref, hidden_ref, norm_ref, scale_ref, probs_ref, meta_ref):
    gain = gain_row(misc_ref, ranks, 1)
    hidden = x_ref[...].astype(F32) + RESIDUAL_SCALE * branch_ref[...]
    hidden_ref[...] = hidden
    scale = norm_scale(hidden)
    scale_ref[...] = jnp.broadcast_to(scale, scale_ref.shape)
    norm_ref[...] = (hidden * scale * gain).astype(BF16)
    real, kept, place = route_tables(n_expert, slots, routes_ref[...], blocks_ref[0:1, :])
    router = router_ref[...].reshape(-1, 128)
    logits = jnp.where(real, dot(norm_ref[...], router), MASKED_SCORE)
    weight = jnp.exp(logits - jnp.max(logits, axis=-1, keepdims=True))
    probs = weight / jnp.sum(weight, axis=-1, keepdims=True)
    probs_ref[...] = probs
    used = n_expert * SLOT_STRIDE
    meta_ref[0] = place.T[:used]
    meta_ref[1] = jnp.where(kept, probs, 0.0).T[:used]


def experts(n_expert, slots, tokens, nh_ref, og_ref, meta_ref, up_ref, down_ref, out_ref, back_ref, gate_grad_ref, d_up_ref, d_down_ref, x_sc, og_sc, eo_sc, gx_sc, nh_in, og_in, sems):
    step = pl.program_id(0)
    mine = pl.ds(pl.multiple_of(lax.axis_index("expert") * SLOT_STRIDE, SLOT_STRIDE), SLOT_STRIDE)
    width = nh_ref.shape[2]
    hidden = down_ref.shape[1]

    def fetch(q):
        slot = q % 2
        return [
            pltpu.make_async_copy(nh_ref.at[q], nh_in.at[slot], sems.at[0, slot]),
            pltpu.make_async_copy(og_ref.at[q], og_in.at[slot], sems.at[1, slot]),
        ]

    packed = slots * SLOT_ROWS
    number = lax.broadcasted_iota(jnp.int32, (SLOT_ROWS, tokens), 0).astype(F32)

    def picks(q):
        place = meta_ref[q, 0, mine, :]
        return jnp.concatenate([jnp.where(number == place[s : s + 1], 1.0, 0.0) for s in range(slots)], axis=0)

    @pl.when(step == 0)
    def _():
        for copy in fetch(0):
            copy.start()

        def one(q, carry):
            @pl.when(q + 1 < n_expert)
            def _():
                for copy in fetch(q + 1):
                    copy.start()

            for copy in fetch(q):
                copy.wait()
            pick = picks(q).astype(BF16)
            x_sc[q] = dot(pick, nh_in[q % 2]).astype(BF16)
            og_sc[q] = dot(pick, og_in[q % 2]).astype(BF16)
            gate_grad_ref[q] = jnp.zeros((SLOT_STRIDE, tokens), F32)
            return carry

        lax.fori_loop(0, n_expert, one, 0)

    place_of = pl.ds(pl.multiple_of(step * SLOT_ROWS, SLOT_ROWS), SLOT_ROWS)
    slot_row = lax.broadcasted_iota(jnp.int32, (SLOT_STRIDE, tokens), 0) == step
    rows = n_expert * SLOT_ROWS
    x = x_sc[:, place_of, :].reshape(rows, width)
    both = dot(x, up_ref[0])
    gate, up = both[:, :hidden], both[:, hidden:]
    squash = jax.nn.sigmoid(gate)
    inner = (gate * squash * up).astype(BF16)
    produced = dot(inner, down_ref[0]).astype(BF16)
    eo_sc[:, place_of, :] = produced.reshape(n_expert, SLOT_ROWS, width)
    masks, gates = [], []
    for q in range(n_expert):
        place = jnp.sum(jnp.where(slot_row, meta_ref[q, 0, mine, :], 0.0), axis=0, keepdims=True)
        share = jnp.sum(jnp.where(slot_row, meta_ref[q, 1, mine, :], 0.0), axis=0, keepdims=True)
        masks.append(number == place)
        gates.append(jnp.sum(jnp.where(masks[q], share, 0.0), axis=1, keepdims=True))
    mix_grad = RESIDUAL_SCALE * og_sc[:, place_of, :].reshape(rows, width).astype(F32)
    grad_rows = (jnp.concatenate(gates, axis=0) * mix_grad).astype(BF16)
    gate_grad = jnp.sum(mix_grad * produced.astype(F32), axis=1, keepdims=True)
    for q in range(n_expert):
        spread = jnp.where(masks[q], gate_grad[q * SLOT_ROWS : (q + 1) * SLOT_ROWS], 0.0)
        gate_grad_ref[q] = jnp.where(slot_row, jnp.sum(spread, axis=0, keepdims=True), gate_grad_ref[q])
    grad_inner = dot(grad_rows, down_ref[0], ((1,), (1,)))
    grad_both = jnp.concatenate(
        [grad_inner * up * squash * (1.0 + gate * (1.0 - squash)), grad_inner * (gate * squash)], axis=1
    ).astype(BF16)
    gx_sc[:, place_of, :] = dot(grad_both, up_ref[0], ((1,), (1,))).astype(BF16).reshape(n_expert, SLOT_ROWS, width)
    tile = 256
    for i in range(width // tile):
        here = slice(i * tile, (i + 1) * tile)
        d_up_ref[0, here, :] = dot(x[:, here], grad_both, ((0,), (0,))).astype(d_up_ref.dtype)
    for i in range(hidden // tile):
        here = slice(i * tile, (i + 1) * tile)
        d_down_ref[0, here, :] = dot(inner[:, here], grad_rows, ((0,), (0,))).astype(d_down_ref.dtype)

    @pl.when(step == slots - 1)
    def _():
        def one(q, carry):
            pick = picks(q)
            share = meta_ref[q, 1, mine, :]
            share = jnp.concatenate([jnp.broadcast_to(share[s : s + 1], (SLOT_ROWS, tokens)) for s in range(slots)], axis=0)
            high, low = halves(pick * share)
            over = ((0,), (0,))
            out_ref[q] = (dot(high, eo_sc[q], over) + dot(low, eo_sc[q], over)).astype(BF16)
            back_ref[q] = dot(pick.astype(BF16), gx_sc[q], over).astype(BF16)
            return carry

        lax.fori_loop(0, n_expert, one, 0)


def route_backward(ranks, n_expert, shard, hidden_ref, norm_ref, scale_ref, probs_ref, misc_ref, router_ref, og_ref, mixture_ref, back_ref, gate_grad_ref, out_ref, grad_hidden_ref, branch_ref, small_ref):
    tokens, width = hidden_ref.shape
    gain = gain_row(misc_ref, ranks, 1)
    hidden = hidden_ref[...]
    out_ref[...] = (hidden + RESIDUAL_SCALE * mixture_ref[...]).astype(BF16)
    used = n_expert * SLOT_STRIDE
    spread = gate_grad_ref[...].reshape(used, tokens)
    if used < 128:
        spread = jnp.concatenate([spread, jnp.zeros((128 - used, tokens), F32)], axis=0)
    grad_probs = spread.T
    probs = probs_ref[...]
    grad_logits = probs * (grad_probs - jnp.sum(probs * grad_probs, axis=1, keepdims=True))
    high, low = halves(grad_logits)
    router = router_ref[...].reshape(width, 128)
    across = ((1,), (1,))
    grad_norm = back_ref[...] + (dot(high, router, across) + dot(low, router, across))
    scale = scale_ref[:, 0:1]
    normed = hidden * scale
    grad_hidden = og_ref[...].astype(F32) + norm_back(grad_norm, normed, scale, gain)
    grad_hidden_ref[...] = grad_hidden
    branch_ref[...] = (RESIDUAL_SCALE * grad_hidden).astype(BF16)
    over = ((0,), (0,))
    norm = norm_ref[...]
    grad_router = dot(high, norm, over) + dot(low, norm, over)
    grad_gain = jnp.sum(grad_norm * normed, axis=0, keepdims=True)
    for i in range(ranks):
        here = slice(i * shard, (i + 1) * shard)
        small_ref[i, :used, :] = grad_router[:used, here]
        small_ref[i, used:, :] = jnp.broadcast_to(grad_gain[:, here], (8, shard))


def attention_backward(ranks, heads, length, branch_ref, att_ref, qkv_ref, o_ref, misc_ref, cos_ref, sin_ref, grad_ref, d_o_ref):
    d_o_ref[...] = dot(
        att_ref[...].reshape(ranks * length, heads.q_cols), branch_ref[...].reshape(ranks * length, -1), ((0,), (0,))
    ).astype(BF16)

    def one(b, carry):
        grad_att = dot(branch_ref[b], o_ref[...], ((1,), (1,))).astype(BF16)
        att, qkv = att_ref[b], qkv_ref[b]
        allowed = allowed_pairs(misc_ref[b, 8:9, :length])
        allowed = jnp.concatenate([allowed] * heads.group, axis=0)
        d_q, d_k, d_v = [], [], []
        for kv in range(heads.kv):
            queries, keys = heads.stack(qkv, kv), heads.key(qkv, kv)
            soft = attention_weights(queries, keys, allowed)
            grads = heads.stack(grad_att, kv)
            d_v.append(dot(soft.astype(BF16), grads, ((0,), (0,))))
            delta = jnp.sum(grads.astype(F32) * heads.stack(att, kv).astype(F32), axis=1, keepdims=True)
            inner = dot(grads, heads.value(qkv, kv), ((1,), (1,)))
            d_scores = (soft * (inner - delta) * SCORE_SCALE).astype(BF16)
            rows = dot(d_scores, keys)
            d_q += [rows[i * length : (i + 1) * length] for i in range(heads.group)]
            d_k.append(dot(d_scores, queries, ((0,), (0,))))
        spare = heads.cols - heads.q_cols - 2 * heads.kv_cols
        fill = [jnp.zeros((length, spare), F32)] if spare else []
        grads = jnp.concatenate(d_q + d_k + d_v + fill, axis=1)
        grad_ref[b] = rotary(grads, cos_ref[...], sin_ref[...], back=True).astype(BF16)
        return carry

    lax.fori_loop(0, ranks, one, 0)


def projection_backward(ranks, heads, shard, x_ref, scale_ref, gain_ref, grad_ref, w_ref, small_ref, grad_x_ref, d_w_ref, sums_ref):
    normed = x_ref[...].astype(F32) * scale_ref[:, 0:1]
    norm_input = (normed * gain_ref[0:1, :]).astype(BF16)
    total = None
    for i in range(ranks):
        grads = grad_ref[i].reshape(-1, heads.cols)
        term = dot(grads, w_ref[i], ((1,), (1,)))
        total = term if total is None else total + term
        d_w_ref[:, i * heads.cols : (i + 1) * heads.cols] = dot(norm_input, grads, ((0,), (0,))).astype(BF16)
    grad_x_ref[...] = total
    small = small_ref[0]
    for i in range(1, ranks):
        small = small + small_ref[i]
    gain_grad = jnp.sum(total * normed, axis=0, keepdims=True)
    used = small.shape[0] - 8
    sums_ref[...] = jnp.zeros_like(sums_ref)
    sums_ref[:used, :] = small[:used].astype(BF16)
    second = lax.broadcasted_iota(jnp.int32, (8, shard), 0)
    sums_ref[used : used + 8, :] = jnp.where(second == 0, small[used:], jnp.where(second == 1, gain_grad, 0.0)).astype(BF16)


def last_norm(ranks, grad_ref, x_ref, misc_ref, grad_hidden_ref, out_ref):
    gain = gain_row(misc_ref, ranks, 0)
    grad = jnp.concatenate([grad_ref[i] for i in range(ranks)], axis=1)
    x = x_ref[...].astype(F32)
    scale = norm_scale(x)
    out_ref[...] = grad_hidden_ref[...] + norm_back(grad, x * scale, scale, gain)


def on_device(
    inputs,
    segment_ids,
    routes,
    expert_blocks,
    norm1_gain,
    q_weight,
    k_weight,
    value_matrix,
    o_weight,
    norm2_gain,
    router_weight,
    expert_gate_up,
    expert_down,
    out_grad,
):
    ranks, n_expert = lax.axis_size("dp"), lax.axis_size("expert")
    tokens, width = inputs.shape
    shard = q_weight.shape[0]
    slots, _, double = expert_gate_up.shape
    hidden = expert_down.shape[1]
    heads = Heads(ranks)
    group = ("dp", ranks // 2, 2)
    plane = ("expert", 4, n_expert // 4)
    used = n_expert * SLOT_STRIDE
    cosine, sine = rope_tables(tokens, heads)

    weights = jnp.concatenate(
        [w.reshape(shard, ranks, -1) for w in (q_weight, k_weight, value_matrix)], axis=2
    ).transpose(1, 0, 2)
    weights = jnp.pad(weights, ((0, 0), (0, 0), (0, heads.cols - weights.shape[2])))
    router = jnp.pad(router_weight, ((0, 0), (0, slots * n_expert - router_weight.shape[1])))
    router = router.reshape(shard, slots, n_expert).transpose(0, 2, 1)
    router = jnp.pad(router, ((0, 0), (0, 0), (0, SLOT_STRIDE - slots))).reshape(shard, used)
    router = jnp.pad(router, ((0, 0), (0, 128 - used)))
    blocks = jnp.pad(expert_blocks, (0, slots * n_expert - expert_blocks.shape[0])).reshape(slots, n_expert).T
    blocks = jnp.pad(blocks, ((0, 0), (0, SLOT_STRIDE - slots))).reshape(1, used)
    blocks = jnp.pad(blocks, ((0, 7), (0, 128 - used)))
    misc = jnp.concatenate(
        [
            jnp.stack([norm1_gain, norm2_gain]).astype(F32),
            jnp.zeros((6, shard), F32),
            jnp.pad(segment_ids.astype(F32), ((0, 7), (0, shard - tokens))),
        ]
    )

    def opening(*refs):
        take = taker(refs)
        ins, outs = take(5), take(5)
        x, w, rt, ms, og = ins
        x_all, w_all, rt_all, ms_all, og_all = outs
        dp, ex = Grid(*group), Grid(*plane)
        greet(dp.all() + ex.near())
        x_all[dp.me] = x[...]
        rt_all[dp.me] = rt[...]
        ms_all[dp.me] = ms[...]
        og_all[ex.me] = og[...]
        run(
            gather(dp, x, x_all, take(4)),
            gather(dp, ms, ms_all, take(4)),
            gather(dp, rt, rt_all, take(4)),
            exchange(dp, w, w_all, take(2)),
            gather(ex, og, og_all, take(4)),
        )

    x_all, w_all, router_all, misc_all, og_all = call(
        opening,
        "opening",
        [
            ((ranks, tokens, width), BF16),
            ((ranks, shard, heads.cols), BF16),
            ((ranks, shard, 128), BF16),
            ((ranks, 16, shard), F32),
            ((n_expert, tokens, width), BF16),
        ],
        (inputs, weights, router, misc, out_grad),
        line_sems(*group[1:]) * 3 + exchange_sems(ranks) + line_sems(*plane[1:]),
        cid=0,
        us=40,
    )

    part, qkv, att, scale_all = call(
        functools.partial(attention_forward, ranks, heads, tokens),
        "attention_forward",
        [
            ((ranks, tokens, width), BF16),
            ((ranks, tokens, heads.cols), BF16),
            ((ranks, tokens, heads.q_cols), BF16),
            ((ranks, tokens, 128), F32),
        ],
        (x_all, w_all, o_weight, misc_all, cosine, sine),
        us=15,
    )

    def branch_sum(*refs):
        take = taker(refs)
        terms, out = take(2)
        dp = Grid(*group)
        greet(dp.near())

        def finish(total):
            out[...] = total

        run(reduce(dp, lambda i: terms.at[i], finish, take(4), take(4)))

    (branch,) = call(
        branch_sum,
        "branch_sum",
        [((tokens, width), F32)],
        (part,),
        line_sems(*group[1:]) + sum_slots(*group[1:], (tokens, width)),
        cid=1,
        us=15,
    )

    hidden_rows, norm_hidden, scale_two, probs, meta = call(
        functools.partial(route_forward, ranks, n_expert, slots),
        "route_forward",
        [
            ((tokens, width), F32),
            ((tokens, width), BF16),
            ((tokens, 128), F32),
            ((tokens, 128), F32),
            ((2, used, tokens), F32),
        ],
        (inputs, branch, misc_all, router_all, routes, blocks),
        us=5,
    )

    def dispatch(*refs):
        take = taker(refs)
        (nh, mt), (nh_all, mt_all) = take(2), take(2)
        ex = Grid(*plane)
        greet(ex.near())
        nh_all[ex.me] = nh[...]
        mt_all[ex.me] = mt[...]
        run(gather(ex, nh, nh_all, take(4)), gather(ex, mt, mt_all, take(4)))

    norm_all, meta_all = call(
        dispatch,
        "dispatch",
        [((n_expert, tokens, width), BF16), ((n_expert, 2, used, tokens), F32)],
        (norm_hidden, meta),
        line_sems(*plane[1:]) * 2,
        cid=2,
        us=42,
    )

    fixed = lambda shape: pl.BlockSpec(shape, lambda s: (0,) * len(shape), pipeline_mode=pl.Buffered(1))
    moving = lambda shape: pl.BlockSpec((1,) + shape, lambda s: (s,) + (0,) * len(shape))
    packed = (n_expert, slots * SLOT_ROWS, width)
    out_part, back_part, gate_grad, d_up, d_down = call(
        functools.partial(experts, n_expert, slots, tokens),
        "experts",
        [
            ((n_expert, tokens, width), BF16),
            ((n_expert, tokens, width), BF16),
            ((n_expert, SLOT_STRIDE, tokens), F32),
            ((slots, width, double), BF16),
            ((slots, hidden, width), BF16),
        ],
        (norm_all, og_all, meta_all, expert_gate_up, expert_down),
        [pltpu.VMEM(packed, BF16)] * 4
        + [pltpu.VMEM((2, tokens, width), BF16)] * 2
        + [pltpu.SemaphoreType.DMA((2, 2))],
        us=50,
        grid=(slots,),
        in_specs=[
            pl.BlockSpec(memory_space=pl.ANY),
            pl.BlockSpec(memory_space=pl.ANY),
            fixed((n_expert, 2, used, tokens)),
            moving((width, double)),
            moving((hidden, width)),
        ],
        out_specs=[
            fixed((n_expert, tokens, width)),
            fixed((n_expert, tokens, width)),
            fixed((n_expert, SLOT_STRIDE, tokens)),
            moving((width, double)),
            moving((hidden, width)),
        ],
    )
    d_up = lax.psum_scatter(d_up, "dp", scatter_dimension=1, tiled=True).astype(F32)
    d_down = lax.psum_scatter(d_down, "dp", scatter_dimension=2, tiled=True).astype(F32)

    def combine(*refs):
        take = taker(refs)
        (terms, back_terms, gg), (out, back, gg_all) = take(3), take(3)
        ex = Grid(*plane)
        greet(ex.all())

        def finish(to):
            def store(total):
                to[...] = total

            return store

        run(
            exchange(ex, gg, gg_all, take(2)),
            reduce(ex, lambda i: back_terms.at[i], finish(back), take(4), take(4)),
            reduce(ex, lambda i: terms.at[i], finish(out), take(4), take(4)),
        )

    mixture, back, gate_grads = call(
        combine,
        "combine",
        [((tokens, width), F32), ((tokens, width), F32), ((n_expert, SLOT_STRIDE, tokens), F32)],
        (out_part, back_part, gate_grad),
        exchange_sems(n_expert) + (line_sems(*plane[1:]) + sum_slots(*plane[1:], (tokens, width))) * 2,
        cid=3,
        us=78,
    )

    output, grad_hidden, grad_branch, small = call(
        functools.partial(route_backward, ranks, n_expert, shard),
        "route_backward",
        [
            ((tokens, width), BF16),
            ((tokens, width), F32),
            ((tokens, width), BF16),
            ((ranks, used + 8, shard), F32),
        ],
        (hidden_rows, norm_hidden, scale_two, probs, misc_all, router_all, out_grad, mixture, back, gate_grads),
        us=6,
    )

    def share_branch(*refs):
        take = taker(refs)
        (br, sm), (br_all, sm_all) = take(2), take(2)
        dp = Grid(*group)
        greet(dp.all())
        br_all[dp.me] = br[...]
        run(gather(dp, br, br_all, take(4)), exchange(dp, sm, sm_all, take(2)))

    branch_all, small_all = call(
        share_branch,
        "share_branch",
        [((ranks, tokens, width), BF16), ((ranks, used + 8, shard), F32)],
        (grad_branch, small),
        line_sems(*group[1:]) + exchange_sems(ranks),
        cid=4,
        us=15,
    )

    grads, d_o = call(
        functools.partial(attention_backward, ranks, heads, tokens),
        "attention_backward",
        [((ranks, tokens, heads.cols), BF16), ((shard, width), BF16)],
        (branch_all, att, qkv, o_weight, misc_all, cosine, sine),
        us=15,
    )
    d_o = d_o.reshape(n_expert, shard // n_expert, width)

    def share_grads(*refs):
        take = taker(refs)
        (gr, do), (gr_all, do_all) = take(2), take(2)
        dp, ex = Grid(*group), Grid(*plane)
        greet(dp.near() + ex.near())
        gr_all[dp.me] = gr[...]
        run(
            gather(dp, gr, gr_all, take(4)),
            reduce_gather(ex, lambda i: do.at[i], do_all, take(), take(8), take(4)),
        )

    grads_all, d_o = call(
        share_grads,
        "share_grads",
        [((ranks, ranks, tokens, heads.cols), BF16), (d_o.shape, BF16)],
        (grads, d_o),
        line_sems(*group[1:])
        + [pltpu.VMEM(d_o.shape[1:], BF16)]
        + line_sems(*plane[1:]) * 2
        + sum_slots(*plane[1:], d_o.shape[1:]),
        cid=5,
        us=30,
    )

    x_cols = lax.dynamic_slice_in_dim(x_all.reshape(ranks * tokens, width), lax.axis_index("dp") * shard, shard, axis=1)
    sum_rows = 16 * n_expert
    grad_x, d_w, sums = call(
        functools.partial(projection_backward, ranks, heads, shard),
        "projection_backward",
        [
            ((ranks * tokens, shard), F32),
            ((shard, ranks * heads.cols), BF16),
            ((sum_rows, shard), BF16),
        ],
        (x_cols, scale_all.reshape(ranks * tokens, 128), misc, grads_all, weights, small_all),
        us=10,
    )
    grad_x = grad_x.reshape(ranks, tokens, shard)
    d_w = d_w.reshape(n_expert, shard // n_expert, ranks * heads.cols)
    sums = sums.reshape(n_expert, 16, shard)

    def closing(*refs):
        take = taker(refs)
        (gx, dw, sm), (gx_all, dw_all, sm_all) = take(3), take(3)
        dp, ex = Grid(*group), Grid(*plane)
        greet(dp.all() + ex.near())
        run(
            exchange(dp, gx, gx_all, take(2)),
            reduce_gather(ex, lambda i: sm.at[i], sm_all, take(), take(8), take(4)),
            reduce_gather(ex, lambda i: dw.at[i], dw_all, take(), take(8), take(4)),
        )

    grad_x, d_w, sums = call(
        closing,
        "closing",
        [(grad_x.shape, F32), (d_w.shape, BF16), (sums.shape, BF16)],
        (grad_x, d_w, sums),
        exchange_sems(ranks)
        + [pltpu.VMEM(sums.shape[1:], BF16)]
        + line_sems(*plane[1:]) * 2
        + sum_slots(*plane[1:], sums.shape[1:])
        + [pltpu.VMEM(d_w.shape[1:], BF16)]
        + line_sems(*plane[1:]) * 2
        + sum_slots(*plane[1:], d_w.shape[1:]),
        cid=6,
        us=55,
    )

    (grad_inputs,) = call(
        functools.partial(last_norm, ranks),
        "last_norm",
        [((tokens, width), F32)],
        (grad_x, inputs, misc_all, grad_hidden),
        us=4,
    )

    d_w = d_w.reshape(shard, ranks, heads.cols).astype(F32)
    first, second = heads.q_cols, heads.q_cols + heads.kv_cols
    d_q = d_w[:, :, :first].reshape(shard, -1)
    d_k = d_w[:, :, first:second].reshape(shard, -1)
    d_v = d_w[:, :, second : second + heads.kv_cols].reshape(shard, -1)
    d_o = d_o.reshape(shard, width).astype(F32)
    sums = sums.reshape(sum_rows, shard).astype(F32)
    d_router = sums[:used].reshape(n_expert, SLOT_STRIDE, shard)[:, :slots].transpose(2, 1, 0)
    d_router = d_router.reshape(shard, slots * n_expert)[:, : router_weight.shape[1]]
    return (output, grad_inputs, sums[used + 1], d_q, d_k, d_v, d_o, sums[used], d_router, d_up, d_down)


def solution(mesh):
    tokens = P(("dp", "expert"), None)
    rows = P("dp", None)
    return jax.shard_map(
        on_device,
        mesh=mesh,
        in_specs=(
            tokens,
            tokens,
            tokens,
            P(),
            P("dp"),
            rows,
            rows,
            rows,
            rows,
            P("dp"),
            rows,
            P("expert", None, None),
            P("expert", None, None),
            tokens,
        ),
        out_specs=(
            tokens,
            tokens,
            P("dp"),
            rows,
            rows,
            rows,
            rows,
            P("dp"),
            rows,
            P("expert", "dp", None),
            P("expert", None, "dp"),
        ),
        check_vma=False,
    )
```

time: 1400 us -> 566 us (0.40)
  waiting for transfers between devices: 1070 us -> 0.71 us
  Pallas kernels: 0 us -> 471 us
  matrix products: 109 us -> 0 us
  blocking collectives: 81 us -> 0 us
  starting transfers between devices: 20.3 us -> 0.08 us
  other arithmetic: 34.4 us -> 16.3 us
    reduce_scatter x7 -> x1, waiting for transfers between devices: 554 us -> 0.01 us  [on_device(): lax.psum_scatter(d_up, 'dp', scatter_dimension=1, tiled=True).astype(F32)]
    pallas_call x0 -> x14, Pallas kernels: none -> 471 us  [call(): pl.pallas_call(body, out_shape=[jax.ShapeDtypeStruct(shape, dtype) for sh...]
    all_to_all x4 -> x0, waiting for transfers between devices: 282 us -> none  [the longest x1 79.1 us: on_device(): lax.all_to_all(grad_xrows, 'expert', split_axis=0, concat_axis=0, tiled=T...]
    psum x1 -> x0, waiting for transfers between devices: 147 us -> none  [on_device(): lax.psum((grad_gain_one, grad_wq, grad_wk, grad_wv, grad_wo, grad_gain_tw...]
    dot_general x27 -> x0, matrix products: 109 us -> none  [the longest x1 17.6 us: on_device(): jnp.einsum('jscd,jscf->sdf', received, grad_gu, preferred_element_type=jn...]
    all_gather x4 -> x0, waiting for transfers between devices: 85.8 us -> none  [the longest x1 36.8 us: on_device(): lax.all_gather(q_weight, 'dp', axis=0, tiled=True)]
    psum x1 -> x0, blocking collectives: 41.9 us -> none  [on_device(): lax.psum((grad_gain_one, grad_wq, grad_wk, grad_wv, grad_wo, grad_gain_tw...]
    unnamed x130 -> x15, local copies, waits for them, and re-layouts: 14.8 us -> 43.6 us
  transfers between devices with their start and end apart: 16 -> 2, of which waited for: 14 -> 0; matrix products, arithmetic and copies ran while one was open for 9% -> 5% of each run, Pallas kernels for 0% -> 50%
where the time goes in v1:
time: 566 us; the launch traced here: 564 us
  Pallas kernels  471 us (83%)
  local copies, waits for them, and re-layouts  62.2 us (11%)
  other arithmetic  16.3 us (3%)
  between operations  14.2 us (3%)
    pallas_call x14, Pallas kernels, call(): pl.pallas_call(body, out_shape=[jax.ShapeDtypeStruct(shape, dtype) for sh...  471 us
    unnamed x15, local copies, waits for them, and re-layouts  43.6 us
  transfers between devices with their start and end apart: 2, of which 0 were waited for; matrix products, arithmetic and copies ran while one was open for 5% of the time, Pallas kernels for 50%

profile of v1, /device:TPU:0, one launch (start us, length us, event | category | flops | bytes accessed | tf_op | source)
XLA Modules:
  0.0 564.1 jit_solution(1370755346927319397)
XLA Ops:
  20.5 74.3 %opening.1 = (bf16[4,128,1536]{2,1,0:T(8,128)(2,1)}, bf16[4,384,640]{2,1,0:T(8,128)(2,1)}, bf16[4,384,128]{2,1,0:T(8,128)(2,1)}, f32[4,16,384]{2,1,0:T(8,128)}, bf16[8,128,1536]{2,1,0:T(8,128)(2,1)}) custom-call(bf16[128,1536]{1,0:T(8,128)(2,1)} %x_ref.3, bf16[4,384,640]{2,1,0:T(8,128)(2,1)} %maximum_bitcast_fusion.refs_1_.w_ref, ...), custom_call_target="tpu_custom_call" | custom-call | bytes 120000000 | tf_op jit(solution)/shard_map/opening/pallas_call | solution.py:351
  94.8 10.6 %attention_forward.1 = (bf16[4,128,1536]{2,1,0:T(8,128)(2,1)}, bf16[4,128,640]{2,1,0:T(8,128)(2,1)}, bf16[4,128,384]{2,1,0:T(8,128)(2,1)}, f32[4,128,128]{2,1,0:T(8,128)}) custom-call(bf16[4,128,1536]{2,1,0:T(8,128)(2,1)} %get-tuple-element.51.x_ref, bf16[4,384,640]{2,1,0:T(8,128)(2,1)} %get-tuple-element.52.w_ref, bf16[384,1536]{1,0:T(8,128)(2,1)} %o_ref.3, ...), custom_call_target="tpu_custom_call" | custom-call | bytes 45000000 | tf_op jit(solution)/shard_map/attention_forward/pallas_call | solution.py:351
  105.4 15.1 %branch_sum.1.branch_ref = f32[128,1536]{1,0:T(8,128)} custom-call(bf16[4,128,1536]{2,1,0:T(8,128)(2,1)} %get-tuple-element.54.refs_0_), custom_call_target="tpu_custom_call" | custom-call | bytes 45000000 | tf_op jit(solution)/shard_map/branch_sum/pallas_call | solution.py:351
  120.5 2.9 route_forward.1
  123.4 46.2 %dispatch.1 = (bf16[8,128,1536]{2,1,0:T(8,128)(2,1)}, f32[8,2,64,128]{3,2,1,0:T(8,128)}) custom-call(bf16[128,1536]{1,0:T(8,128)(2,1)} %get-tuple-element.57.refs_0_.norm_ref, f32[2,64,128]{2,1,0:T(8,128)} %get-tuple-element.60.refs_1_), custom_call_target="tpu_custom_call" | custom-call | bytes 126000000 | tf_op jit(solution)/shard_map/dispatch/pallas_call | solution.py:351
  169.6 39.5 %experts.1 = (bf16[8,128,1536]{2,1,0:T(8,128)(2,1)}, bf16[8,128,1536]{2,1,0:T(8,128)(2,1)}, f32[8,8,128]{2,1,0:T(8,128)}, bf16[5,1536,1024]{2,1,0:T(8,128)(2,1)}, bf16[5,512,1536]{2,1,0:T(8,128)(2,1)}) custom-call(bf16[8,128,1536]{2,1,0:T(8,128)(2,1)} %get-tuple-element.61.nh_ref, bf16[8,128,1536]{2,1,0:T(8,128)(2,1)} %get-tuple-element.62.og_ref, ...), custom_call_target="tpu_custom_call" | custom-call | bytes 150000000 | tf_op jit(solution)/shard_map/experts/pallas_call | solution.py:351
  209.1 15.7 %copy.63 = bf16[5,512,1536]{1,0,2:T(8,128)(2,1)} copy(bf16[5,512,1536]{2,1,0:T(8,128)(2,1)} %get-tuple-element.90) | data formatting | bytes 15728640
  224.8 13.0 %copy.70 = bf16[192,8,5,512]{3,1,2,0:T(8,128)(2,1)} copy(bf16[192,8,5,512]{3,2,1,0:T(8,128)(2,1)} %bitcast.39) | data formatting | bytes 15728640
  238.6 91.1 %combine.1 = (f32[128,1536]{1,0:T(8,128)}, f32[128,1536]{1,0:T(8,128)}, f32[8,8,128]{2,1,0:T(8,128)}) custom-call(bf16[8,128,1536]{2,1,0:T(8,128)(2,1)} %get-tuple-element.64.refs_0_, bf16[8,128,1536]{2,1,0:T(8,128)(2,1)} %get-tuple-element.65.refs_1_, f32[8,8,128]{2,1,0:T(8,128)} %get-tuple-element.66.refs_2_), custom_call_target="tpu_custom_call" | custom-call | bytes 234000000 | tf_op jit(solution)/shard_map/combine/pallas_call | solution.py:351
  329.7 4.0 route_backward.1
  333.7 33.7 %share_branch.1 = (bf16[4,128,1536]{2,1,0:T(8,128)(2,1)}, f32[4,72,384]{2,1,0:T(8,128)}) custom-call(bf16[128,1536]{1,0:T(8,128)(2,1)} %get-tuple-element.72.refs_0_, f32[4,72,384]{2,1,0:T(8,128)} %get-tuple-element.73.refs_1_), custom_call_target="tpu_custom_call" | custom-call | bytes 45000000 | tf_op jit(solution)/shard_map/share_branch/pallas_call | solution.py:351
  367.5 12.0 %attention_backward.1 = (bf16[4,128,640]{2,1,0:T(8,128)(2,1)}, bf16[384,1536]{1,0:T(8,128)(2,1)}) custom-call(bf16[4,128,1536]{2,1,0:T(8,128)(2,1)} %get-tuple-element.74.branch_ref, bf16[4,128,384]{2,1,0:T(8,128)(2,1)} %get-tuple-element.75.att_ref, bf16[4,128,640]{2,1,0:T(8,128)(2,1)} %get-tuple-element.76.qkv_ref, bf16[384,1536]{1,0:T(8,128)(2,1)} %o_ref.3, ...), custom_call_target="tpu_custom_call" | custom-call | bytes 45000000 | tf_op jit(solution)/shard_map/attention_backward/pallas_call | solution.py:351
  379.5 66.3 %share_grads.1 = (bf16[4,4,128,640]{3,2,1,0:T(8,128)(2,1)}, bf16[8,48,1536]{2,1,0:T(8,128)(2,1)}) custom-call(bf16[4,128,640]{2,1,0:T(8,128)(2,1)} %get-tuple-element.77.refs_0_, bf16[8,48,1536]{2,1,0:T(8,128)(2,1)} %bitcast.51), custom_call_target="tpu_custom_call" | custom-call | bytes 90000000 | tf_op jit(solution)/shard_map/share_grads/pallas_call | solution.py:351
  445.8 1.8 constant_dynamic-slice_fusion.x_ref
  447.6 7.0 %projection_backward.1 = (f32[512,384]{1,0:T(8,128)}, bf16[384,2560]{1,0:T(8,128)(2,1)}, bf16[128,384]{1,0:T(8,128)(2,1)}) custom-call(bf16[512,384]{1,0:T(8,128)(2,1)} %constant_dynamic-slice_fusion.x_ref, f32[512,128]{1,0:T(8,128)} %bitcast.54, f32[16,384]{1,0:T(8,128)} %select_maximum_fusion.refs_3_.gain_ref, ...), custom_call_target="tpu_custom_call" | custom-call | bytes 30000000 | tf_op jit(solution)/shard_map/projection_backward/pallas_call | solution.py:351
  454.6 65.2 %closing.1 = (f32[4,128,384]{2,1,0:T(8,128)}, bf16[8,48,2560]{2,1,0:T(8,128)(2,1)}, bf16[8,16,384]{2,1,0:T(8,128)(2,1)}) custom-call(f32[4,128,384]{2,1,0:T(8,128)} %bitcast.52, bf16[8,48,2560]{2,1,0:T(8,128)(2,1)} %bitcast.48, bf16[8,16,384]{2,1,0:T(8,128)(2,1)} %bitcast.56), custom_call_target="tpu_custom_call" | custom-call | bytes 165000000 | tf_op jit(solution)/shard_map/closing/pallas_call | solution.py:351
  522.8 4.7 reshape.104
  527.5 1.7 slice-done
  530.7 2.7 last_norm.1
  538.1 1.8 bitcast_convert_fusion
  539.9 4.3 reshape.107
  544.3 3.0 copy.64
  547.2 3.7 convert_element_type.45
  551.0 6.3 %convert_element_type.44 = f32[5,384,1024]{2,1,0:T(8,128)} convert(bf16[5,384,1024]{2,1,0:T(8,128)(2,1)} %reduce-scatter.5.cloned.1.call-done) | non-fusion elementwise | flops 1966080 | bytes 11796480 | tf_op jit(solution)/shard_map/convert_element_type | solution.py:880
  (43 shorter events, 23.3 us)
Async XLA Ops:
  7.2 8.9 %copy-start.1 = (bf16[384,1536]{1,0:T(8,128)(2,1)S(1)}, bf16[384,1536]{1,0:T(8,128)(2,1)}, u32[]{:S(2)}) copy-start(bf16[384,1536]{1,0:T(8,128)(2,1)} %param.21) | copy-start | bytes 3538948
  7.2 532.7 %reduce-scatter.7.cloned.1.call-start = ((), (), s32[]{:S(2)}) async-start(), calls=%async_computation.3 | async-start | bytes 9830400
  237.9 313.1 %reduce-scatter.5.cloned.1.call-start = ((), (), s32[]{:S(2)}) async-start(), calls=%async_computation.2 | async-start | bytes 19660800 | tf_op jit(solution)/shard_map/reduce_scatter | solution.py:880
  527.5 1.7 slice-start
  536.3 1.8 copy-start
Sparse Core Ops, SparseCore 0:
  238.0 67.0 reduce-scatter.6
  307.7 143.6 reduce-scatter.4

commit v2 on v1

--- a/solution.py
+++ b/solution.py
@@ -93,6 +93,11 @@
     )
 
 
+def begin(step):
+    next(step)
+    return step
+
+
 def run(*steps):
     steps = list(steps)
     while steps:
@@ -111,7 +116,7 @@
     return [dma((2, A)), dma((2, A)), dma((2, A, B)), dma((2, A, B))]
 
 
-def gather(g, own, out, sems):
+def gather(g, own, out, sems, arrived=lambda i, block: None):
     send_a, recv_a, send_b, recv_b = sems
     A, B = g.A, g.B
     row = lambda way, k: g.a - k if way == 0 else g.a + k
@@ -145,6 +150,7 @@
         along_a(way, 0, own, start)
     for way in (0, 1):
         along_b(way, 0, g.a, g.me, own, start)
+    arrived(g.me, own)
     yield
     for k in range(1, A):
         for way in (0, 1):
@@ -156,6 +162,7 @@
                 along_a(way, k, out.at[i], start)
                 for w in (0, 1):
                     along_b(w, 0, row(way, k), i, out.at[i], start)
+                arrived(i, out.at[i])
 
             yield
     for j in range(1, B):
@@ -168,6 +175,7 @@
                     a = row(way, k)
                     remote(out.at[i], out.at[i], send_b.at[w, a, j], recv_b.at[w, a, j], g.here()).wait_recv()
                     along_b(w, j, a, i, out.at[i], start)
+                    arrived(i, out.at[i])
 
             yield
     for way, k in rows:
@@ -323,6 +331,30 @@
 
 def exchange_sems(n):
     return [pltpu.SemaphoreType.DMA((n,)), pltpu.SemaphoreType.DMA((n,))]
+
+
+def pass_slices(g, out, sems):
+    send, recv = sems
+    n = g.A * g.B
+
+    def copies(i, block):
+        for r in range(1, n):
+            to = (g.me + r) % n
+            yield remote(block.at[to], out.at[g.me, i], send.at[i, r], recv.at[i, r], {g.axis: to})
+
+    def arrived(i, block):
+        for copy in copies(i, block):
+            copy.start()
+
+    def end(blocks, block):
+        for i in blocks:
+            for r in range(1, n):
+                mine = out.at[(g.me + n - r) % n, i]
+                remote(mine, mine, send.at[i, r], recv.at[i, r], g.here()).wait_recv()
+            for copy in copies(i, block):
+                copy.wait_send()
+
+    return arrived, end
 
 
 def exchange(g, part, out, sems):
@@ -343,8 +375,12 @@
         copy.wait_send()
 
 
+VMEM = pl.BlockSpec(memory_space=pltpu.VMEM)
+ANY = pl.BlockSpec(memory_space=pl.ANY)
+
+
 def call(body, name, outs, ins, scratch=(), cid=None, us=10.0, **grid):
-    whole = pl.BlockSpec(memory_space=pltpu.VMEM)
+    whole = VMEM
     params = dict(vmem_limit_bytes=VMEM_MOST)
     if cid is not None:
         params |= dict(collective_id=cid, has_side_effects=True)
@@ -477,34 +513,51 @@
     lax.fori_loop(0, ranks, one, 0)
 
 
-def route_tables(n_expert, slots, routes, blocks):
-    tokens = routes.shape[0]
+def column_experts(n_expert, slots):
     column = lax.broadcasted_iota(jnp.int32, (1, 128), 1)
     owner, slot = column // SLOT_STRIDE, column % SLOT_STRIDE
     expert = slot * n_expert + owner
     real = (owner < n_expert) & (slot < slots) & (expert < EXPERT_COUNT)
-    expert = jnp.where(real, expert, -1)
+    return real, jnp.where(real, expert, -1)
+
+
+def column_picks(n_expert, slots):
+    _, expert = column_experts(n_expert, slots)
+    return jnp.where(lax.broadcasted_iota(jnp.int32, (EXPERT_COUNT, 128), 0) == expert, 1.0, 0.0)
+
+
+def route_tables(expert, routes, blocks_ref):
+    tokens = routes.shape[0]
     named = jnp.zeros((tokens, 128), F32)
     for k in range(routes.shape[1]):
         named = named + jnp.where(routes[:, k : k + 1] == expert, 1.0, 0.0)
+    limit = jnp.zeros((1, 128), jnp.int32)
+    for e in range(EXPERT_COUNT):
+        limit = jnp.where(expert == e, blocks_ref[e] * BLK, limit)
     rows = lax.broadcasted_iota(jnp.int32, (tokens, tokens), 0)
     cols = lax.broadcasted_iota(jnp.int32, (tokens, tokens), 1)
     earlier = jnp.where(cols < rows, 1.0, 0.0).astype(BF16)
     rank = dot(earlier, named.astype(BF16))
-    kept = (named > 0.0) & (rank < (blocks * BLK).astype(F32))
-    return real, kept, jnp.where(kept, rank, -1.0)
-
-
-def route_forward(ranks, n_expert, slots, x_ref, branch_ref, misc_ref, router_ref, routes_ref, blocks_ref, hidden_ref, norm_ref, scale_ref, probs_ref, meta_ref):
+    kept = (named > 0.0) & (rank < limit.astype(F32))
+    return kept, jnp.where(kept, rank, -1.0)
+
+
+def route_forward(ranks, n_expert, slots, x_ref, branch_ref, misc_ref, router_ref, routes_ref, blocks_ref, hidden_ref, norm_ref, scale_ref, probs_ref, meta_ref, table_ref):
     gain = gain_row(misc_ref, ranks, 1)
+    width = x_ref.shape[1]
+    shard = width // ranks
     hidden = x_ref[...].astype(F32) + RESIDUAL_SCALE * branch_ref[...]
     hidden_ref[...] = hidden
     scale = norm_scale(hidden)
     scale_ref[...] = jnp.broadcast_to(scale, scale_ref.shape)
-    norm_ref[...] = (hidden * scale * gain).astype(BF16)
-    real, kept, place = route_tables(n_expert, slots, routes_ref[...], blocks_ref[0:1, :])
-    router = router_ref[...].reshape(-1, 128)
-    logits = jnp.where(real, dot(norm_ref[...], router), MASKED_SCORE)
+    norm = (hidden * scale * gain).astype(BF16)
+    for i in range(ranks):
+        norm_ref[i] = norm[:, i * shard : (i + 1) * shard]
+    real, expert = column_experts(n_expert, slots)
+    kept, place = route_tables(expert, routes_ref[...], blocks_ref)
+    router = router_ref[...].reshape(width, -1)
+    table_ref[...] = dot(router, column_picks(n_expert, slots).astype(BF16)).astype(BF16)
+    logits = jnp.where(real, dot(norm, table_ref[...]), MASKED_SCORE)
     weight = jnp.exp(logits - jnp.max(logits, axis=-1, keepdims=True))
     probs = weight / jnp.sum(weight, axis=-1, keepdims=True)
     probs_ref[...] = probs
@@ -513,10 +566,22 @@
     meta_ref[1] = jnp.where(kept, probs, 0.0).T[:used]
 
 
-def experts(n_expert, slots, tokens, nh_ref, og_ref, meta_ref, up_ref, down_ref, out_ref, back_ref, gate_grad_ref, d_up_ref, d_down_ref, x_sc, og_sc, eo_sc, gx_sc, nh_in, og_in, sems):
+def row_picks(slots, place):
+    number = lax.broadcasted_iota(jnp.int32, (SLOT_ROWS, place.shape[1]), 0).astype(F32)
+    return jnp.concatenate([jnp.where(number == place[s : s + 1], 1.0, 0.0) for s in range(slots)], axis=0)
+
+
+def row_shares(slots, share):
+    return jnp.concatenate(
+        [jnp.broadcast_to(share[s : s + 1], (SLOT_ROWS, share.shape[1])) for s in range(slots)], axis=0
+    )
+
+
+def experts(n_expert, slots, tokens, nh_ref, og_ref, meta_ref, up_ref, down_ref, out_ref, back_ref, gate_grad_ref, inner_ref, both_ref, x_sc, og_sc, eo_sc, gx_sc, nh_in, og_in, sems):
     step = pl.program_id(0)
     mine = pl.ds(pl.multiple_of(lax.axis_index("expert") * SLOT_STRIDE, SLOT_STRIDE), SLOT_STRIDE)
-    width = nh_ref.shape[2]
+    ranks, _, shard = nh_ref.shape[1:]
+    width = ranks * shard
     hidden = down_ref.shape[1]
 
     def fetch(q):
@@ -526,13 +591,6 @@
             pltpu.make_async_copy(og_ref.at[q], og_in.at[slot], sems.at[1, slot]),
         ]
 
-    packed = slots * SLOT_ROWS
-    number = lax.broadcasted_iota(jnp.int32, (SLOT_ROWS, tokens), 0).astype(F32)
-
-    def picks(q):
-        place = meta_ref[q, 0, mine, :]
-        return jnp.concatenate([jnp.where(number == place[s : s + 1], 1.0, 0.0) for s in range(slots)], axis=0)
-
     @pl.when(step == 0)
     def _():
         for copy in fetch(0):
@@ -546,9 +604,11 @@
 
             for copy in fetch(q):
                 copy.wait()
-            pick = picks(q).astype(BF16)
-            x_sc[q] = dot(pick, nh_in[q % 2]).astype(BF16)
-            og_sc[q] = dot(pick, og_in[q % 2]).astype(BF16)
+            pick = row_picks(slots, meta_ref[q, 0, mine, :]).astype(BF16)
+            for i in range(ranks):
+                here = slice(i * shard, (i + 1) * shard)
+                x_sc[q, :, here] = dot(pick, nh_in[q % 2, i]).astype(BF16)
+                og_sc[q, :, here] = dot(pick, og_in[q % 2, i]).astype(BF16)
             gate_grad_ref[q] = jnp.zeros((SLOT_STRIDE, tokens), F32)
             return carry
 
@@ -556,12 +616,14 @@
 
     place_of = pl.ds(pl.multiple_of(step * SLOT_ROWS, SLOT_ROWS), SLOT_ROWS)
     slot_row = lax.broadcasted_iota(jnp.int32, (SLOT_STRIDE, tokens), 0) == step
+    number = lax.broadcasted_iota(jnp.int32, (SLOT_ROWS, tokens), 0).astype(F32)
     rows = n_expert * SLOT_ROWS
     x = x_sc[:, place_of, :].reshape(rows, width)
     both = dot(x, up_ref[0])
     gate, up = both[:, :hidden], both[:, hidden:]
     squash = jax.nn.sigmoid(gate)
     inner = (gate * squash * up).astype(BF16)
+    inner_ref[0] = inner
     produced = dot(inner, down_ref[0]).astype(BF16)
     eo_sc[:, place_of, :] = produced.reshape(n_expert, SLOT_ROWS, width)
     masks, gates = [], []
@@ -580,22 +642,14 @@
     grad_both = jnp.concatenate(
         [grad_inner * up * squash * (1.0 + gate * (1.0 - squash)), grad_inner * (gate * squash)], axis=1
     ).astype(BF16)
+    both_ref[0] = grad_both
     gx_sc[:, place_of, :] = dot(grad_both, up_ref[0], ((1,), (1,))).astype(BF16).reshape(n_expert, SLOT_ROWS, width)
-    tile = 256
-    for i in range(width // tile):
-        here = slice(i * tile, (i + 1) * tile)
-        d_up_ref[0, here, :] = dot(x[:, here], grad_both, ((0,), (0,))).astype(d_up_ref.dtype)
-    for i in range(hidden // tile):
-        here = slice(i * tile, (i + 1) * tile)
-        d_down_ref[0, here, :] = dot(inner[:, here], grad_rows, ((0,), (0,))).astype(d_down_ref.dtype)
 
     @pl.when(step == slots - 1)
     def _():
         def one(q, carry):
-            pick = picks(q)
-            share = meta_ref[q, 1, mine, :]
-            share = jnp.concatenate([jnp.broadcast_to(share[s : s + 1], (SLOT_ROWS, tokens)) for s in range(slots)], axis=0)
-            high, low = halves(pick * share)
+            pick = row_picks(slots, meta_ref[q, 0, mine, :])
+            high, low = halves(pick * row_shares(slots, meta_ref[q, 1, mine, :]))
             over = ((0,), (0,))
             out_ref[q] = (dot(high, eo_sc[q], over) + dot(low, eo_sc[q], over)).astype(BF16)
             back_ref[q] = dot(pick.astype(BF16), gx_sc[q], over).astype(BF16)
@@ -617,7 +671,7 @@
     probs = probs_ref[...]
     grad_logits = probs * (grad_probs - jnp.sum(probs * grad_probs, axis=1, keepdims=True))
     high, low = halves(grad_logits)
-    router = router_ref[...].reshape(width, 128)
+    router = router_ref[...]
     across = ((1,), (1,))
     grad_norm = back_ref[...] + (dot(high, router, across) + dot(low, router, across))
     scale = scale_ref[:, 0:1]
@@ -626,12 +680,11 @@
     grad_hidden_ref[...] = grad_hidden
     branch_ref[...] = (RESIDUAL_SCALE * grad_hidden).astype(BF16)
     over = ((0,), (0,))
-    norm = norm_ref[...]
-    grad_router = dot(high, norm, over) + dot(low, norm, over)
     grad_gain = jnp.sum(grad_norm * normed, axis=0, keepdims=True)
     for i in range(ranks):
         here = slice(i * shard, (i + 1) * shard)
-        small_ref[i, :used, :] = grad_router[:used, here]
+        grad_router = dot(high, norm_ref[i], over) + dot(low, norm_ref[i], over)
+        small_ref[i, :used, :] = grad_router[:used]
         small_ref[i, used:, :] = jnp.broadcast_to(grad_gain[:, here], (8, shard))
 
 
@@ -687,12 +740,78 @@
     sums_ref[used : used + 8, :] = jnp.where(second == 0, small[used:], jnp.where(second == 1, gain_grad, 0.0)).astype(BF16)
 
 
-def last_norm(ranks, grad_ref, x_ref, misc_ref, grad_hidden_ref, out_ref):
-    gain = gain_row(misc_ref, ranks, 0)
-    grad = jnp.concatenate([grad_ref[i] for i in range(ranks)], axis=1)
-    x = x_ref[...].astype(F32)
-    scale = norm_scale(x)
-    out_ref[...] = grad_hidden_ref[...] + norm_back(grad, x * scale, scale, gain)
+def finish(ranks, n_expert, slots, heads, tokens, nh_ref, og_ref, xd_ref, ogd_ref, meta_ref, own_both_ref, both_ref, own_inner_ref, inner_ref, grad_ref, x_ref, misc_ref, grad_hidden_ref, d_w_ref, d_o_ref, sums_ref, d_up_ref, d_down_ref, grad_inputs_ref, q_ref, k_ref, v_ref, o_ref, router_ref, gain_one_ref, gain_two_ref, x_sc, og_sc, x_in, og_in, sems):
+    step = pl.program_id(0)
+    me = lax.axis_index("dp")
+    rows = n_expert * SLOT_ROWS
+    shard = x_in.shape[2]
+
+    @pl.when(step == 0)
+    def _():
+        def fetch(j, q, do):
+            at, slot = (me + j) % ranks, q % 2
+
+            def both(x, og):
+                do(pltpu.make_async_copy(x, x_in.at[slot], sems.at[0, slot]))
+                do(pltpu.make_async_copy(og, og_in.at[slot], sems.at[1, slot]))
+
+            if j == 0:
+                both(nh_ref.at[q, me], og_ref.at[q, me])
+            else:
+                both(xd_ref.at[at, q], ogd_ref.at[at, q])
+
+        for j in range(ranks):
+            fetch(j, 0, lambda copy: copy.start())
+
+            def one(q, carry):
+                @pl.when(q + 1 < n_expert)
+                def _():
+                    fetch(j, q + 1, lambda copy: copy.start())
+
+                fetch(j, q, lambda copy: copy.wait())
+                at = (me + j) % ranks
+                pick = row_picks(slots, meta_ref[at, q, 0])
+                share = jnp.sum(pick * row_shares(slots, meta_ref[at, q, 1]), axis=1, keepdims=True)
+                pick = pick.astype(BF16)
+                x_sc[j, q] = dot(pick, x_in[q % 2]).astype(BF16)
+                og_sc[j, q] = (share * (RESIDUAL_SCALE * dot(pick, og_in[q % 2]))).astype(BF16)
+                return carry
+
+            lax.fori_loop(0, n_expert, one, 0)
+        gain = gain_row(misc_ref, ranks, 0)
+        grad = jnp.concatenate([grad_ref[i] for i in range(ranks)], axis=1)
+        x = x_ref[...].astype(F32)
+        scale = norm_scale(x)
+        grad_inputs_ref[...] = grad_hidden_ref[...] + norm_back(grad, x * scale, scale, gain)
+        first, second = heads.q_cols, heads.q_cols + heads.kv_cols
+        for i in range(ranks):
+            start = i * heads.cols
+            q_ref[:, i * heads.q_cols : (i + 1) * heads.q_cols] = d_w_ref[:, start : start + first].astype(F32)
+            here = slice(i * heads.kv_cols, (i + 1) * heads.kv_cols)
+            k_ref[:, here] = d_w_ref[:, start + first : start + second].astype(F32)
+            v_ref[:, here] = d_w_ref[:, start + second : start + second + heads.kv_cols].astype(F32)
+        o_ref[...] = d_o_ref[...].astype(F32)
+        used = n_expert * SLOT_STRIDE
+        picks = column_picks(n_expert, slots).astype(BF16)
+        router_ref[...] = lax.dot_general(
+            sums_ref[:128], picks, (((0,), (1,)), ((), ())), preferred_element_type=F32
+        )
+        ends = sums_ref[used : used + 16, :].astype(F32)
+        gain_two_ref[...] = ends[0:1]
+        gain_one_ref[...] = ends[1:2]
+
+    place_of = pl.ds(pl.multiple_of(step * SLOT_ROWS, SLOT_ROWS), SLOT_ROWS)
+    over = ((0,), (0,))
+    d_up = d_down = None
+    for j in range(ranks):
+        at = (me + j) % ranks
+        x = x_sc[j, :, place_of, :].reshape(rows, shard)
+        og = og_sc[j, :, place_of, :].reshape(rows, shard)
+        up = dot(x, own_both_ref[0] if j == 0 else both_ref[at, 0], over)
+        down = dot(own_inner_ref[0] if j == 0 else inner_ref[at, 0], og, over)
+        d_up, d_down = (up, down) if j == 0 else (d_up + up, d_down + down)
+    d_up_ref[0] = d_up
+    d_down_ref[0] = d_down
 
 
 def on_device(
@@ -722,56 +841,52 @@
     used = n_expert * SLOT_STRIDE
     cosine, sine = rope_tables(tokens, heads)
 
-    weights = jnp.concatenate(
-        [w.reshape(shard, ranks, -1) for w in (q_weight, k_weight, value_matrix)], axis=2
-    ).transpose(1, 0, 2)
-    weights = jnp.pad(weights, ((0, 0), (0, 0), (0, heads.cols - weights.shape[2])))
-    router = jnp.pad(router_weight, ((0, 0), (0, slots * n_expert - router_weight.shape[1])))
-    router = router.reshape(shard, slots, n_expert).transpose(0, 2, 1)
-    router = jnp.pad(router, ((0, 0), (0, 0), (0, SLOT_STRIDE - slots))).reshape(shard, used)
-    router = jnp.pad(router, ((0, 0), (0, 128 - used)))
-    blocks = jnp.pad(expert_blocks, (0, slots * n_expert - expert_blocks.shape[0])).reshape(slots, n_expert).T
-    blocks = jnp.pad(blocks, ((0, 0), (0, SLOT_STRIDE - slots))).reshape(1, used)
-    blocks = jnp.pad(blocks, ((0, 7), (0, 128 - used)))
-    misc = jnp.concatenate(
-        [
-            jnp.stack([norm1_gain, norm2_gain]).astype(F32),
-            jnp.zeros((6, shard), F32),
-            jnp.pad(segment_ids.astype(F32), ((0, 7), (0, shard - tokens))),
-        ]
-    )
+    gains = jnp.stack([norm1_gain, norm2_gain]).astype(F32)
 
     def opening(*refs):
         take = taker(refs)
-        ins, outs = take(5), take(5)
-        x, w, rt, ms, og = ins
-        x_all, w_all, rt_all, ms_all, og_all = outs
+        x, wq, wk, wv, rt, gn, sg, og = take(8)
+        x_all, w, w_all, rt_all, ms_all, og_all, ms, og_own = take(8)
         dp, ex = Grid(*group), Grid(*plane)
-        greet(dp.all() + ex.near())
+        for i in range(ranks):
+            at = 0
+            for ref, cols in ((wq, heads.q_cols), (wk, heads.kv_cols), (wv, heads.kv_cols)):
+                w[i, :, at : at + cols] = ref[:, i * cols : (i + 1) * cols]
+                at += cols
+            if at < heads.cols:
+                w[i, :, at:] = jnp.zeros((shard, heads.cols - at), BF16)
+            og_own[i] = og[:, i * shard : (i + 1) * shard]
+        ms[...] = jnp.zeros_like(ms)
+        ms[0:2, :] = gn[...]
+        ms[8:9, :tokens] = sg[...].astype(F32)
         x_all[dp.me] = x[...]
         rt_all[dp.me] = rt[...]
         ms_all[dp.me] = ms[...]
-        og_all[ex.me] = og[...]
-        run(
-            gather(dp, x, x_all, take(4)),
-            gather(dp, ms, ms_all, take(4)),
-            gather(dp, rt, rt_all, take(4)),
-            exchange(dp, w, w_all, take(2)),
-            gather(ex, og, og_all, take(4)),
-        )
-
-    x_all, w_all, router_all, misc_all, og_all = call(
+        og_all[ex.me] = og_own[...]
+        greet(dp.all() + ex.near())
+        small = [begin(gather(dp, ms, ms_all, take(4))), begin(gather(dp, rt, rt_all, take(4)))]
+        xs = begin(gather(dp, x, x_all, take(4)))
+        ogs = begin(gather(ex, og_own, og_all, take(4)))
+        ws = begin(exchange(dp, w, w_all, take(2)))
+        run(*small, xs, ogs)
+        run(ws)
+
+    x_all, weights, w_all, router_all, misc_all, og_all = call(
         opening,
         "opening",
         [
             ((ranks, tokens, width), BF16),
             ((ranks, shard, heads.cols), BF16),
-            ((ranks, shard, 128), BF16),
+            ((ranks, shard, heads.cols), BF16),
+            ((ranks, shard, router_weight.shape[1]), BF16),
             ((ranks, 16, shard), F32),
-            ((n_expert, tokens, width), BF16),
+            ((n_expert, ranks, tokens, shard), BF16),
         ],
-        (inputs, weights, router, misc, out_grad),
-        line_sems(*group[1:]) * 3 + exchange_sems(ranks) + line_sems(*plane[1:]),
+        (inputs, q_weight, k_weight, value_matrix, router_weight, gains, segment_ids, out_grad),
+        [pltpu.VMEM((16, shard), F32), pltpu.VMEM((ranks, tokens, shard), BF16)]
+        + line_sems(*group[1:]) * 3
+        + line_sems(*plane[1:])
+        + exchange_sems(ranks),
         cid=0,
         us=40,
     )
@@ -810,81 +925,87 @@
         us=15,
     )
 
-    hidden_rows, norm_hidden, scale_two, probs, meta = call(
+    hidden_rows, norm_hidden, scale_two, probs, meta, router = call(
         functools.partial(route_forward, ranks, n_expert, slots),
         "route_forward",
         [
             ((tokens, width), F32),
-            ((tokens, width), BF16),
+            ((ranks, tokens, shard), BF16),
             ((tokens, 128), F32),
             ((tokens, 128), F32),
             ((2, used, tokens), F32),
+            ((width, 128), BF16),
         ],
-        (inputs, branch, misc_all, router_all, routes, blocks),
+        (inputs, branch, misc_all, router_all, routes, expert_blocks),
         us=5,
+        in_specs=[VMEM] * 5 + [pl.BlockSpec(memory_space=pltpu.SMEM)],
     )
 
     def dispatch(*refs):
         take = taker(refs)
-        (nh, mt), (nh_all, mt_all) = take(2), take(2)
-        ex = Grid(*plane)
-        greet(ex.near())
+        (nh, mt), (nh_all, mt_all, xd) = take(2), take(3)
+        dp, ex = Grid(*group), Grid(*plane)
         nh_all[ex.me] = nh[...]
         mt_all[ex.me] = mt[...]
-        run(gather(ex, nh, nh_all, take(4)), gather(ex, mt, mt_all, take(4)))
-
-    norm_all, meta_all = call(
+        greet(dp.all() + ex.near())
+        arrived, end = pass_slices(dp, xd, take(2))
+        run(gather(ex, nh, nh_all, take(4), arrived), gather(ex, mt, mt_all, take(4)))
+        end(range(n_expert), nh)
+
+    norm_all, meta_all, norm_slices = call(
         dispatch,
         "dispatch",
-        [((n_expert, tokens, width), BF16), ((n_expert, 2, used, tokens), F32)],
+        [
+            ((n_expert, ranks, tokens, shard), BF16),
+            ((n_expert, 2, used, tokens), F32),
+            ((ranks, n_expert, tokens, shard), BF16),
+        ],
         (norm_hidden, meta),
-        line_sems(*plane[1:]) * 2,
+        [pltpu.SemaphoreType.DMA((n_expert, ranks))] * 2 + line_sems(*plane[1:]) * 2,
         cid=2,
         us=42,
+        out_specs=[VMEM, VMEM, ANY],
     )
 
     fixed = lambda shape: pl.BlockSpec(shape, lambda s: (0,) * len(shape), pipeline_mode=pl.Buffered(1))
     moving = lambda shape: pl.BlockSpec((1,) + shape, lambda s: (s,) + (0,) * len(shape))
     packed = (n_expert, slots * SLOT_ROWS, width)
-    out_part, back_part, gate_grad, d_up, d_down = call(
+    rows = n_expert * SLOT_ROWS
+    out_part, back_part, gate_grad, inner, grad_both = call(
         functools.partial(experts, n_expert, slots, tokens),
         "experts",
         [
             ((n_expert, tokens, width), BF16),
             ((n_expert, tokens, width), BF16),
             ((n_expert, SLOT_STRIDE, tokens), F32),
-            ((slots, width, double), BF16),
-            ((slots, hidden, width), BF16),
+            ((slots, rows, hidden), BF16),
+            ((slots, rows, double), BF16),
         ],
         (norm_all, og_all, meta_all, expert_gate_up, expert_down),
         [pltpu.VMEM(packed, BF16)] * 4
-        + [pltpu.VMEM((2, tokens, width), BF16)] * 2
+        + [pltpu.VMEM((2, ranks, tokens, shard), BF16)] * 2
         + [pltpu.SemaphoreType.DMA((2, 2))],
-        us=50,
+        us=40,
         grid=(slots,),
-        in_specs=[
-            pl.BlockSpec(memory_space=pl.ANY),
-            pl.BlockSpec(memory_space=pl.ANY),
-            fixed((n_expert, 2, used, tokens)),
-            moving((width, double)),
-            moving((hidden, width)),
-        ],
+        in_specs=[ANY, ANY, fixed((n_expert, 2, used, tokens)), moving((width, double)), moving((hidden, width))],
         out_specs=[
             fixed((n_expert, tokens, width)),
             fixed((n_expert, tokens, width)),
             fixed((n_expert, SLOT_STRIDE, tokens)),
-            moving((width, double)),
-            moving((hidden, width)),
+            moving((rows, hidden)),
+            moving((rows, double)),
         ],
     )
-    d_up = lax.psum_scatter(d_up, "dp", scatter_dimension=1, tiled=True).astype(F32)
-    d_down = lax.psum_scatter(d_down, "dp", scatter_dimension=2, tiled=True).astype(F32)
 
     def combine(*refs):
         take = taker(refs)
-        (terms, back_terms, gg), (out, back, gg_all) = take(3), take(3)
-        ex = Grid(*plane)
-        greet(ex.all())
+        (terms, back_terms, gg, mt, gb, og), (out, back, gg_all, mt_all, gb_all, ogd) = take(6), take(6)
+        mt_own = take()
+        dp, ex = Grid(*group), Grid(*plane)
+        mine = pl.ds(pl.multiple_of(ex.me * SLOT_STRIDE, SLOT_STRIDE), SLOT_STRIDE)
+        mt_own[...] = mt[:, :, mine, :]
+        mt_all[dp.me] = mt_own[...]
+        greet(dp.all() + ex.all())
 
         def finish(to):
             def store(total):
@@ -892,20 +1013,45 @@
 
             return store
 
-        run(
-            exchange(ex, gg, gg_all, take(2)),
-            reduce(ex, lambda i: back_terms.at[i], finish(back), take(4), take(4)),
-            reduce(ex, lambda i: terms.at[i], finish(out), take(4), take(4)),
-        )
-
-    mixture, back, gate_grads = call(
+        ggs = begin(exchange(ex, gg, gg_all, take(2)))
+        mts = begin(gather(dp, mt_own, mt_all, take(4)))
+        backs = begin(reduce(ex, lambda i: back_terms.at[i], finish(back), take(4), take(4)))
+        gbs = begin(gather(dp, gb, gb_all, take(4)))
+        arrived, end = pass_slices(dp, ogd, take(2))
+        for i in range(n_expert):
+            arrived(i, og.at[i])
+        outs = begin(reduce(ex, lambda i: terms.at[i], finish(out), take(4), take(4)))
+        run(ggs, mts)
+        run(backs)
+        run(gbs)
+        run(outs)
+        end(range(n_expert), og.at[0])
+
+    mixture, back, gate_grads, meta_group, both_all, og_slices = call(
         combine,
         "combine",
-        [((tokens, width), F32), ((tokens, width), F32), ((n_expert, SLOT_STRIDE, tokens), F32)],
-        (out_part, back_part, gate_grad),
-        exchange_sems(n_expert) + (line_sems(*plane[1:]) + sum_slots(*plane[1:], (tokens, width))) * 2,
+        [
+            ((tokens, width), F32),
+            ((tokens, width), F32),
+            ((n_expert, SLOT_STRIDE, tokens), F32),
+            ((ranks, n_expert, 2, SLOT_STRIDE, tokens), F32),
+            ((ranks, slots, rows, double), BF16),
+            ((ranks, n_expert, tokens, shard), BF16),
+        ],
+        (out_part, back_part, gate_grad, meta_all, grad_both, og_all),
+        [pltpu.VMEM((n_expert, 2, SLOT_STRIDE, tokens), F32)]
+        + exchange_sems(n_expert)
+        + line_sems(*group[1:])
+        + line_sems(*plane[1:])
+        + sum_slots(*plane[1:], (tokens, width))
+        + line_sems(*group[1:])
+        + [pltpu.SemaphoreType.DMA((n_expert, ranks))] * 2
+        + line_sems(*plane[1:])
+        + sum_slots(*plane[1:], (tokens, width)),
         cid=3,
         us=78,
+        in_specs=[VMEM] * 4 + [ANY] * 2,
+        out_specs=[VMEM] * 4 + [ANY] * 2,
     )
 
     output, grad_hidden, grad_branch, small = call(
@@ -917,7 +1063,7 @@
             ((tokens, width), BF16),
             ((ranks, used + 8, shard), F32),
         ],
-        (hidden_rows, norm_hidden, scale_two, probs, misc_all, router_all, out_grad, mixture, back, gate_grads),
+        (hidden_rows, norm_hidden, scale_two, probs, misc_all, router, out_grad, mixture, back, gate_grads),
         us=6,
     )
 
@@ -927,7 +1073,10 @@
         dp = Grid(*group)
         greet(dp.all())
         br_all[dp.me] = br[...]
-        run(gather(dp, br, br_all, take(4)), exchange(dp, sm, sm_all, take(2)))
+        brs = begin(gather(dp, br, br_all, take(4)))
+        sms = begin(exchange(dp, sm, sm_all, take(2)))
+        run(brs)
+        run(sms)
 
     branch_all, small_all = call(
         share_branch,
@@ -982,7 +1131,7 @@
             ((shard, ranks * heads.cols), BF16),
             ((sum_rows, shard), BF16),
         ],
-        (x_cols, scale_all.reshape(ranks * tokens, 128), misc, grads_all, weights, small_all),
+        (x_cols, scale_all.reshape(ranks * tokens, 128), gains, grads_all, weights, small_all),
         us=10,
     )
     grad_x = grad_x.reshape(ranks, tokens, shard)
@@ -991,49 +1140,87 @@
 
     def closing(*refs):
         take = taker(refs)
-        (gx, dw, sm), (gx_all, dw_all, sm_all) = take(3), take(3)
+        (gx, dw, sm, inr), (gx_all, dw_all, sm_all, inr_all) = take(4), take(4)
         dp, ex = Grid(*group), Grid(*plane)
         greet(dp.all() + ex.near())
-        run(
-            exchange(dp, gx, gx_all, take(2)),
-            reduce_gather(ex, lambda i: sm.at[i], sm_all, take(), take(8), take(4)),
-            reduce_gather(ex, lambda i: dw.at[i], dw_all, take(), take(8), take(4)),
-        )
-
-    grad_x, d_w, sums = call(
+        gxs = begin(exchange(dp, gx, gx_all, take(2)))
+        sms = begin(reduce_gather(ex, lambda i: sm.at[i], sm_all, take(), take(8), take(4)))
+        dws = begin(reduce_gather(ex, lambda i: dw.at[i], dw_all, take(), take(8), take(4)))
+        inrs = begin(gather(dp, inr, inr_all, take(4)))
+        run(sms, dws)
+        run(gxs)
+        run(inrs)
+
+    grad_x, d_w, sums, inner_all = call(
         closing,
         "closing",
-        [(grad_x.shape, F32), (d_w.shape, BF16), (sums.shape, BF16)],
-        (grad_x, d_w, sums),
+        [(grad_x.shape, F32), (d_w.shape, BF16), (sums.shape, BF16), ((ranks, slots, rows, hidden), BF16)],
+        (grad_x, d_w, sums, inner),
         exchange_sems(ranks)
         + [pltpu.VMEM(sums.shape[1:], BF16)]
         + line_sems(*plane[1:]) * 2
         + sum_slots(*plane[1:], sums.shape[1:])
         + [pltpu.VMEM(d_w.shape[1:], BF16)]
         + line_sems(*plane[1:]) * 2
-        + sum_slots(*plane[1:], d_w.shape[1:]),
+        + sum_slots(*plane[1:], d_w.shape[1:])
+        + line_sems(*group[1:]),
         cid=6,
         us=55,
-    )
-
-    (grad_inputs,) = call(
-        functools.partial(last_norm, ranks),
-        "last_norm",
-        [((tokens, width), F32)],
-        (grad_x, inputs, misc_all, grad_hidden),
-        us=4,
-    )
-
-    d_w = d_w.reshape(shard, ranks, heads.cols).astype(F32)
-    first, second = heads.q_cols, heads.q_cols + heads.kv_cols
-    d_q = d_w[:, :, :first].reshape(shard, -1)
-    d_k = d_w[:, :, first:second].reshape(shard, -1)
-    d_v = d_w[:, :, second : second + heads.kv_cols].reshape(shard, -1)
-    d_o = d_o.reshape(shard, width).astype(F32)
-    sums = sums.reshape(sum_rows, shard).astype(F32)
-    d_router = sums[:used].reshape(n_expert, SLOT_STRIDE, shard)[:, :slots].transpose(2, 1, 0)
-    d_router = d_router.reshape(shard, slots * n_expert)[:, : router_weight.shape[1]]
-    return (output, grad_inputs, sums[used + 1], d_q, d_k, d_v, d_o, sums[used], d_router, d_up, d_down)
+        in_specs=[VMEM] * 3 + [ANY],
+        out_specs=[VMEM] * 3 + [ANY],
+    )
+
+    gathered = lambda shape: pl.BlockSpec((ranks, 1) + shape, lambda s: (0, s) + (0,) * len(shape))
+    d_w = d_w.reshape(shard, ranks * heads.cols)
+    d_o = d_o.reshape(shard, width)
+    sums = sums.reshape(sum_rows, shard)
+    ins = (grad_x, inputs, misc_all, grad_hidden, d_w, d_o, sums)
+    outs = [
+        ((slots, shard, double), F32),
+        ((slots, hidden, shard), F32),
+        ((tokens, width), F32),
+        ((shard, QUERY_HEADS * HEAD_DIMENSION), F32),
+        ((shard, KEY_VALUE_HEADS * HEAD_DIMENSION), F32),
+        ((shard, KEY_VALUE_HEADS * HEAD_DIMENSION), F32),
+        ((shard, width), F32),
+        (router_weight.shape, F32),
+        ((1, shard), F32),
+        ((1, shard), F32),
+    ]
+    d_up, d_down, grad_inputs, d_q, d_k, d_v, d_o, d_router, gain_one, gain_two = call(
+        functools.partial(finish, ranks, n_expert, slots, heads, tokens),
+        "finish",
+        outs,
+        (norm_all, og_all, norm_slices, og_slices, meta_group, grad_both, both_all, inner, inner_all) + ins,
+        [pltpu.VMEM((ranks, n_expert, slots * SLOT_ROWS, shard), BF16)] * 2
+        + [pltpu.VMEM((2, tokens, shard), BF16)] * 2
+        + [pltpu.SemaphoreType.DMA((2, 2))],
+        us=20,
+        grid=(slots,),
+        in_specs=[ANY] * 4
+        + [
+            fixed(meta_group.shape),
+            moving((rows, double)),
+            gathered((rows, double)),
+            moving((rows, hidden)),
+            gathered((rows, hidden)),
+        ]
+        + [fixed(array.shape) for array in ins],
+        out_specs=[moving((shard, double)), moving((hidden, shard))] + [fixed(shape) for shape, _ in outs[2:]],
+    )
+    return (
+        output,
+        grad_inputs,
+        gain_one.reshape(shard),
+        d_q,
+        d_k,
+        d_v,
+        d_o,
+        gain_two.reshape(shard),
+        d_router,
+        d_up,
+        d_down,
+    )
 
 
 def solution(mesh):

time: 566 us -> 480 us (0.85)
  local copies, waits for them, and re-layouts: 62.2 us -> 7.73 us
  between operations: 14.2 us -> 0.73 us
  other arithmetic: 16.3 us -> 3.14 us
    unnamed x15 -> x3, local copies, waits for them, and re-layouts: 43.6 us -> 4.57 us
    convert_element_type x6 -> x1, other arithmetic: 14.2 us -> 0.59 us  [on_device(): gains = jnp.stack([norm1_gain, norm2_gain]).astype(F32)]
  transfers between devices with their start and end apart: 2 -> 0, of which waited for: 0 -> 0; matrix products, arithmetic and copies ran while one was open for 5% -> 0% of each run, Pallas kernels for 50% -> 0%
where the time goes in v2:
time: 480 us; the launch traced here: 479 us
  Pallas kernels  467 us (97%)
  local copies, waits for them, and re-layouts  7.73 us (2%)
    pallas_call x14, Pallas kernels, call(): pl.pallas_call(body, out_shape=[jax.ShapeDtypeStruct(shape, dtype) for sh...  467 us

profile of v2, /device:TPU:0, one launch (start us, length us, event | category | flops | bytes accessed | tf_op | source)
XLA Modules:
  0.0 479.0 jit_solution(16882027075633282975)
XLA Ops:
  0.6 0.7 stack.9
  1.3 0.7 stack.10
  2.0 0.6 maximum_convert_fusion.refs_5_.gain_ref
  2.6 1.4 copy.28.routes_ref
  4.0 1.5 copy.27.refs_4_
  5.5 49.4 %opening.1 = (bf16[4,128,1536]{2,1,0:T(8,128)(2,1)}, bf16[4,384,640]{2,1,0:T(8,128)(2,1)}, bf16[4,384,640]{2,1,0:T(8,128)(2,1)}, bf16[4,384,40]{2,1,0:T(8,128)(2...) custom-call(bf16[128,1536]{1,0:T(8,128)(2,1)} %x_ref.3, bf16[384,1536]{1,0:T(8,128)(2,1)} %refs_1_.1, ...), custom_call_target="tpu_custom_call" | custom-call | bytes 120000000 | tf_op jit(solution)/shard_map/opening/pallas_call | solution.py:387
  54.9 1.8 constant_dynamic-slice_fusion.x_ref
  56.7 10.6 %attention_forward.1 = (bf16[4,128,1536]{2,1,0:T(8,128)(2,1)}, bf16[4,128,640]{2,1,0:T(8,128)(2,1)}, bf16[4,128,384]{2,1,0:T(8,128)(2,1)}, f32[4,128,128]{2,1,0:T(8,128)}) custom-call(bf16[4,128,1536]{2,1,0:T(8,128)(2,1)} %get-tuple-element.68.x_ref, bf16[4,384,640]{2,1,0:T(8,128)(2,1)} %get-tuple-element.69.w_ref, bf16[384,1536]{1,0:T(8,128)(2,1)} %o_ref.3, ...), custom_call_target="tpu_custom_call" | custom-call | bytes 45000000 | tf_op jit(solution)/shard_map/attention_forward/pallas_call | solution.py:387
  67.3 16.0 %branch_sum.1.branch_ref = f32[128,1536]{1,0:T(8,128)} custom-call(bf16[4,128,1536]{2,1,0:T(8,128)(2,1)} %get-tuple-element.71.refs_0_), custom_call_target="tpu_custom_call" | custom-call | bytes 45000000 | tf_op jit(solution)/shard_map/branch_sum/pallas_call | solution.py:387
  83.3 3.3 route_forward.1
  86.6 57.4 %dispatch.1 = (bf16[8,4,128,384]{3,2,1,0:T(8,128)(2,1)}, f32[8,2,64,128]{3,2,1,0:T(8,128)}, bf16[4,8,128,384]{3,2,1,0:T(8,128)(2,1)}) custom-call(bf16[4,128,384]{2,1,0:T(8,128)(2,1)} %get-tuple-element.74.refs_0_.norm_ref, f32[2,64,128]{2,1,0:T(8,128)} %get-tuple-element.78.refs_1_), custom_call_target="tpu_custom_call" | custom-call | bytes 126000000 | tf_op jit(solution)/shard_map/dispatch/pallas_call | solution.py:387
  144.0 32.2 %experts.1 = (bf16[8,128,1536]{2,1,0:T(8,128)(2,1)}, bf16[8,128,1536]{2,1,0:T(8,128)(2,1)}, f32[8,8,128]{2,1,0:T(8,128)}, bf16[5,256,512]{2,1,0:T(8,128)(2,1)}, bf16[5,256,1024]{2,1,0:T(8,128)(2,1)}) custom-call(bf16[8,4,128,384]{3,2,1,0:T(8,128)(2,1)} %get-tuple-element.79.nh_ref, bf16[8,4,128,384]{3,2,1,0:T(8,128)(2,1)} %get-tuple-element.80.og_ref.refs_5_, ...), custom_call_target="tpu_custom_call" | custom-call | bytes 120000000 | tf_op jit(solution)/shard_map/experts/pallas_call | solution.py:387
  176.2 104.1 %combine.1 = (f32[128,1536]{1,0:T(8,128)}, f32[128,1536]{1,0:T(8,128)}, f32[8,8,128]{2,1,0:T(8,128)}, f32[4,8,2,8,128]{4,3,2,1,0:T(8,128)}, bf16[4,5,256,1024]{3...) custom-call(bf16[8,128,1536]{2,1,0:T(8,128)(2,1)} %get-tuple-element.82.refs_0_, ...), custom_call_target="tpu_custom_call" | custom-call | bytes 234000000 | tf_op jit(solution)/shard_map/combine/pallas_call | solution.py:387
  280.4 4.0 route_backward.1
  284.4 17.7 %share_branch.1 = (bf16[4,128,1536]{2,1,0:T(8,128)(2,1)}, f32[4,72,384]{2,1,0:T(8,128)}) custom-call(bf16[128,1536]{1,0:T(8,128)(2,1)} %get-tuple-element.96.refs_0_, f32[4,72,384]{2,1,0:T(8,128)} %get-tuple-element.97.refs_1_), custom_call_target="tpu_custom_call" | custom-call | bytes 45000000 | tf_op jit(solution)/shard_map/share_branch/pallas_call | solution.py:387
  302.1 12.0 %attention_backward.1 = (bf16[4,128,640]{2,1,0:T(8,128)(2,1)}, bf16[384,1536]{1,0:T(8,128)(2,1)}) custom-call(bf16[4,128,1536]{2,1,0:T(8,128)(2,1)} %get-tuple-element.98.branch_ref, bf16[4,128,384]{2,1,0:T(8,128)(2,1)} %get-tuple-element.99.att_ref, bf16[4,128,640]{2,1,0:T(8,128)(2,1)} %get-tuple-element.100.qkv_ref, bf16[384,1536]{1,0:T(8,128)(2,1)} %o_ref.3, ...), custom_call_target="tpu_custom_call" | custom-call | bytes 45000000 | tf_op jit(solution)/shard_map/attention_backward/pallas_call | solution.py:387
  314.1 53.9 %share_grads.1 = (bf16[4,4,128,640]{3,2,1,0:T(8,128)(2,1)}, bf16[8,48,1536]{2,1,0:T(8,128)(2,1)}) custom-call(bf16[4,128,640]{2,1,0:T(8,128)(2,1)} %get-tuple-element.101.refs_0_, bf16[8,48,1536]{2,1,0:T(8,128)(2,1)} %bitcast.13), custom_call_target="tpu_custom_call" | custom-call | bytes 90000000 | tf_op jit(solution)/shard_map/share_grads/pallas_call | solution.py:387
  368.0 7.0 %projection_backward.1 = (f32[512,384]{1,0:T(8,128)}, bf16[384,2560]{1,0:T(8,128)(2,1)}, bf16[128,384]{1,0:T(8,128)(2,1)}) custom-call(bf16[512,384]{1,0:T(8,128)(2,1)} %constant_dynamic-slice_fusion.x_ref, f32[512,128]{1,0:T(8,128)} %bitcast.15, f32[2,384]{1,0:T(2,128)} %maximum_convert_fusion.refs_5_.gain_ref, ...), custom_call_target="tpu_custom_call" | custom-call | bytes 30000000 | tf_op jit(solution)/shard_map/projection_backward/pallas_call | solution.py:387
  375.0 60.2 %closing.1 = (f32[4,128,384]{2,1,0:T(8,128)}, bf16[8,48,2560]{2,1,0:T(8,128)(2,1)}, bf16[8,16,384]{2,1,0:T(8,128)(2,1)}, bf16[4,5,256,512]{3,2,1,0:T(8,128)(2,1)}) custom-call(f32[4,128,384]{2,1,0:T(8,128)} %bitcast.14, bf16[8,48,2560]{2,1,0:T(8,128)(2,1)} %bitcast.11, bf16[8,16,384]{2,1,0:T(8,128)(2,1)} %bitcast.17, ...), custom_call_target="tpu_custom_call" | custom-call | bytes 165000000 | tf_op jit(solution)/shard_map/closing/pallas_call | solution.py:387
  435.1 39.6 %finish.1 = (f32[5,384,1024]{2,1,0:T(8,128)}, f32[5,512,384]{2,1,0:T(8,128)}, f32[128,1536]{1,0:T(8,128)}, f32[384,1536]{1,0:T(8,128)}, f32[384,512]{1,0:T(8,128...) custom-call(bf16[8,4,128,384]{3,2,1,0:T(8,128)(2,1)} %get-tuple-elem, ...), custom_call_target="tpu_custom_call" | custom-call | bytes 60000000 | tf_op jit(solution)/shard_map/finish/pallas_call | solution.py:387
  474.8 1.3 reduce
  476.1 1.3 reduce.1
  477.3 1.7 copy.29

commit v3 on v2

--- a/solution.py
+++ b/solution.py
@@ -93,6 +93,14 @@
     )
 
 
+class Part:
+    def __init__(self, ref, *rest):
+        self.ref, self.rest, self.at = ref, rest, self
+
+    def __getitem__(self, i):
+        return self.ref.at[(i,) + self.rest]
+
+
 def begin(step):
     next(step)
     return step
@@ -197,8 +205,8 @@
 
 def sum_slots(A, B, block, dtype=BF16):
     return [
-        pltpu.VMEM((2, A) + block, dtype),
-        pltpu.VMEM((2, A) + block, dtype),
+        pltpu.VMEM((2, A - 1) + block, dtype),
+        pltpu.VMEM((2, A - 1) + block, dtype),
         pltpu.VMEM((2, A, B - 1) + block, dtype),
         pltpu.VMEM((2, A, B - 2) + block if B > 2 else (8, 128), dtype),
     ]
@@ -277,14 +285,14 @@
                 def _():
                     if k < A - 1:
                         remote(land_a.at[way, k], land_a.at[way, k], send_a.at[way, k], recv_a.at[way, k], here).wait_recv()
-                        out_a[way, k] = (near() + land_a[way, k].astype(F32)).astype(out_a.dtype)
+                        out_a[way, k - 1] = (near() + land_a[way, k].astype(F32)).astype(out_a.dtype)
 
                 @pl.when(first("a", way))
                 def _():
-                    out_a[way, k] = near().astype(out_a.dtype)
+                    out_a[way, k - 1] = near().astype(out_a.dtype)
 
                 remote(
-                    out_a.at[way, k], land_a.at[way, k - 1], send_a.at[way, k], recv_a.at[way, k - 1], g.next("a", way)[1]
+                    out_a.at[way, k - 1], land_a.at[way, k - 1], send_a.at[way, k], recv_a.at[way, k - 1], g.next("a", way)[1]
                 ).start()
             else:
                 for w in (0, 1):
@@ -317,7 +325,7 @@
                         remote(part(g.me), land_b.at[w, a, j - 1], send_b.at[w, a, j], recv_b.at[w, a, j - 1], here).wait_send()
 
             if k > 0:
-                remote(out_a.at[way, k], land_a.at[way, k - 1], send_a.at[way, k], recv_a.at[way, k - 1], here).wait_send()
+                remote(out_a.at[way, k - 1], land_a.at[way, k - 1], send_a.at[way, k], recv_a.at[way, k - 1], here).wait_send()
 
 
 def reduce_gather(g, part, out, kept, sems, slots):
@@ -513,8 +521,8 @@
     lax.fori_loop(0, ranks, one, 0)
 
 
-def column_experts(n_expert, slots):
-    column = lax.broadcasted_iota(jnp.int32, (1, 128), 1)
+def column_experts(n_expert, slots, axis):
+    column = lax.broadcasted_iota(jnp.int32, (1, 128) if axis else (128, 1), axis)
     owner, slot = column // SLOT_STRIDE, column % SLOT_STRIDE
     expert = slot * n_expert + owner
     real = (owner < n_expert) & (slot < slots) & (expert < EXPERT_COUNT)
@@ -522,22 +530,23 @@
 
 
 def column_picks(n_expert, slots):
-    _, expert = column_experts(n_expert, slots)
+    _, expert = column_experts(n_expert, slots, 1)
     return jnp.where(lax.broadcasted_iota(jnp.int32, (EXPERT_COUNT, 128), 0) == expert, 1.0, 0.0)
 
 
-def route_tables(expert, routes, blocks_ref):
-    tokens = routes.shape[0]
-    named = jnp.zeros((tokens, 128), F32)
-    for k in range(routes.shape[1]):
-        named = named + jnp.where(routes[:, k : k + 1] == expert, 1.0, 0.0)
-    limit = jnp.zeros((1, 128), jnp.int32)
+def route_tables(n_expert, slots, routes, blocks_ref):
+    tokens = routes.shape[1]
+    _, expert = column_experts(n_expert, slots, 0)
+    named = jnp.zeros((128, tokens), F32)
+    for k in range(routes.shape[0]):
+        named = named + jnp.where(routes[k : k + 1, :] == expert, 1.0, 0.0)
+    limit = jnp.zeros((128, 1), jnp.int32)
     for e in range(EXPERT_COUNT):
         limit = jnp.where(expert == e, blocks_ref[e] * BLK, limit)
     rows = lax.broadcasted_iota(jnp.int32, (tokens, tokens), 0)
     cols = lax.broadcasted_iota(jnp.int32, (tokens, tokens), 1)
-    earlier = jnp.where(cols < rows, 1.0, 0.0).astype(BF16)
-    rank = dot(earlier, named.astype(BF16))
+    earlier = jnp.where(rows < cols, 1.0, 0.0).astype(BF16)
+    rank = dot(named.astype(BF16), earlier)
     kept = (named > 0.0) & (rank < limit.astype(F32))
     return kept, jnp.where(kept, rank, -1.0)
 
@@ -551,19 +560,20 @@
     scale = norm_scale(hidden)
     scale_ref[...] = jnp.broadcast_to(scale, scale_ref.shape)
     norm = (hidden * scale * gain).astype(BF16)
+    picks = column_picks(n_expert, slots).astype(BF16)
     for i in range(ranks):
-        norm_ref[i] = norm[:, i * shard : (i + 1) * shard]
-    real, expert = column_experts(n_expert, slots)
-    kept, place = route_tables(expert, routes_ref[...], blocks_ref)
-    router = router_ref[...].reshape(width, -1)
-    table_ref[...] = dot(router, column_picks(n_expert, slots).astype(BF16)).astype(BF16)
+        here = slice(i * shard, (i + 1) * shard)
+        norm_ref[i] = norm[:, here]
+        table_ref[here, :] = dot(router_ref[i], picks, ((0,), (0,))).astype(BF16)
+    kept, place = route_tables(n_expert, slots, routes_ref[...], blocks_ref)
+    real, _ = column_experts(n_expert, slots, 1)
     logits = jnp.where(real, dot(norm, table_ref[...]), MASKED_SCORE)
     weight = jnp.exp(logits - jnp.max(logits, axis=-1, keepdims=True))
     probs = weight / jnp.sum(weight, axis=-1, keepdims=True)
     probs_ref[...] = probs
     used = n_expert * SLOT_STRIDE
-    meta_ref[0] = place.T[:used]
-    meta_ref[1] = jnp.where(kept, probs, 0.0).T[:used]
+    meta_ref[0] = place[:used]
+    meta_ref[1] = jnp.where(kept, probs.T, 0.0)[:used]
 
 
 def row_picks(slots, place):
@@ -658,11 +668,10 @@
         lax.fori_loop(0, n_expert, one, 0)
 
 
-def route_backward(ranks, n_expert, shard, hidden_ref, norm_ref, scale_ref, probs_ref, misc_ref, router_ref, og_ref, mixture_ref, back_ref, gate_grad_ref, out_ref, grad_hidden_ref, branch_ref, small_ref):
+def route_backward(ranks, n_expert, shard, hidden_ref, norm_ref, scale_ref, probs_ref, misc_ref, router_ref, og_ref, back_ref, gate_grad_ref, grad_hidden_ref, branch_ref, small_ref):
     tokens, width = hidden_ref.shape
     gain = gain_row(misc_ref, ranks, 1)
     hidden = hidden_ref[...]
-    out_ref[...] = (hidden + RESIDUAL_SCALE * mixture_ref[...]).astype(BF16)
     used = n_expert * SLOT_STRIDE
     spread = gate_grad_ref[...].reshape(used, tokens)
     if used < 128:
@@ -688,10 +697,15 @@
         small_ref[i, used:, :] = jnp.broadcast_to(grad_gain[:, here], (8, shard))
 
 
+def store_blocks(ref, cols, values):
+    count, rows = ref.shape[0], ref.shape[1]
+    for i in range(count):
+        ref[i, :, cols] = values[i * rows : (i + 1) * rows]
+
+
 def attention_backward(ranks, heads, length, branch_ref, att_ref, qkv_ref, o_ref, misc_ref, cos_ref, sin_ref, grad_ref, d_o_ref):
-    d_o_ref[...] = dot(
-        att_ref[...].reshape(ranks * length, heads.q_cols), branch_ref[...].reshape(ranks * length, -1), ((0,), (0,))
-    ).astype(BF16)
+    d_o = dot(att_ref[...].reshape(ranks * length, heads.q_cols), branch_ref[...].reshape(ranks * length, -1), ((0,), (0,)))
+    store_blocks(d_o_ref, slice(None), d_o.astype(BF16))
 
     def one(b, carry):
         grad_att = dot(branch_ref[b], o_ref[...], ((1,), (1,))).astype(BF16)
@@ -727,8 +741,8 @@
         grads = grad_ref[i].reshape(-1, heads.cols)
         term = dot(grads, w_ref[i], ((1,), (1,)))
         total = term if total is None else total + term
-        d_w_ref[:, i * heads.cols : (i + 1) * heads.cols] = dot(norm_input, grads, ((0,), (0,))).astype(BF16)
-    grad_x_ref[...] = total
+        store_blocks(d_w_ref, slice(i * heads.cols, (i + 1) * heads.cols), dot(norm_input, grads, ((0,), (0,))).astype(BF16))
+    grad_x_ref[...] = total.reshape(grad_x_ref.shape)
     small = small_ref[0]
     for i in range(1, ranks):
         small = small + small_ref[i]
@@ -740,44 +754,40 @@
     sums_ref[used : used + 8, :] = jnp.where(second == 0, small[used:], jnp.where(second == 1, gain_grad, 0.0)).astype(BF16)
 
 
-def finish(ranks, n_expert, slots, heads, tokens, nh_ref, og_ref, xd_ref, ogd_ref, meta_ref, own_both_ref, both_ref, own_inner_ref, inner_ref, grad_ref, x_ref, misc_ref, grad_hidden_ref, d_w_ref, d_o_ref, sums_ref, d_up_ref, d_down_ref, grad_inputs_ref, q_ref, k_ref, v_ref, o_ref, router_ref, gain_one_ref, gain_two_ref, x_sc, og_sc, x_in, og_in, sems):
+def finish(ranks, n_expert, slots, early, heads, tokens, nh_ref, og_ref, xd_ref, ogd_ref, meta_ref, own_both_ref, both_ref, late_both_ref, own_inner_ref, inner_ref, grad_ref, x_ref, misc_ref, grad_hidden_ref, hidden_ref, mixture_ref, d_w_ref, d_o_ref, sums_ref, d_up_ref, d_down_ref, output_ref, grad_inputs_ref, q_ref, k_ref, v_ref, o_ref, router_ref, gain_one_ref, gain_two_ref, x_sc, og_sc, x_in, og_in, sems):
     step = pl.program_id(0)
     me = lax.axis_index("dp")
     rows = n_expert * SLOT_ROWS
-    shard = x_in.shape[2]
+    shard = x_in.shape[3]
 
     @pl.when(step == 0)
     def _():
-        def fetch(j, q, do):
-            at, slot = (me + j) % ranks, q % 2
-
-            def both(x, og):
-                do(pltpu.make_async_copy(x, x_in.at[slot], sems.at[0, slot]))
-                do(pltpu.make_async_copy(og, og_in.at[slot], sems.at[1, slot]))
-
-            if j == 0:
-                both(nh_ref.at[q, me], og_ref.at[q, me])
-            else:
-                both(xd_ref.at[at, q], ogd_ref.at[at, q])
-
+        def fetch(j, do):
+            at, slot = (me + j) % ranks, j % 2
+            x, og = (nh_ref.at[:, me], og_ref.at[:, me]) if j == 0 else (xd_ref.at[at], ogd_ref.at[at])
+            do(pltpu.make_async_copy(x, x_in.at[slot], sems.at[0, slot]))
+            do(pltpu.make_async_copy(og, og_in.at[slot], sems.at[1, slot]))
+
+        fetch(0, lambda copy: copy.start())
         for j in range(ranks):
-            fetch(j, 0, lambda copy: copy.start())
+            if j + 1 < ranks:
+                fetch(j + 1, lambda copy: copy.start())
+            fetch(j, lambda copy: copy.wait())
 
             def one(q, carry):
-                @pl.when(q + 1 < n_expert)
-                def _():
-                    fetch(j, q + 1, lambda copy: copy.start())
-
-                fetch(j, q, lambda copy: copy.wait())
                 at = (me + j) % ranks
                 pick = row_picks(slots, meta_ref[at, q, 0])
                 share = jnp.sum(pick * row_shares(slots, meta_ref[at, q, 1]), axis=1, keepdims=True)
                 pick = pick.astype(BF16)
-                x_sc[j, q] = dot(pick, x_in[q % 2]).astype(BF16)
-                og_sc[j, q] = (share * (RESIDUAL_SCALE * dot(pick, og_in[q % 2]))).astype(BF16)
+                x_sc[j, q] = dot(pick, x_in[j % 2, q]).astype(BF16)
+                og_sc[j, q] = (share * (RESIDUAL_SCALE * dot(pick, og_in[j % 2, q]))).astype(BF16)
                 return carry
 
             lax.fori_loop(0, n_expert, one, 0)
+
+    @pl.when(step == slots - 1)
+    def _():
+        output_ref[...] = (hidden_ref[...] + RESIDUAL_SCALE * mixture_ref[...]).astype(BF16)
         gain = gain_row(misc_ref, ranks, 0)
         grad = jnp.concatenate([grad_ref[i] for i in range(ranks)], axis=1)
         x = x_ref[...].astype(F32)
@@ -792,26 +802,33 @@
             v_ref[:, here] = d_w_ref[:, start + second : start + second + heads.kv_cols].astype(F32)
         o_ref[...] = d_o_ref[...].astype(F32)
         used = n_expert * SLOT_STRIDE
-        picks = column_picks(n_expert, slots).astype(BF16)
-        router_ref[...] = lax.dot_general(
-            sums_ref[:128], picks, (((0,), (1,)), ((), ())), preferred_element_type=F32
-        )
+        router_ref[...] = dot(column_picks(n_expert, slots).astype(BF16), sums_ref[:128])
         ends = sums_ref[used : used + 16, :].astype(F32)
         gain_two_ref[...] = ends[0:1]
         gain_one_ref[...] = ends[1:2]
 
     place_of = pl.ds(pl.multiple_of(step * SLOT_ROWS, SLOT_ROWS), SLOT_ROWS)
     over = ((0,), (0,))
-    d_up = d_down = None
-    for j in range(ranks):
-        at = (me + j) % ranks
-        x = x_sc[j, :, place_of, :].reshape(rows, shard)
-        og = og_sc[j, :, place_of, :].reshape(rows, shard)
-        up = dot(x, own_both_ref[0] if j == 0 else both_ref[at, 0], over)
-        down = dot(own_inner_ref[0] if j == 0 else inner_ref[at, 0], og, over)
-        d_up, d_down = (up, down) if j == 0 else (d_up + up, d_down + down)
-    d_up_ref[0] = d_up
-    d_down_ref[0] = d_down
+
+    def form(their_both):
+        d_up = d_down = None
+        for j in range(ranks):
+            at = (me + j) % ranks
+            x = x_sc[j, :, place_of, :].reshape(rows, shard)
+            og = og_sc[j, :, place_of, :].reshape(rows, shard)
+            up = dot(x, own_both_ref[0] if j == 0 else their_both[at, 0], over)
+            down = dot(own_inner_ref[0] if j == 0 else inner_ref[at, 0], og, over)
+            d_up, d_down = (up, down) if j == 0 else (d_up + up, d_down + down)
+        d_up_ref[0] = d_up
+        d_down_ref[0] = d_down
+
+    @pl.when(step < early)
+    def _():
+        form(both_ref)
+
+    @pl.when(step >= early)
+    def _():
+        form(late_both_ref)
 
 
 def on_device(
@@ -878,11 +895,11 @@
             ((ranks, tokens, width), BF16),
             ((ranks, shard, heads.cols), BF16),
             ((ranks, shard, heads.cols), BF16),
-            ((ranks, shard, router_weight.shape[1]), BF16),
+            ((ranks, router_weight.shape[1], shard), BF16),
             ((ranks, 16, shard), F32),
             ((n_expert, ranks, tokens, shard), BF16),
         ],
-        (inputs, q_weight, k_weight, value_matrix, router_weight, gains, segment_ids, out_grad),
+        (inputs, q_weight, k_weight, value_matrix, router_weight.T, gains, segment_ids, out_grad),
         [pltpu.VMEM((16, shard), F32), pltpu.VMEM((ranks, tokens, shard), BF16)]
         + line_sems(*group[1:]) * 3
         + line_sems(*plane[1:])
@@ -936,7 +953,7 @@
             ((2, used, tokens), F32),
             ((width, 128), BF16),
         ],
-        (inputs, branch, misc_all, router_all, routes, expert_blocks),
+        (inputs, branch, misc_all, router_all, routes.T, expert_blocks),
         us=5,
         in_specs=[VMEM] * 5 + [pl.BlockSpec(memory_space=pltpu.SMEM)],
     )
@@ -997,9 +1014,11 @@
         ],
     )
 
+    early = slots * 3 // 5
+
     def combine(*refs):
         take = taker(refs)
-        (terms, back_terms, gg, mt, gb, og), (out, back, gg_all, mt_all, gb_all, ogd) = take(6), take(6)
+        (back_terms, gg, mt, gb), (back, gg_all, mt_all, gb_all) = take(4), take(4)
         mt_own = take()
         dp, ex = Grid(*group), Grid(*plane)
         mine = pl.ds(pl.multiple_of(ex.me * SLOT_STRIDE, SLOT_STRIDE), SLOT_STRIDE)
@@ -1007,193 +1026,192 @@
         mt_all[dp.me] = mt_own[...]
         greet(dp.all() + ex.all())
 
-        def finish(to):
-            def store(total):
-                to[...] = total
-
-            return store
+        def store(total):
+            back[...] = total
 
         ggs = begin(exchange(ex, gg, gg_all, take(2)))
         mts = begin(gather(dp, mt_own, mt_all, take(4)))
-        backs = begin(reduce(ex, lambda i: back_terms.at[i], finish(back), take(4), take(4)))
-        gbs = begin(gather(dp, gb, gb_all, take(4)))
-        arrived, end = pass_slices(dp, ogd, take(2))
-        for i in range(n_expert):
-            arrived(i, og.at[i])
-        outs = begin(reduce(ex, lambda i: terms.at[i], finish(out), take(4), take(4)))
+        backs = begin(reduce(ex, lambda i: back_terms.at[i], store, take(4), take(4)))
+        gbs = begin(gather(dp, gb.at[pl.ds(0, early)], gb_all, take(4)))
         run(ggs, mts)
         run(backs)
         run(gbs)
-        run(outs)
-        end(range(n_expert), og.at[0])
-
-    mixture, back, gate_grads, meta_group, both_all, og_slices = call(
+
+    back, gate_grads, meta_group, both_all = call(
         combine,
         "combine",
         [
             ((tokens, width), F32),
-            ((tokens, width), F32),
             ((n_expert, SLOT_STRIDE, tokens), F32),
             ((ranks, n_expert, 2, SLOT_STRIDE, tokens), F32),
-            ((ranks, slots, rows, double), BF16),
-            ((ranks, n_expert, tokens, shard), BF16),
+            ((ranks, early, rows, double), BF16),
         ],
-        (out_part, back_part, gate_grad, meta_all, grad_both, og_all),
+        (back_part, gate_grad, meta_all, grad_both),
         [pltpu.VMEM((n_expert, 2, SLOT_STRIDE, tokens), F32)]
         + exchange_sems(n_expert)
         + line_sems(*group[1:])
         + line_sems(*plane[1:])
         + sum_slots(*plane[1:], (tokens, width))
-        + line_sems(*group[1:])
-        + [pltpu.SemaphoreType.DMA((n_expert, ranks))] * 2
-        + line_sems(*plane[1:])
-        + sum_slots(*plane[1:], (tokens, width)),
+        + line_sems(*group[1:]),
         cid=3,
-        us=78,
-        in_specs=[VMEM] * 4 + [ANY] * 2,
-        out_specs=[VMEM] * 4 + [ANY] * 2,
-    )
-
-    output, grad_hidden, grad_branch, small = call(
+        us=42,
+        in_specs=[VMEM] * 3 + [ANY],
+        out_specs=[VMEM] * 3 + [ANY],
+    )
+
+    grad_hidden, grad_branch, small = call(
         functools.partial(route_backward, ranks, n_expert, shard),
         "route_backward",
         [
-            ((tokens, width), BF16),
             ((tokens, width), F32),
             ((tokens, width), BF16),
             ((ranks, used + 8, shard), F32),
         ],
-        (hidden_rows, norm_hidden, scale_two, probs, misc_all, router, out_grad, mixture, back, gate_grads),
+        (hidden_rows, norm_hidden, scale_two, probs, misc_all, router, out_grad, back, gate_grads),
         us=6,
     )
 
-    def share_branch(*refs):
+    sum_rows = 16 * n_expert
+    part_rows = shard // n_expert
+    o_block, w_block, s_block = (part_rows, width), (part_rows, ranks * heads.cols), (16, shard)
+
+    def backward(*refs):
         take = taker(refs)
-        (br, sm), (br_all, sm_all) = take(2), take(2)
-        dp = Grid(*group)
-        greet(dp.all())
+        br, sm, at, qkv, wo, ms, cs, sn, xa, sc, gn, w, terms, og, gb, inr = take(16)
+        mix, gx_all, do_all, dw_all, su_all, ogd, gb_all, inr_all = take(8)
+        br_all, sm_all, gr, gr_all, do, dw, su, gx, xc = take(9)
+        dp, ex = Grid(*group), Grid(*plane)
         br_all[dp.me] = br[...]
+        greet(dp.all() + ex.near())
+
+        def store(total):
+            mix[...] = total
+
         brs = begin(gather(dp, br, br_all, take(4)))
         sms = begin(exchange(dp, sm, sm_all, take(2)))
+        outs = begin(reduce(ex, lambda i: terms.at[i], store, take(4), take(4)))
         run(brs)
+        arrived, end = pass_slices(dp, ogd, take(2))
+        for i in range(n_expert // 3):
+            arrived(i, og.at[i])
+        for i in range(ranks):
+
+            @pl.when(dp.me == i)
+            def _():
+                for b in range(ranks):
+                    xc[b * tokens : (b + 1) * tokens, :] = xa[b, :, i * shard : (i + 1) * shard]
+
+        attention_backward(ranks, heads, tokens, br_all, at, qkv, wo, ms, cs, sn, gr, do)
+        gr_all[dp.me] = gr[...]
+        grs = begin(gather(dp, gr, gr_all, take(4)))
+        dos = begin(reduce_gather(ex, lambda i: do.at[i], do_all, take(), take(8), take(4)))
         run(sms)
-
-    branch_all, small_all = call(
-        share_branch,
-        "share_branch",
-        [((ranks, tokens, width), BF16), ((ranks, used + 8, shard), F32)],
-        (grad_branch, small),
-        line_sems(*group[1:]) + exchange_sems(ranks),
-        cid=4,
-        us=15,
-    )
-
-    grads, d_o = call(
-        functools.partial(attention_backward, ranks, heads, tokens),
-        "attention_backward",
-        [((ranks, tokens, heads.cols), BF16), ((shard, width), BF16)],
-        (branch_all, att, qkv, o_weight, misc_all, cosine, sine),
-        us=15,
-    )
-    d_o = d_o.reshape(n_expert, shard // n_expert, width)
-
-    def share_grads(*refs):
-        take = taker(refs)
-        (gr, do), (gr_all, do_all) = take(2), take(2)
-        dp, ex = Grid(*group), Grid(*plane)
-        greet(dp.near() + ex.near())
-        gr_all[dp.me] = gr[...]
-        run(
-            gather(dp, gr, gr_all, take(4)),
-            reduce_gather(ex, lambda i: do.at[i], do_all, take(), take(8), take(4)),
-        )
-
-    grads_all, d_o = call(
-        share_grads,
-        "share_grads",
-        [((ranks, ranks, tokens, heads.cols), BF16), (d_o.shape, BF16)],
-        (grads, d_o),
-        line_sems(*group[1:])
-        + [pltpu.VMEM(d_o.shape[1:], BF16)]
-        + line_sems(*plane[1:]) * 2
-        + sum_slots(*plane[1:], d_o.shape[1:]),
-        cid=5,
-        us=30,
-    )
-
-    x_cols = lax.dynamic_slice_in_dim(x_all.reshape(ranks * tokens, width), lax.axis_index("dp") * shard, shard, axis=1)
-    sum_rows = 16 * n_expert
-    grad_x, d_w, sums = call(
-        functools.partial(projection_backward, ranks, heads, shard),
-        "projection_backward",
-        [
-            ((ranks * tokens, shard), F32),
-            ((shard, ranks * heads.cols), BF16),
-            ((sum_rows, shard), BF16),
-        ],
-        (x_cols, scale_all.reshape(ranks * tokens, 128), gains, grads_all, weights, small_all),
-        us=10,
-    )
-    grad_x = grad_x.reshape(ranks, tokens, shard)
-    d_w = d_w.reshape(n_expert, shard // n_expert, ranks * heads.cols)
-    sums = sums.reshape(n_expert, 16, shard)
-
-    def closing(*refs):
-        take = taker(refs)
-        (gx, dw, sm, inr), (gx_all, dw_all, sm_all, inr_all) = take(4), take(4)
-        dp, ex = Grid(*group), Grid(*plane)
-        greet(dp.all() + ex.near())
+        run(outs)
+        run(grs)
+        for i in range(n_expert // 3, n_expert):
+            arrived(i, og.at[i])
+        inrs = begin(gather(dp, inr, inr_all, take(4)))
+        gbs = begin(gather(dp, gb.at[pl.ds(early, slots - early)], gb_all, take(4)))
+        projection_backward(ranks, heads, shard, xc, sc, gn, gr_all, w, sm_all, gx, dw, su)
         gxs = begin(exchange(dp, gx, gx_all, take(2)))
-        sms = begin(reduce_gather(ex, lambda i: sm.at[i], sm_all, take(), take(8), take(4)))
+        sus = begin(reduce_gather(ex, lambda i: su.at[pl.ds(pl.multiple_of(i * 16, 16), 16)], su_all, take(), take(8), take(4)))
         dws = begin(reduce_gather(ex, lambda i: dw.at[i], dw_all, take(), take(8), take(4)))
-        inrs = begin(gather(dp, inr, inr_all, take(4)))
-        run(sms, dws)
+        run(dos)
+        run(sus)
+        run(dws)
         run(gxs)
         run(inrs)
-
-    grad_x, d_w, sums, inner_all = call(
-        closing,
-        "closing",
-        [(grad_x.shape, F32), (d_w.shape, BF16), (sums.shape, BF16), ((ranks, slots, rows, hidden), BF16)],
-        (grad_x, d_w, sums, inner),
-        exchange_sems(ranks)
-        + [pltpu.VMEM(sums.shape[1:], BF16)]
-        + line_sems(*plane[1:]) * 2
-        + sum_slots(*plane[1:], sums.shape[1:])
-        + [pltpu.VMEM(d_w.shape[1:], BF16)]
-        + line_sems(*plane[1:]) * 2
-        + sum_slots(*plane[1:], d_w.shape[1:])
-        + line_sems(*group[1:]),
-        cid=6,
-        us=55,
-        in_specs=[VMEM] * 3 + [ANY],
-        out_specs=[VMEM] * 3 + [ANY],
-    )
-
-    gathered = lambda shape: pl.BlockSpec((ranks, 1) + shape, lambda s: (0, s) + (0,) * len(shape))
+        run(gbs)
+        end(range(n_expert), og.at[0])
+
+    summed = lambda block: [pltpu.VMEM(block, BF16)] + line_sems(*plane[1:]) * 2 + sum_slots(*plane[1:], block)
+    mixture, grad_x, d_o, d_w, sums, og_slices, both_late, inner_all = call(
+        backward,
+        "backward",
+        [
+            ((tokens, width), F32),
+            ((ranks, tokens, shard), F32),
+            ((n_expert,) + o_block, BF16),
+            ((n_expert,) + w_block, BF16),
+            ((n_expert,) + s_block, BF16),
+            ((ranks, n_expert, tokens, shard), BF16),
+            ((ranks, slots - early, rows, double), BF16),
+            ((ranks, slots, rows, hidden), BF16),
+        ],
+        (
+            grad_branch,
+            small,
+            att,
+            qkv,
+            o_weight,
+            misc_all,
+            cosine,
+            sine,
+            x_all,
+            scale_all.reshape(ranks * tokens, 128),
+            gains,
+            weights,
+            out_part,
+            og_all,
+            grad_both,
+            inner,
+        ),
+        [
+            pltpu.VMEM((ranks, tokens, width), BF16),
+            pltpu.VMEM((ranks, used + 8, shard), F32),
+            pltpu.VMEM((ranks, tokens, heads.cols), BF16),
+            pltpu.VMEM((ranks, ranks, tokens, heads.cols), BF16),
+            pltpu.VMEM((n_expert,) + o_block, BF16),
+            pltpu.VMEM((n_expert,) + w_block, BF16),
+            pltpu.VMEM((sum_rows, shard), BF16),
+            pltpu.VMEM((ranks, tokens, shard), F32),
+            pltpu.VMEM((ranks * tokens, shard), BF16),
+        ]
+        + line_sems(*group[1:])
+        + exchange_sems(ranks)
+        + line_sems(*plane[1:])
+        + sum_slots(*plane[1:], (tokens, width))
+        + [pltpu.SemaphoreType.DMA((n_expert, ranks))] * 2
+        + line_sems(*group[1:])
+        + summed(o_block)
+        + line_sems(*group[1:]) * 2
+        + exchange_sems(ranks)
+        + summed(s_block)
+        + summed(w_block),
+        cid=4,
+        us=130,
+        in_specs=[VMEM] * 13 + [ANY] * 3,
+        out_specs=[VMEM] * 5 + [ANY] * 3,
+    )
+
+    held = pl.Buffered(2 if ranks * rows <= 1024 else 1)
+    gathered = lambda shape, at: pl.BlockSpec(
+        (ranks, 1) + shape, lambda s: (0, at(s)) + (0,) * len(shape), pipeline_mode=held
+    )
     d_w = d_w.reshape(shard, ranks * heads.cols)
     d_o = d_o.reshape(shard, width)
     sums = sums.reshape(sum_rows, shard)
-    ins = (grad_x, inputs, misc_all, grad_hidden, d_w, d_o, sums)
+    ins = (grad_x, inputs, misc_all, grad_hidden, hidden_rows, mixture, d_w, d_o, sums)
     outs = [
         ((slots, shard, double), F32),
         ((slots, hidden, shard), F32),
+        ((tokens, width), BF16),
         ((tokens, width), F32),
         ((shard, QUERY_HEADS * HEAD_DIMENSION), F32),
         ((shard, KEY_VALUE_HEADS * HEAD_DIMENSION), F32),
         ((shard, KEY_VALUE_HEADS * HEAD_DIMENSION), F32),
         ((shard, width), F32),
-        (router_weight.shape, F32),
+        ((router_weight.shape[1], shard), F32),
         ((1, shard), F32),
         ((1, shard), F32),
     ]
-    d_up, d_down, grad_inputs, d_q, d_k, d_v, d_o, d_router, gain_one, gain_two = call(
-        functools.partial(finish, ranks, n_expert, slots, heads, tokens),
+    d_up, d_down, output, grad_inputs, d_q, d_k, d_v, d_o, d_router, gain_one, gain_two = call(
+        functools.partial(finish, ranks, n_expert, slots, early, heads, tokens),
         "finish",
         outs,
-        (norm_all, og_all, norm_slices, og_slices, meta_group, grad_both, both_all, inner, inner_all) + ins,
+        (norm_all, og_all, norm_slices, og_slices, meta_group, grad_both, both_all, both_late, inner, inner_all) + ins,
         [pltpu.VMEM((ranks, n_expert, slots * SLOT_ROWS, shard), BF16)] * 2
-        + [pltpu.VMEM((2, tokens, shard), BF16)] * 2
+        + [pltpu.VMEM((2, n_expert, tokens, shard), BF16)] * 2
         + [pltpu.SemaphoreType.DMA((2, 2))],
         us=20,
         grid=(slots,),
@@ -1201,9 +1219,10 @@
         + [
             fixed(meta_group.shape),
             moving((rows, double)),
-            gathered((rows, double)),
+            gathered((rows, double), lambda s: jnp.minimum(s, early - 1)),
+            gathered((rows, double), lambda s: jnp.maximum(s - early, 0)),
             moving((rows, hidden)),
-            gathered((rows, hidden)),
+            gathered((rows, hidden), lambda s: s),
         ]
         + [fixed(array.shape) for array in ins],
         out_specs=[moving((shard, double)), moving((hidden, shard))] + [fixed(shape) for shape, _ in outs[2:]],
@@ -1217,7 +1236,7 @@
         d_v,
         d_o,
         gain_two.reshape(shard),
-        d_router,
+        d_router.T,
         d_up,
         d_down,
     )

time: 480 us -> 429 us (0.89)
  Pallas kernels: 467 us -> 423 us
  local copies, waits for them, and re-layouts: 7.73 us -> 1.36 us
    pallas_call x14 -> x10, Pallas kernels: 467 us -> 423 us  [call(): pl.pallas_call(body, out_shape=[jax.ShapeDtypeStruct(shape, dtype) for sh...]
where the time goes in v3:
time: 429 us
  Pallas kernels  423 us (99%)
    pallas_call x10, Pallas kernels, call(): pl.pallas_call(body, out_shape=[jax.ShapeDtypeStruct(shape, dtype) for sh...  423 us

profile of v3, /device:TPU:0, one launch (start us, length us, event | category | flops | bytes accessed | tf_op | source)
XLA Modules:
  0.0 428.5 jit_solution(10495199306958596874)
XLA Ops:
  0.6 0.7 stack.9
  1.3 0.7 stack.10
  2.0 0.6 maximum_convert_fusion.refs_5_.refs_10_
  2.6 47.8 %opening.1 = (bf16[4,128,1536]{2,1,0:T(8,128)(2,1)}, bf16[4,384,640]{2,1,0:T(8,128)(2,1)}, bf16[4,384,640]{2,1,0:T(8,128)(2,1)}, bf16[4,40,384]{2,1,0:T(8,128)(2...) custom-call(bf16[128,1536]{1,0:T(8,128)(2,1)} %x_ref.3, bf16[384,1536]{1,0:T(8,128)(2,1)} %refs_1_.1, ...), custom_call_target="tpu_custom_call" | custom-call | bytes 120000000 | tf_op jit(solution)/shard_map/opening/pallas_call | solution.py:395
  50.4 10.6 %attention_forward.1 = (bf16[4,128,1536]{2,1,0:T(8,128)(2,1)}, bf16[4,128,640]{2,1,0:T(8,128)(2,1)}, bf16[4,128,384]{2,1,0:T(8,128)(2,1)}, f32[4,128,128]{2,1,0:T(8,128)}) custom-call(bf16[4,128,1536]{2,1,0:T(8,128)(2,1)} %get-tuple-element.61.x_ref.refs_8_, bf16[4,384,640]{2,1,0:T(8,128)(2,1)} %get-tuple-element.62.w_ref, bf16[384,1536]{1,0:T(8,128)(2,1)} %refs_4_.1, ...), custom_call_target="tpu_custom_call" | custom-call | bytes 45000000 | tf_op jit(solution)/shard_map/attention_forward/pallas_call | solution.py:395
  61.0 16.1 %branch_sum.1.branch_ref = f32[128,1536]{1,0:T(8,128)} custom-call(bf16[4,128,1536]{2,1,0:T(8,128)(2,1)} %get-tuple-element.64.refs_0_), custom_call_target="tpu_custom_call" | custom-call | bytes 45000000 | tf_op jit(solution)/shard_map/branch_sum/pallas_call | solution.py:395
  77.1 2.9 route_forward.1
  80.0 57.5 %dispatch.1 = (bf16[8,4,128,384]{3,2,1,0:T(8,128)(2,1)}, f32[8,2,64,128]{3,2,1,0:T(8,128)}, bf16[4,8,128,384]{3,2,1,0:T(8,128)(2,1)}) custom-call(bf16[4,128,384]{2,1,0:T(8,128)(2,1)} %get-tuple-element.66.refs_0_.norm_ref, f32[2,64,128]{2,1,0:T(8,128)} %get-tuple-element.67.refs_1_), custom_call_target="tpu_custom_call" | custom-call | bytes 126000000 | tf_op jit(solution)/shard_map/dispatch/pallas_call | solution.py:395
  137.4 32.2 %experts.1 = (bf16[8,128,1536]{2,1,0:T(8,128)(2,1)}, bf16[8,128,1536]{2,1,0:T(8,128)(2,1)}, f32[8,8,128]{2,1,0:T(8,128)}, bf16[5,256,512]{2,1,0:T(8,128)(2,1)}, bf16[5,256,1024]{2,1,0:T(8,128)(2,1)}) custom-call(bf16[8,4,128,384]{3,2,1,0:T(8,128)(2,1)} %get-tuple-element.68.nh_ref, bf16[8,4,128,384]{3,2,1,0:T(8,128)(2,1)} %get-tuple-element.69.og_ref.refs_13_, ...), custom_call_target="tpu_custom_call" | custom-call | bytes 120000000 | tf_op jit(solution)/shard_map/experts/pallas_call | solution.py:395
  169.7 51.9 %combine.1 = (f32[128,1536]{1,0:T(8,128)}, f32[8,8,128]{2,1,0:T(8,128)}, f32[4,8,2,8,128]{4,3,2,1,0:T(8,128)}, bf16[4,3,256,1024]{3,2,1,0:T(8,128)(2,1)}) custom-call(bf16[8,128,1536]{2,1,0:T(8,128)(2,1)} %get-tuple-element.76.refs_0_, f32[8,8,128]{2,1,0:T(8,128)} %get-tuple-element.77.refs_1_, f32[8,2,64,128]{3,2,1,0:T(8,128)} %get-tuple-element.75.meta_ref.refs_2_, ...), custom_call_target="tpu_custom_call" | custom-call | bytes 126000000 | tf_op jit(solution)/shard_map/combine/pallas_call | solution.py:395
  221.5 3.7 route_backward.1
  225.3 170.2 %backward.1 = (f32[128,1536]{1,0:T(8,128)}, f32[4,128,384]{2,1,0:T(8,128)}, bf16[8,48,1536]{2,1,0:T(8,128)(2,1)}, bf16[8,48,2560]{2,1,0:T(8,128)(2,1)}, bf16[8,1...) custom-call(bf16[128,1536]{1,0:T(8,128)(2,1)} %get-tuple-element.81., ...), custom_call_target="tpu_custom_call" | custom-call | bytes 390000000 | tf_op jit(solution)/shard_map/backward/pallas_call | solution.py:395
  395.5 30.4 %finish.1 = (f32[5,384,1024]{2,1,0:T(8,128)}, f32[5,512,384]{2,1,0:T(8,128)}, bf16[128,1536]{1,0:T(8,128)(2,1)}, f32[128,1536]{1,0:T(8,128)}, f32[384,1536]{1,0:...) custom-call(bf16[8,4,128,384]{3,2,1,0:T(8,128)(2,1)} %get-tuple-elem, ...), custom_call_target="tpu_custom_call" | custom-call | bytes 60000000 | tf_op jit(solution)/shard_map/finish/pallas_call | solution.py:395
  426.0 1.3 reduce
  427.3 1.3 reduce.1

commit v4 on v3

--- a/solution.py
+++ b/solution.py
@@ -30,13 +30,14 @@
 
 
 class Grid:
-    def __init__(self, axis, A, B):
+    def __init__(self, axis, A, B, step_a=None, step_b=1):
         self.axis, self.A, self.B = axis, A, B
+        self.step_a, self.step_b = B if step_a is None else step_a, step_b
         self.me = lax.axis_index(axis)
-        self.a, self.b = self.me // B, self.me % B
+        self.a, self.b = self.me // self.step_a % A, self.me // self.step_b % B
 
     def at(self, a, b):
-        return a * self.B + b
+        return a * self.step_a + b * self.step_b
 
     def dev(self, a, b):
         return {self.axis: self.at(a, b)}
@@ -51,11 +52,7 @@
                 (self.a > 0, self.dev(self.a - 1, self.b)),
                 (self.a < self.A - 1, self.dev(self.a + 1, self.b)),
             ]
-        if self.B > 1:
-            found += [
-                (self.b > 0, self.dev(self.a, self.b - 1)),
-                (self.b < self.B - 1, self.dev(self.a, self.b + 1)),
-            ]
+        found += [(self.me >= 0, self.dev(self.a, (self.b + r) % self.B)) for r in range(1, self.B)]
         return found
 
     def all(self):
@@ -104,6 +101,11 @@
 def begin(step):
     next(step)
     return step
+
+
+def advance(step, count):
+    for _ in range(count):
+        next(step)
 
 
 def run(*steps):
@@ -205,110 +207,87 @@
 
 def sum_slots(A, B, block, dtype=BF16):
     return [
-        pltpu.VMEM((2, A - 1) + block, dtype),
-        pltpu.VMEM((2, A - 1) + block, dtype),
-        pltpu.VMEM((2, A, B - 1) + block, dtype),
-        pltpu.VMEM((2, A, B - 2) + block if B > 2 else (8, 128), dtype),
+        pltpu.VMEM((A + 1,) + block, dtype),
+        pltpu.VMEM((A,) + block, dtype),
+        pltpu.VMEM((A, B - 1) + block, dtype),
     ]
 
 
 def reduce(g, part, finish, sems, slots):
     send_a, recv_a, send_b, recv_b = sems
-    land_a, out_a, land_b, out_b = slots
+    land_a, out_a, land_b = slots
     A, B = g.A, g.B
     row = lambda way, k: g.a + k if way == 0 else g.a - k
-    col = lambda way, k: g.b + k if way == 0 else g.b - k
     rows = [(way, k) for k in range(A - 1, 0, -1) for way in (0, 1)] + [(0, 0)]
     here = g.here()
-    first = lambda kind, way: jnp.logical_not(g.behind(kind, way, 1))
-
+
+    def across(a, r):
+        to = (g.b + r) % B
+        return remote(part(g.at(a, to)), land_b.at[a, r - 1], send_b.at[0, a, r], recv_b.at[0, a, r], g.dev(g.a, to))
+
+    def landing(way, k):
+        return land_a.at[A if k == 0 and way == 1 else row(way, k)]
+
+    def along(way, k):
+        to = A if k == 1 and way == 1 else row(way, k)
+        return remote(
+            out_a.at[row(way, k)], land_a.at[to], send_a.at[way, k], recv_a.at[way, k - 1], g.next("a", way)[1]
+        )
+
+    def landed(way, k):
+        remote(landing(way, k), landing(way, k), send_a.at[way, k], recv_a.at[way, k], here).wait_recv()
+
+    for way, k in rows:
+
+        @pl.when(g.ahead("a", way, k))
+        def _():
+            for r in range(1, B):
+                across(row(way, k), r).start()
+
+    yield
     for way, k in rows:
 
         @pl.when(g.ahead("a", way, k))
         def _():
             a = row(way, k)
-            for j in range(B - 1, 0, -1):
-                for w in (0, 1):
-
-                    @pl.when(g.ahead("b", w, j) & first("b", w))
-                    def _():
-                        remote(
-                            part(g.at(a, col(w, j))),
-                            land_b.at[w, a, j - 1],
-                            send_b.at[w, a, j],
-                            recv_b.at[w, a, j - 1],
-                            g.next("b", w)[1],
-                        ).start()
-
-    yield
-    for way, k in rows:
-
-        @pl.when(g.ahead("a", way, k))
-        def _():
-            a = row(way, k)
-            for j in range(B - 2, 0, -1):
-                for w in (0, 1):
-
-                    @pl.when(g.ahead("b", w, j) & g.behind("b", w, 1))
-                    def _():
-                        remote(land_b.at[w, a, j], land_b.at[w, a, j], send_b.at[w, a, j], recv_b.at[w, a, j], here).wait_recv()
-                        out_b[w, a, j - 1] = (
-                            part(g.at(a, col(w, j)))[...].astype(F32) + land_b[w, a, j].astype(F32)
-                        ).astype(out_b.dtype)
-                        remote(
-                            out_b.at[w, a, j - 1],
-                            land_b.at[w, a, j - 1],
-                            send_b.at[w, a, j],
-                            recv_b.at[w, a, j - 1],
-                            g.next("b", w)[1],
-                        ).start()
-
-            for w in (0, 1):
-                if B > 1:
-
-                    @pl.when(g.behind("b", w, 1))
-                    def _():
-                        remote(land_b.at[w, a, 0], land_b.at[w, a, 0], send_b.at[w, a, 0], recv_b.at[w, a, 0], here).wait_recv()
+            for r in range(1, B):
+                mine = land_b.at[a, r - 1]
+                remote(mine, mine, send_b.at[0, a, r], recv_b.at[0, a, r], here).wait_recv()
 
             def near():
                 total = part(g.at(a, g.b))[...].astype(F32)
-                if B == 2:
-                    return total + land_b[1 - g.b, a, 0].astype(F32)
-                for w in (0, 1):
-                    if B > 1:
-                        total = total + jnp.where(g.behind("b", w, 1), land_b[w, a, 0].astype(F32), 0.0)
+                for r in range(1, B):
+                    total = total + land_b[a, r - 1].astype(F32)
                 return total
 
             if k > 0:
-
-                @pl.when(g.behind("a", way, 1))
+                if k < A - 1:
+
+                    @pl.when(g.behind("a", way, 1))
+                    def _():
+                        landed(way, k)
+                        out_a[a] = (near() + landing(way, k)[...].astype(F32)).astype(out_a.dtype)
+
+                @pl.when(jnp.logical_not(g.behind("a", way, 1)))
                 def _():
-                    if k < A - 1:
-                        remote(land_a.at[way, k], land_a.at[way, k], send_a.at[way, k], recv_a.at[way, k], here).wait_recv()
-                        out_a[way, k - 1] = (near() + land_a[way, k].astype(F32)).astype(out_a.dtype)
-
-                @pl.when(first("a", way))
-                def _():
-                    out_a[way, k - 1] = near().astype(out_a.dtype)
-
-                remote(
-                    out_a.at[way, k - 1], land_a.at[way, k - 1], send_a.at[way, k], recv_a.at[way, k - 1], g.next("a", way)[1]
-                ).start()
+                    out_a[a] = near().astype(out_a.dtype)
+
+                along(way, k).start()
             else:
                 for w in (0, 1):
                     if A > 1:
 
                         @pl.when(g.behind("a", w, 1))
                         def _():
-                            remote(land_a.at[w, 0], land_a.at[w, 0], send_a.at[w, 0], recv_a.at[w, 0], here).wait_recv()
+                            landed(w, 0)
 
                 total = near()
                 if A == 2:
-                    total = total + land_a[1 - g.a, 0].astype(F32)
+                    total = total + land_a[jnp.where(g.a == 1, 1, A)].astype(F32)
                 else:
                     for w in (0, 1):
                         if A > 1:
-                            total = total + jnp.where(g.behind("a", w, 1), land_a[w, 0].astype(F32), 0.0)
+                            total = total + jnp.where(g.behind("a", w, 1), landing(w, 0)[...].astype(F32), 0.0)
                 finish(total)
 
         yield
@@ -316,16 +295,10 @@
 
         @pl.when(g.ahead("a", way, k))
         def _():
-            a = row(way, k)
-            for j in range(B - 1, 0, -1):
-                for w in (0, 1):
-
-                    @pl.when(g.ahead("b", w, j))
-                    def _():
-                        remote(part(g.me), land_b.at[w, a, j - 1], send_b.at[w, a, j], recv_b.at[w, a, j - 1], here).wait_send()
-
+            for r in range(1, B):
+                across(row(way, k), r).wait_send()
             if k > 0:
-                remote(out_a.at[way, k - 1], land_a.at[way, k - 1], send_a.at[way, k], recv_a.at[way, k - 1], here).wait_send()
+                along(way, k).wait_send()
 
 
 def reduce_gather(g, part, out, kept, sems, slots):
@@ -587,55 +560,30 @@
     )
 
 
-def experts(n_expert, slots, tokens, nh_ref, og_ref, meta_ref, up_ref, down_ref, out_ref, back_ref, gate_grad_ref, inner_ref, both_ref, x_sc, og_sc, eo_sc, gx_sc, nh_in, og_in, sems):
-    step = pl.program_id(0)
-    mine = pl.ds(pl.multiple_of(lax.axis_index("expert") * SLOT_STRIDE, SLOT_STRIDE), SLOT_STRIDE)
-    ranks, _, shard = nh_ref.shape[1:]
-    width = ranks * shard
-    hidden = down_ref.shape[1]
-
-    def fetch(q):
-        slot = q % 2
-        return [
-            pltpu.make_async_copy(nh_ref.at[q], nh_in.at[slot], sems.at[0, slot]),
-            pltpu.make_async_copy(og_ref.at[q], og_in.at[slot], sems.at[1, slot]),
-        ]
-
-    @pl.when(step == 0)
-    def _():
-        for copy in fetch(0):
-            copy.start()
-
-        def one(q, carry):
-            @pl.when(q + 1 < n_expert)
-            def _():
-                for copy in fetch(q + 1):
-                    copy.start()
-
-            for copy in fetch(q):
-                copy.wait()
-            pick = row_picks(slots, meta_ref[q, 0, mine, :]).astype(BF16)
-            for i in range(ranks):
-                here = slice(i * shard, (i + 1) * shard)
-                x_sc[q, :, here] = dot(pick, nh_in[q % 2, i]).astype(BF16)
-                og_sc[q, :, here] = dot(pick, og_in[q % 2, i]).astype(BF16)
-            gate_grad_ref[q] = jnp.zeros((SLOT_STRIDE, tokens), F32)
-            return carry
-
-        lax.fori_loop(0, n_expert, one, 0)
-
-    place_of = pl.ds(pl.multiple_of(step * SLOT_ROWS, SLOT_ROWS), SLOT_ROWS)
-    slot_row = lax.broadcasted_iota(jnp.int32, (SLOT_STRIDE, tokens), 0) == step
+def pick_rows(slots, n_expert, mine, meta_ref, block, to_sc):
+    def one(q, carry):
+        pick = row_picks(slots, meta_ref[q, 0, mine, :]).astype(BF16)
+        ranks, _, shard = block(q).shape
+        for i in range(ranks):
+            to_sc[q, :, i * shard : (i + 1) * shard] = dot(pick, block(q)[i]).astype(BF16)
+        return carry
+
+    lax.fori_loop(0, n_expert, one, 0)
+
+
+def expert_slot(n_expert, tokens, s, mine, meta_ref, up_ref, down_ref, gate_grad_ref, inner_ref, both_ref, x_sc, og_sc):
+    width = x_sc.shape[2]
+    hidden = down_ref.shape[0]
+    place_of = pl.ds(pl.multiple_of(s * SLOT_ROWS, SLOT_ROWS), SLOT_ROWS)
+    slot_row = lax.broadcasted_iota(jnp.int32, (SLOT_STRIDE, tokens), 0) == s
     number = lax.broadcasted_iota(jnp.int32, (SLOT_ROWS, tokens), 0).astype(F32)
     rows = n_expert * SLOT_ROWS
-    x = x_sc[:, place_of, :].reshape(rows, width)
-    both = dot(x, up_ref[0])
+    both = dot(x_sc[:, place_of, :].reshape(rows, width), up_ref[...])
     gate, up = both[:, :hidden], both[:, hidden:]
     squash = jax.nn.sigmoid(gate)
     inner = (gate * squash * up).astype(BF16)
-    inner_ref[0] = inner
-    produced = dot(inner, down_ref[0]).astype(BF16)
-    eo_sc[:, place_of, :] = produced.reshape(n_expert, SLOT_ROWS, width)
+    inner_ref[s] = inner
+    produced = dot(inner, down_ref[...]).astype(BF16)
     masks, gates = [], []
     for q in range(n_expert):
         place = jnp.sum(jnp.where(slot_row, meta_ref[q, 0, mine, :], 0.0), axis=0, keepdims=True)
@@ -645,27 +593,28 @@
     mix_grad = RESIDUAL_SCALE * og_sc[:, place_of, :].reshape(rows, width).astype(F32)
     grad_rows = (jnp.concatenate(gates, axis=0) * mix_grad).astype(BF16)
     gate_grad = jnp.sum(mix_grad * produced.astype(F32), axis=1, keepdims=True)
+    og_sc[:, place_of, :] = produced.reshape(n_expert, SLOT_ROWS, width)
     for q in range(n_expert):
         spread = jnp.where(masks[q], gate_grad[q * SLOT_ROWS : (q + 1) * SLOT_ROWS], 0.0)
         gate_grad_ref[q] = jnp.where(slot_row, jnp.sum(spread, axis=0, keepdims=True), gate_grad_ref[q])
-    grad_inner = dot(grad_rows, down_ref[0], ((1,), (1,)))
+    grad_inner = dot(grad_rows, down_ref[...], ((1,), (1,)))
     grad_both = jnp.concatenate(
         [grad_inner * up * squash * (1.0 + gate * (1.0 - squash)), grad_inner * (gate * squash)], axis=1
     ).astype(BF16)
-    both_ref[0] = grad_both
-    gx_sc[:, place_of, :] = dot(grad_both, up_ref[0], ((1,), (1,))).astype(BF16).reshape(n_expert, SLOT_ROWS, width)
-
-    @pl.when(step == slots - 1)
-    def _():
-        def one(q, carry):
-            pick = row_picks(slots, meta_ref[q, 0, mine, :])
-            high, low = halves(pick * row_shares(slots, meta_ref[q, 1, mine, :]))
-            over = ((0,), (0,))
-            out_ref[q] = (dot(high, eo_sc[q], over) + dot(low, eo_sc[q], over)).astype(BF16)
-            back_ref[q] = dot(pick.astype(BF16), gx_sc[q], over).astype(BF16)
-            return carry
-
-        lax.fori_loop(0, n_expert, one, 0)
+    both_ref[s] = grad_both
+    x_sc[:, place_of, :] = dot(grad_both, up_ref[...], ((1,), (1,))).astype(BF16).reshape(n_expert, SLOT_ROWS, width)
+
+
+def sum_rows_back(slots, n_expert, mine, meta_ref, out_ref, back_ref, eo_sc, gx_sc):
+    def one(q, carry):
+        pick = row_picks(slots, meta_ref[q, 0, mine, :])
+        high, low = halves(pick * row_shares(slots, meta_ref[q, 1, mine, :]))
+        over = ((0,), (0,))
+        back_ref[q] = dot(pick.astype(BF16), gx_sc[q], over).astype(BF16)
+        out_ref[q] = (dot(high, eo_sc[q], over) + dot(low, eo_sc[q], over)).astype(BF16)
+        return carry
+
+    lax.fori_loop(0, n_expert, one, 0)
 
 
 def route_backward(ranks, n_expert, shard, hidden_ref, norm_ref, scale_ref, probs_ref, misc_ref, router_ref, og_ref, back_ref, gate_grad_ref, grad_hidden_ref, branch_ref, small_ref):
@@ -754,7 +703,7 @@
     sums_ref[used : used + 8, :] = jnp.where(second == 0, small[used:], jnp.where(second == 1, gain_grad, 0.0)).astype(BF16)
 
 
-def finish(ranks, n_expert, slots, early, heads, tokens, nh_ref, og_ref, xd_ref, ogd_ref, meta_ref, own_both_ref, both_ref, late_both_ref, own_inner_ref, inner_ref, grad_ref, x_ref, misc_ref, grad_hidden_ref, hidden_ref, mixture_ref, d_w_ref, d_o_ref, sums_ref, d_up_ref, d_down_ref, output_ref, grad_inputs_ref, q_ref, k_ref, v_ref, o_ref, router_ref, gain_one_ref, gain_two_ref, x_sc, og_sc, x_in, og_in, sems):
+def finish(ranks, n_expert, slots, early, heads, tokens, og_ref, xd_ref, ogd_ref, meta_ref, own_both_ref, both_ref, late_both_ref, own_inner_ref, inner_ref, grad_ref, x_ref, misc_ref, grad_hidden_ref, hidden_ref, mixture_ref, d_w_ref, d_o_ref, sums_ref, d_up_ref, d_down_ref, output_ref, grad_inputs_ref, q_ref, k_ref, v_ref, o_ref, router_ref, gain_one_ref, gain_two_ref, x_sc, og_sc, x_in, og_in, sems):
     step = pl.program_id(0)
     me = lax.axis_index("dp")
     rows = n_expert * SLOT_ROWS
@@ -764,8 +713,8 @@
     def _():
         def fetch(j, do):
             at, slot = (me + j) % ranks, j % 2
-            x, og = (nh_ref.at[:, me], og_ref.at[:, me]) if j == 0 else (xd_ref.at[at], ogd_ref.at[at])
-            do(pltpu.make_async_copy(x, x_in.at[slot], sems.at[0, slot]))
+            og = og_ref.at[:, me] if j == 0 else ogd_ref.at[at]
+            do(pltpu.make_async_copy(xd_ref.at[at], x_in.at[slot], sems.at[0, slot]))
             do(pltpu.make_async_copy(og, og_in.at[slot], sems.at[1, slot]))
 
         fetch(0, lambda copy: copy.start())
@@ -859,11 +808,13 @@
     cosine, sine = rope_tables(tokens, heads)
 
     gains = jnp.stack([norm1_gain, norm2_gain]).astype(F32)
-
-    def opening(*refs):
+    dma = pltpu.SemaphoreType.DMA
+
+    def forward(*refs):
         take = taker(refs)
-        x, wq, wk, wv, rt, gn, sg, og = take(8)
-        x_all, w, w_all, rt_all, ms_all, og_all, ms, og_own = take(8)
+        x, wq, wk, wv, rt, gn, sg, og, wo, cs, sn, routes_ref, blocks_ref = take(13)
+        w, ms_all, og_all, qkv, att, scale_one, xc, hidden_ref, norm, scale_two, probs, meta, table = take(13)
+        x_all, w_all, rt_all, ms, og_own, part, branch, own_sem = take(8)
         dp, ex = Grid(*group), Grid(*plane)
         for i in range(ranks):
             at = 0
@@ -879,73 +830,58 @@
         x_all[dp.me] = x[...]
         rt_all[dp.me] = rt[...]
         ms_all[dp.me] = ms[...]
-        og_all[ex.me] = og_own[...]
         greet(dp.all() + ex.near())
+        keep = pltpu.make_async_copy(og_own, og_all.at[ex.me], own_sem)
+        keep.start()
         small = [begin(gather(dp, ms, ms_all, take(4))), begin(gather(dp, rt, rt_all, take(4)))]
         xs = begin(gather(dp, x, x_all, take(4)))
+        ws = begin(exchange(dp, w, w_all, take(2)))
         ogs = begin(gather(ex, og_own, og_all, take(4)))
-        ws = begin(exchange(dp, w, w_all, take(2)))
-        run(*small, xs, ogs)
+        run(*small, xs)
+        for i in range(ranks):
+
+            @pl.when(dp.me == i)
+            def _():
+                for b in range(ranks):
+                    xc[b * tokens : (b + 1) * tokens, :] = x_all[b, :, i * shard : (i + 1) * shard]
+
+        advance(ogs, 2 * (plane[1] - 1))
         run(ws)
-
-    x_all, weights, w_all, router_all, misc_all, og_all = call(
-        opening,
-        "opening",
+        attention_forward(ranks, heads, tokens, x_all, w_all, wo, ms_all, cs, sn, part, qkv, att, scale_one)
+
+        def store(total):
+            branch[...] = total
+
+        run(reduce(dp, lambda i: part.at[i], store, take(4), take(3)))
+        route_forward(ranks, n_expert, slots, x, branch, ms_all, rt_all, routes_ref, blocks_ref, hidden_ref, norm, scale_two, probs, meta, table)
+        run(ogs)
+        keep.wait()
+
+    (
+        weights,
+        misc_all,
+        og_all,
+        qkv,
+        att,
+        scale_one,
+        x_cols,
+        hidden_rows,
+        norm_hidden,
+        scale_two,
+        probs,
+        meta,
+        router,
+    ) = call(
+        forward,
+        "forward",
         [
-            ((ranks, tokens, width), BF16),
             ((ranks, shard, heads.cols), BF16),
-            ((ranks, shard, heads.cols), BF16),
-            ((ranks, router_weight.shape[1], shard), BF16),
             ((ranks, 16, shard), F32),
             ((n_expert, ranks, tokens, shard), BF16),
-        ],
-        (inputs, q_weight, k_weight, value_matrix, router_weight.T, gains, segment_ids, out_grad),
-        [pltpu.VMEM((16, shard), F32), pltpu.VMEM((ranks, tokens, shard), BF16)]
-        + line_sems(*group[1:]) * 3
-        + line_sems(*plane[1:])
-        + exchange_sems(ranks),
-        cid=0,
-        us=40,
-    )
-
-    part, qkv, att, scale_all = call(
-        functools.partial(attention_forward, ranks, heads, tokens),
-        "attention_forward",
-        [
-            ((ranks, tokens, width), BF16),
             ((ranks, tokens, heads.cols), BF16),
             ((ranks, tokens, heads.q_cols), BF16),
             ((ranks, tokens, 128), F32),
-        ],
-        (x_all, w_all, o_weight, misc_all, cosine, sine),
-        us=15,
-    )
-
-    def branch_sum(*refs):
-        take = taker(refs)
-        terms, out = take(2)
-        dp = Grid(*group)
-        greet(dp.near())
-
-        def finish(total):
-            out[...] = total
-
-        run(reduce(dp, lambda i: terms.at[i], finish, take(4), take(4)))
-
-    (branch,) = call(
-        branch_sum,
-        "branch_sum",
-        [((tokens, width), F32)],
-        (part,),
-        line_sems(*group[1:]) + sum_slots(*group[1:], (tokens, width)),
-        cid=1,
-        us=15,
-    )
-
-    hidden_rows, norm_hidden, scale_two, probs, meta, router = call(
-        functools.partial(route_forward, ranks, n_expert, slots),
-        "route_forward",
-        [
+            ((ranks * tokens, shard), BF16),
             ((tokens, width), F32),
             ((ranks, tokens, shard), BF16),
             ((tokens, 128), F32),
@@ -953,122 +889,184 @@
             ((2, used, tokens), F32),
             ((width, 128), BF16),
         ],
-        (inputs, branch, misc_all, router_all, routes.T, expert_blocks),
-        us=5,
-        in_specs=[VMEM] * 5 + [pl.BlockSpec(memory_space=pltpu.SMEM)],
+        (
+            inputs,
+            q_weight,
+            k_weight,
+            value_matrix,
+            router_weight.T,
+            gains,
+            segment_ids,
+            out_grad,
+            o_weight,
+            cosine,
+            sine,
+            routes.T,
+            expert_blocks,
+        ),
+        [
+            pltpu.VMEM((ranks, tokens, width), BF16),
+            pltpu.VMEM((ranks, shard, heads.cols), BF16),
+            pltpu.VMEM((ranks, router_weight.shape[1], shard), BF16),
+            pltpu.VMEM((16, shard), F32),
+            pltpu.VMEM((ranks, tokens, shard), BF16),
+            pltpu.VMEM((ranks, tokens, width), BF16),
+            pltpu.VMEM((tokens, width), F32),
+            dma(()),
+        ]
+        + line_sems(*group[1:]) * 3
+        + exchange_sems(ranks)
+        + line_sems(*plane[1:])
+        + line_sems(*group[1:])
+        + sum_slots(*group[1:], (tokens, width)),
+        cid=0,
+        us=70,
+        in_specs=[VMEM] * 12 + [pl.BlockSpec(memory_space=pltpu.SMEM)],
+        out_specs=[VMEM] * 2 + [ANY] + [VMEM] * 10,
     )
 
-    def dispatch(*refs):
+    fixed = lambda shape: pl.BlockSpec(shape, lambda s: (0,) * len(shape), pipeline_mode=pl.Buffered(1))
+    moving = lambda shape: pl.BlockSpec((1,) + shape, lambda s: (s,) + (0,) * len(shape))
+    rows = n_expert * SLOT_ROWS
+    deep = 2 if ranks * rows <= 1024 else 1
+    early = slots * 3 // 5
+
+    def mixture_of_experts(*refs):
         take = taker(refs)
-        (nh, mt), (nh_all, mt_all, xd) = take(2), take(3)
+        nh, mt, hid, sc, pb, ms, tb, og_mine, og, up, down = take(11)
+        out_part, inr, gb, grad_hidden_ref, branch_ref, small_ref, mt_group, xd, gb_all = take(9)
+        nh_all, mt_all, gg, gg_all, back_part, mt_own, x_sc, og_sc, og_in, up_in, down_in = take(11)
+        og_sems, up_sems, own_sems = take(3)
         dp, ex = Grid(*group), Grid(*plane)
+        mine = pl.ds(pl.multiple_of(ex.me * SLOT_STRIDE, SLOT_STRIDE), SLOT_STRIDE)
         nh_all[ex.me] = nh[...]
         mt_all[ex.me] = mt[...]
-        greet(dp.all() + ex.near())
-        arrived, end = pass_slices(dp, xd, take(2))
-        run(gather(ex, nh, nh_all, take(4), arrived), gather(ex, mt, mt_all, take(4)))
+        gg[...] = jnp.zeros_like(gg)
+
+        def fetch(s, do):
+            do(pltpu.make_async_copy(up.at[s], up_in.at[s % deep], up_sems.at[0, s % deep]))
+            do(pltpu.make_async_copy(down.at[s], down_in.at[s % deep], up_sems.at[1, s % deep]))
+
+        for s in range(deep):
+            fetch(s, lambda copy: copy.start())
+        greet(dp.all() + ex.all())
+        mts = begin(gather(ex, mt, mt_all, take(4)))
+        passed, end = pass_slices(dp, xd, take(2))
+
+        def keep(i, block):
+            return pltpu.make_async_copy(block.at[dp.me], xd.at[dp.me, i], own_sems.at[i])
+
+        def arrived(i, block):
+            passed(i, block)
+            keep(i, block).start()
+
+        nhs = begin(gather(ex, nh, nh_all, take(4), arrived))
+        run(mts)
+
+        def fetch_og(q):
+            return pltpu.make_async_copy(og.at[q], og_in.at[q % 2], og_sems.at[q % 2])
+
+        fetch_og(0).start()
+
+        def pick_og(q, carry):
+            @pl.when(q + 1 < n_expert)
+            def _():
+                fetch_og(q + 1).start()
+
+            fetch_og(q).wait()
+            pick = row_picks(slots, mt_all[q, 0, mine, :]).astype(BF16)
+            for i in range(ranks):
+                og_sc[q, :, i * shard : (i + 1) * shard] = dot(pick, og_in[q % 2, i]).astype(BF16)
+            return carry
+
+        lax.fori_loop(0, n_expert, pick_og, 0)
+        mt_own[...] = mt_all[:, :, mine, :]
+        mt_group[dp.me] = mt_own[...]
+        mgs = begin(gather(dp, mt_own, mt_group, take(4)))
+        run(nhs)
+        pick_rows(slots, n_expert, mine, mt_all, lambda q: nh_all.at[q], x_sc)
+
+        def one(s, carry):
+            fetch(s, lambda copy: copy.wait())
+            expert_slot(n_expert, tokens, s, mine, mt_all, up_in.at[s % deep], down_in.at[s % deep], gg, inr, gb, x_sc, og_sc)
+
+            @pl.when(s + deep < slots)
+            def _():
+                fetch(s + deep, lambda copy: copy.start())
+
+            return carry
+
+        lax.fori_loop(0, slots, one, 0)
+        run(mgs)
+        gbs = begin(gather(dp, gb.at[pl.ds(0, early)], gb_all, take(4)))
+        sum_rows_back(slots, n_expert, mine, mt_all, out_part, back_part, og_sc, x_sc)
+
+        def store(total):
+            grad_hidden_ref[...] = total
+
+        ggs = begin(exchange(ex, gg, gg_all, take(2)))
+        run(reduce(ex, lambda i: back_part.at[i], store, take(4), take(3)))
+        run(ggs)
+        route_backward(ranks, n_expert, shard, hid, nh, sc, pb, ms, tb, og_mine, grad_hidden_ref, gg_all, grad_hidden_ref, branch_ref, small_ref)
+        run(gbs)
         end(range(n_expert), nh)
-
-    norm_all, meta_all, norm_slices = call(
-        dispatch,
-        "dispatch",
-        [
-            ((n_expert, ranks, tokens, shard), BF16),
-            ((n_expert, 2, used, tokens), F32),
-            ((ranks, n_expert, tokens, shard), BF16),
-        ],
-        (norm_hidden, meta),
-        [pltpu.SemaphoreType.DMA((n_expert, ranks))] * 2 + line_sems(*plane[1:]) * 2,
-        cid=2,
-        us=42,
-        out_specs=[VMEM, VMEM, ANY],
-    )
-
-    fixed = lambda shape: pl.BlockSpec(shape, lambda s: (0,) * len(shape), pipeline_mode=pl.Buffered(1))
-    moving = lambda shape: pl.BlockSpec((1,) + shape, lambda s: (s,) + (0,) * len(shape))
-    packed = (n_expert, slots * SLOT_ROWS, width)
-    rows = n_expert * SLOT_ROWS
-    out_part, back_part, gate_grad, inner, grad_both = call(
-        functools.partial(experts, n_expert, slots, tokens),
-        "experts",
+        for i in range(n_expert):
+            keep(i, nh).wait()
+
+    out_part, inner, grad_both, grad_hidden, grad_branch, small, meta_group, norm_slices, both_all = call(
+        mixture_of_experts,
+        "mixture_of_experts",
         [
             ((n_expert, tokens, width), BF16),
-            ((n_expert, tokens, width), BF16),
-            ((n_expert, SLOT_STRIDE, tokens), F32),
             ((slots, rows, hidden), BF16),
             ((slots, rows, double), BF16),
-        ],
-        (norm_all, og_all, meta_all, expert_gate_up, expert_down),
-        [pltpu.VMEM(packed, BF16)] * 4
-        + [pltpu.VMEM((2, ranks, tokens, shard), BF16)] * 2
-        + [pltpu.SemaphoreType.DMA((2, 2))],
-        us=40,
-        grid=(slots,),
-        in_specs=[ANY, ANY, fixed((n_expert, 2, used, tokens)), moving((width, double)), moving((hidden, width))],
-        out_specs=[
-            fixed((n_expert, tokens, width)),
-            fixed((n_expert, tokens, width)),
-            fixed((n_expert, SLOT_STRIDE, tokens)),
-            moving((rows, hidden)),
-            moving((rows, double)),
-        ],
-    )
-
-    early = slots * 3 // 5
-
-    def combine(*refs):
-        take = taker(refs)
-        (back_terms, gg, mt, gb), (back, gg_all, mt_all, gb_all) = take(4), take(4)
-        mt_own = take()
-        dp, ex = Grid(*group), Grid(*plane)
-        mine = pl.ds(pl.multiple_of(ex.me * SLOT_STRIDE, SLOT_STRIDE), SLOT_STRIDE)
-        mt_own[...] = mt[:, :, mine, :]
-        mt_all[dp.me] = mt_own[...]
-        greet(dp.all() + ex.all())
-
-        def store(total):
-            back[...] = total
-
-        ggs = begin(exchange(ex, gg, gg_all, take(2)))
-        mts = begin(gather(dp, mt_own, mt_all, take(4)))
-        backs = begin(reduce(ex, lambda i: back_terms.at[i], store, take(4), take(4)))
-        gbs = begin(gather(dp, gb.at[pl.ds(0, early)], gb_all, take(4)))
-        run(ggs, mts)
-        run(backs)
-        run(gbs)
-
-    back, gate_grads, meta_group, both_all = call(
-        combine,
-        "combine",
-        [
-            ((tokens, width), F32),
-            ((n_expert, SLOT_STRIDE, tokens), F32),
-            ((ranks, n_expert, 2, SLOT_STRIDE, tokens), F32),
-            ((ranks, early, rows, double), BF16),
-        ],
-        (back_part, gate_grad, meta_all, grad_both),
-        [pltpu.VMEM((n_expert, 2, SLOT_STRIDE, tokens), F32)]
-        + exchange_sems(n_expert)
-        + line_sems(*group[1:])
-        + line_sems(*plane[1:])
-        + sum_slots(*plane[1:], (tokens, width))
-        + line_sems(*group[1:]),
-        cid=3,
-        us=42,
-        in_specs=[VMEM] * 3 + [ANY],
-        out_specs=[VMEM] * 3 + [ANY],
-    )
-
-    grad_hidden, grad_branch, small = call(
-        functools.partial(route_backward, ranks, n_expert, shard),
-        "route_backward",
-        [
             ((tokens, width), F32),
             ((tokens, width), BF16),
             ((ranks, used + 8, shard), F32),
+            ((ranks, n_expert, 2, SLOT_STRIDE, tokens), F32),
+            ((ranks, n_expert, tokens, shard), BF16),
+            ((ranks, early, rows, double), BF16),
         ],
-        (hidden_rows, norm_hidden, scale_two, probs, misc_all, router, out_grad, back, gate_grads),
-        us=6,
+        (
+            norm_hidden,
+            meta,
+            hidden_rows,
+            scale_two,
+            probs,
+            misc_all,
+            router,
+            out_grad,
+            og_all,
+            expert_gate_up,
+            expert_down,
+        ),
+        [
+            pltpu.VMEM((n_expert, ranks, tokens, shard), BF16),
+            pltpu.VMEM((n_expert, 2, used, tokens), F32),
+            pltpu.VMEM((n_expert, SLOT_STRIDE, tokens), F32),
+            pltpu.VMEM((n_expert, SLOT_STRIDE, tokens), F32),
+            pltpu.VMEM((n_expert, tokens, width), BF16),
+            pltpu.VMEM((n_expert, 2, SLOT_STRIDE, tokens), F32),
+            pltpu.VMEM((n_expert, slots * SLOT_ROWS, width), BF16),
+            pltpu.VMEM((n_expert, slots * SLOT_ROWS, width), BF16),
+            pltpu.VMEM((2, ranks, tokens, shard), BF16),
+            pltpu.VMEM((deep, width, double), BF16),
+            pltpu.VMEM((deep, hidden, width), BF16),
+            dma((2,)),
+            dma((2, deep)),
+            dma((n_expert,)),
+        ]
+        + line_sems(*plane[1:])
+        + [dma((n_expert, ranks))] * 2
+        + line_sems(*plane[1:])
+        + line_sems(*group[1:]) * 2
+        + exchange_sems(n_expert)
+        + line_sems(*plane[1:])
+        + sum_slots(*plane[1:], (tokens, width)),
+        cid=1,
+        us=115,
+        in_specs=[VMEM] * 8 + [ANY] * 3,
+        out_specs=[VMEM] * 7 + [ANY] * 2,
     )
 
     sum_rows = 16 * n_expert
@@ -1077,9 +1075,9 @@
 
     def backward(*refs):
         take = taker(refs)
-        br, sm, at, qkv, wo, ms, cs, sn, xa, sc, gn, w, terms, og, gb, inr = take(16)
+        br, sm, at, qkv, wo, ms, cs, sn, xc, sc, gn, w, terms, og, gb, inr = take(16)
         mix, gx_all, do_all, dw_all, su_all, ogd, gb_all, inr_all = take(8)
-        br_all, sm_all, gr, gr_all, do, dw, su, gx, xc = take(9)
+        br_all, sm_all, gr, gr_all, do, dw, su, gx = take(8)
         dp, ex = Grid(*group), Grid(*plane)
         br_all[dp.me] = br[...]
         greet(dp.all() + ex.near())
@@ -1089,36 +1087,30 @@
 
         brs = begin(gather(dp, br, br_all, take(4)))
         sms = begin(exchange(dp, sm, sm_all, take(2)))
-        outs = begin(reduce(ex, lambda i: terms.at[i], store, take(4), take(4)))
+        outs = begin(reduce(ex, lambda i: terms.at[i], store, take(4), take(3)))
         run(brs)
-        arrived, end = pass_slices(dp, ogd, take(2))
+        passed, end = pass_slices(dp, ogd, take(2))
         for i in range(n_expert // 3):
-            arrived(i, og.at[i])
-        for i in range(ranks):
-
-            @pl.when(dp.me == i)
-            def _():
-                for b in range(ranks):
-                    xc[b * tokens : (b + 1) * tokens, :] = xa[b, :, i * shard : (i + 1) * shard]
-
+            passed(i, og.at[i])
+        advance(outs, 2)
         attention_backward(ranks, heads, tokens, br_all, at, qkv, wo, ms, cs, sn, gr, do)
         gr_all[dp.me] = gr[...]
         grs = begin(gather(dp, gr, gr_all, take(4)))
-        dos = begin(reduce_gather(ex, lambda i: do.at[i], do_all, take(), take(8), take(4)))
+        dos = begin(reduce_gather(ex, lambda i: do.at[i], do_all, take(), take(8), take(3)))
+        advance(outs, 2)
         run(sms)
-        run(outs)
         run(grs)
         for i in range(n_expert // 3, n_expert):
-            arrived(i, og.at[i])
+            passed(i, og.at[i])
         inrs = begin(gather(dp, inr, inr_all, take(4)))
         gbs = begin(gather(dp, gb.at[pl.ds(early, slots - early)], gb_all, take(4)))
+        advance(outs, 2)
         projection_backward(ranks, heads, shard, xc, sc, gn, gr_all, w, sm_all, gx, dw, su)
         gxs = begin(exchange(dp, gx, gx_all, take(2)))
-        sus = begin(reduce_gather(ex, lambda i: su.at[pl.ds(pl.multiple_of(i * 16, 16), 16)], su_all, take(), take(8), take(4)))
-        dws = begin(reduce_gather(ex, lambda i: dw.at[i], dw_all, take(), take(8), take(4)))
-        run(dos)
-        run(sus)
-        run(dws)
+        dws = begin(reduce_gather(ex, lambda i: dw.at[i], dw_all, take(), take(8), take(3)))
+        sus = begin(reduce_gather(ex, lambda i: su.at[pl.ds(pl.multiple_of(i * 16, 16), 16)], su_all, take(), take(8), take(3)))
+        run(outs)
+        run(dos, dws, sus)
         run(gxs)
         run(inrs)
         run(gbs)
@@ -1147,8 +1139,8 @@
             misc_all,
             cosine,
             sine,
-            x_all,
-            scale_all.reshape(ranks * tokens, 128),
+            x_cols,
+            scale_one.reshape(ranks * tokens, 128),
             gains,
             weights,
             out_part,
@@ -1165,7 +1157,6 @@
             pltpu.VMEM((n_expert,) + w_block, BF16),
             pltpu.VMEM((sum_rows, shard), BF16),
             pltpu.VMEM((ranks, tokens, shard), F32),
-            pltpu.VMEM((ranks * tokens, shard), BF16),
         ]
         + line_sems(*group[1:])
         + exchange_sems(ranks)
@@ -1176,15 +1167,15 @@
         + summed(o_block)
         + line_sems(*group[1:]) * 2
         + exchange_sems(ranks)
-        + summed(s_block)
-        + summed(w_block),
-        cid=4,
+        + summed(w_block)
+        + summed(s_block),
+        cid=2,
         us=130,
         in_specs=[VMEM] * 13 + [ANY] * 3,
         out_specs=[VMEM] * 5 + [ANY] * 3,
     )
 
-    held = pl.Buffered(2 if ranks * rows <= 1024 else 1)
+    held = pl.Buffered(deep)
     gathered = lambda shape, at: pl.BlockSpec(
         (ranks, 1) + shape, lambda s: (0, at(s)) + (0,) * len(shape), pipeline_mode=held
     )
@@ -1209,13 +1200,13 @@
         functools.partial(finish, ranks, n_expert, slots, early, heads, tokens),
         "finish",
         outs,
-        (norm_all, og_all, norm_slices, og_slices, meta_group, grad_both, both_all, both_late, inner, inner_all) + ins,
+        (og_all, norm_slices, og_slices, meta_group, grad_both, both_all, both_late, inner, inner_all) + ins,
         [pltpu.VMEM((ranks, n_expert, slots * SLOT_ROWS, shard), BF16)] * 2
         + [pltpu.VMEM((2, n_expert, tokens, shard), BF16)] * 2
         + [pltpu.SemaphoreType.DMA((2, 2))],
         us=20,
         grid=(slots,),
-        in_specs=[ANY] * 4
+        in_specs=[ANY] * 3
         + [
             fixed(meta_group.shape),
             moving((rows, double)),

time: 429 us -> 371 us (0.86)
  Pallas kernels: 423 us -> 366 us
    pallas_call x10 -> x4, Pallas kernels: 423 us -> 366 us  [call(): pl.pallas_call(body, out_shape=[jax.ShapeDtypeStruct(shape, dtype) for sh...]
where the time goes in v4:
time: 371 us
  Pallas kernels  366 us (99%)
    pallas_call x4, Pallas kernels, call(): pl.pallas_call(body, out_shape=[jax.ShapeDtypeStruct(shape, dtype) for sh...  366 us

profile of v4, /device:TPU:0, one launch (start us, length us, event | category | flops | bytes accessed | tf_op | source)
XLA Modules:
  0.0 370.9 jit_solution(5422143355032657464)
XLA Ops:
  0.6 0.7 stack.9
  1.3 0.7 stack.10
  2.0 0.6 maximum_convert_fusion.refs_5_.refs_10_
  2.6 64.3 %forward.1 = (bf16[4,384,640]{2,1,0:T(8,128)(2,1)}, f32[4,16,384]{2,1,0:T(8,128)}, bf16[8,4,128,384]{3,2,1,0:T(8,128)(2,1)}, bf16[4,128,640]{2,1,0:T(8,128)(2,1)...) custom-call(bf16[128,1536]{1,0:T(8,128)(2,1)} %x_ref.1, ...), custom_call_target="tpu_custom_call" | custom-call | bytes 210000000 | tf_op jit(solution)/shard_map/forward/pallas_call | solution.py:368
  66.9 126.3 %mixture_of_experts.1 = (bf16[8,128,1536]{2,1,0:T(8,128)(2,1)}, bf16[5,256,512]{2,1,0:T(8,128)(2,1)}, bf16[5,256,1024]{2,1,0:T(8,128)(2,1)}, f32[128,1536]{1,0:T...) custom-call(bf16[4,128,384]{2,1,0:T(8,128)(2,1)} %get-tuple-element., ...), custom_call_target="tpu_custom_call" | custom-call | bytes 345000000 | tf_op jit(solution)/shard_map/mixture_of_experts/pallas_call | solution.py:368
  193.2 144.6 %backward.1 = (f32[128,1536]{1,0:T(8,128)}, f32[4,128,384]{2,1,0:T(8,128)}, bf16[8,48,1536]{2,1,0:T(8,128)(2,1)}, bf16[8,48,2560]{2,1,0:T(8,128)(2,1)}, bf16[8,1...) custom-call(bf16[128,1536]{1,0:T(8,128)(2,1)} %get-tuple-element.61., ...), custom_call_target="tpu_custom_call" | custom-call | bytes 390000000 | tf_op jit(solution)/shard_map/backward/pallas_call | solution.py:368
  337.9 30.4 %finish.1 = (f32[5,384,1024]{2,1,0:T(8,128)}, f32[5,512,384]{2,1,0:T(8,128)}, bf16[128,1536]{1,0:T(8,128)(2,1)}, f32[128,1536]{1,0:T(8,128)}, f32[384,1536]{1,0:...) custom-call(bf16[8,4,128,384]{3,2,1,0:T(8,128)(2,1)} %get-tuple-elem, ...), custom_call_target="tpu_custom_call" | custom-call | bytes 60000000 | tf_op jit(solution)/shard_map/finish/pallas_call | solution.py:368
  368.3 1.3 reduce
  369.6 1.3 reduce.1

commit v5 on v4

--- a/solution.py
+++ b/solution.py
@@ -301,13 +301,86 @@
                 along(way, k).wait_send()
 
 
-def reduce_gather(g, part, out, kept, sems, slots):
-    def finish(total):
-        kept[...] = total.astype(kept.dtype)
-
-    yield from reduce(g, part, finish, sems[:4], slots)
-    out[g.me] = kept[...]
-    yield from gather(g, kept, out, sems[4:])
+def total_sems(A, B):
+    dma = pltpu.SemaphoreType.DMA
+    return [dma((2, A, B)), dma((2, A)), dma((2, A)), dma((2, A, B))]
+
+
+def total_slots(A, B, block, dtype=BF16):
+    return [
+        pltpu.VMEM(block, dtype),
+        pltpu.VMEM((A, B - 1) + block, dtype),
+        pltpu.VMEM((A - 1,) + block, dtype),
+        pltpu.VMEM((A - 1,) + block, dtype),
+    ]
+
+
+def total(g, part, out, sems, slots):
+    first, second, third, fourth = sems
+    kept, land_b, out_a, land_a = slots
+    A, B = g.A, g.B
+    here = g.here()
+    row = lambda k: (g.a + k) % A
+    col = lambda r: (g.b + r) % B
+
+    def terms(a, r):
+        return remote(part(g.at(a, col(r))), land_b.at[a, r - 1], first.at[0, a, r], first.at[1, a, r], g.dev(g.a, col(r)))
+
+    def sums(k):
+        return remote(out_a.at[k - 1], land_a.at[k - 1], second.at[0, k], second.at[1, k], g.dev(row(k), g.b))
+
+    def rows(k):
+        return remote(kept, out(g.me), third.at[0, k], third.at[1, k], g.dev(row(k), g.b))
+
+    def cols(a, r, src):
+        return remote(src, out(g.at(a, g.b)), fourth.at[0, a, r], fourth.at[1, a, r], g.dev(g.a, col(r)))
+
+    def near(a):
+        value = part(g.at(a, g.b))[...].astype(F32)
+        for r in range(1, B):
+            terms(a, r).wait_recv()
+            value = value + land_b[a, r - 1].astype(F32)
+        return value
+
+    for k in [*range(1, A), 0]:
+        for r in range(1, B):
+            terms(row(k), r).start()
+    yield
+    for k in range(1, A):
+        out_a[k - 1] = near(row(k)).astype(BF16)
+        sums(k).start()
+        yield
+    value = near(g.a)
+    for k in range(1, A):
+        sums(k).wait_recv()
+        value = value + land_a[k - 1].astype(F32)
+    kept[...] = value.astype(BF16)
+    out(g.me)[...] = kept[...]
+    for r in range(1, B):
+        cols(g.a, r, kept).start()
+    for k in range(1, A):
+        rows(k).start()
+    yield
+    for k in range(1, A):
+        a = (g.a + A - k) % A
+        mine = out(g.at(a, g.b))
+        remote(mine, mine, third.at[0, k], third.at[1, k], here).wait_recv()
+        for r in range(1, B):
+            cols(a, r, mine).start()
+        yield
+    for k in [0, *range(1, A)]:
+        a = (g.a + A - k) % A
+        for r in range(1, B):
+            mine = out(g.at(a, (g.b + B - r) % B))
+            remote(mine, mine, fourth.at[0, a, r], fourth.at[1, a, r], here).wait_recv()
+        yield
+    for k in range(A):
+        for r in range(1, B):
+            terms(row(k), r).wait_send()
+            cols(row(k), r, kept).wait_send()
+        if k:
+            sums(k).wait_send()
+            rows(k).wait_send()
 
 
 def exchange_sems(n):
@@ -703,38 +776,22 @@
     sums_ref[used : used + 8, :] = jnp.where(second == 0, small[used:], jnp.where(second == 1, gain_grad, 0.0)).astype(BF16)
 
 
-def finish(ranks, n_expert, slots, early, heads, tokens, og_ref, xd_ref, ogd_ref, meta_ref, own_both_ref, both_ref, late_both_ref, own_inner_ref, inner_ref, grad_ref, x_ref, misc_ref, grad_hidden_ref, hidden_ref, mixture_ref, d_w_ref, d_o_ref, sums_ref, d_up_ref, d_down_ref, output_ref, grad_inputs_ref, q_ref, k_ref, v_ref, o_ref, router_ref, gain_one_ref, gain_two_ref, x_sc, og_sc, x_in, og_in, sems):
+def group_rows(ranks, n_expert, slots, at, x, og, meta_ref, x_rows, og_rows):
+    def one(q, carry):
+        pick = row_picks(slots, meta_ref[at, q, 0])
+        share = jnp.sum(pick * row_shares(slots, meta_ref[at, q, 1]), axis=1, keepdims=True)
+        pick = pick.astype(BF16)
+        x_rows[at, q] = dot(pick, x[q]).astype(BF16)
+        og_rows[at, q] = (share * (RESIDUAL_SCALE * dot(pick, og[q]))).astype(BF16)
+        return carry
+
+    lax.fori_loop(0, n_expert, one, 0)
+
+
+def finish(ranks, n_expert, slots, early, heads, tokens, x_rows_ref, og_rows_ref, both_ref, late_both_ref, inner_ref, grad_ref, x_ref, misc_ref, grad_hidden_ref, hidden_ref, mixture_ref, d_w_ref, d_o_ref, sums_ref, d_up_ref, d_down_ref, output_ref, grad_inputs_ref, q_ref, k_ref, v_ref, o_ref, router_ref, gain_one_ref, gain_two_ref):
     step = pl.program_id(0)
-    me = lax.axis_index("dp")
-    rows = n_expert * SLOT_ROWS
-    shard = x_in.shape[3]
 
     @pl.when(step == 0)
-    def _():
-        def fetch(j, do):
-            at, slot = (me + j) % ranks, j % 2
-            og = og_ref.at[:, me] if j == 0 else ogd_ref.at[at]
-            do(pltpu.make_async_copy(xd_ref.at[at], x_in.at[slot], sems.at[0, slot]))
-            do(pltpu.make_async_copy(og, og_in.at[slot], sems.at[1, slot]))
-
-        fetch(0, lambda copy: copy.start())
-        for j in range(ranks):
-            if j + 1 < ranks:
-                fetch(j + 1, lambda copy: copy.start())
-            fetch(j, lambda copy: copy.wait())
-
-            def one(q, carry):
-                at = (me + j) % ranks
-                pick = row_picks(slots, meta_ref[at, q, 0])
-                share = jnp.sum(pick * row_shares(slots, meta_ref[at, q, 1]), axis=1, keepdims=True)
-                pick = pick.astype(BF16)
-                x_sc[j, q] = dot(pick, x_in[j % 2, q]).astype(BF16)
-                og_sc[j, q] = (share * (RESIDUAL_SCALE * dot(pick, og_in[j % 2, q]))).astype(BF16)
-                return carry
-
-            lax.fori_loop(0, n_expert, one, 0)
-
-    @pl.when(step == slots - 1)
     def _():
         output_ref[...] = (hidden_ref[...] + RESIDUAL_SCALE * mixture_ref[...]).astype(BF16)
         gain = gain_row(misc_ref, ranks, 0)
@@ -742,6 +799,12 @@
         x = x_ref[...].astype(F32)
         scale = norm_scale(x)
         grad_inputs_ref[...] = grad_hidden_ref[...] + norm_back(grad, x * scale, scale, gain)
+        used = n_expert * SLOT_STRIDE
+        router_ref[...] = dot(column_picks(n_expert, slots).astype(BF16), sums_ref[:128])
+        ends = sums_ref[used : used + 16, :].astype(F32)
+        gain_two_ref[...] = ends[0]
+        gain_one_ref[...] = ends[1]
+        o_ref[...] = d_o_ref[...].astype(F32)
         first, second = heads.q_cols, heads.q_cols + heads.kv_cols
         for i in range(ranks):
             start = i * heads.cols
@@ -749,35 +812,20 @@
             here = slice(i * heads.kv_cols, (i + 1) * heads.kv_cols)
             k_ref[:, here] = d_w_ref[:, start + first : start + second].astype(F32)
             v_ref[:, here] = d_w_ref[:, start + second : start + second + heads.kv_cols].astype(F32)
-        o_ref[...] = d_o_ref[...].astype(F32)
-        used = n_expert * SLOT_STRIDE
-        router_ref[...] = dot(column_picks(n_expert, slots).astype(BF16), sums_ref[:128])
-        ends = sums_ref[used : used + 16, :].astype(F32)
-        gain_two_ref[...] = ends[0:1]
-        gain_one_ref[...] = ends[1:2]
-
-    place_of = pl.ds(pl.multiple_of(step * SLOT_ROWS, SLOT_ROWS), SLOT_ROWS)
+
+    flat = lambda value: value.reshape(-1, value.shape[-1])
     over = ((0,), (0,))
-
-    def form(their_both):
-        d_up = d_down = None
-        for j in range(ranks):
-            at = (me + j) % ranks
-            x = x_sc[j, :, place_of, :].reshape(rows, shard)
-            og = og_sc[j, :, place_of, :].reshape(rows, shard)
-            up = dot(x, own_both_ref[0] if j == 0 else their_both[at, 0], over)
-            down = dot(own_inner_ref[0] if j == 0 else inner_ref[at, 0], og, over)
-            d_up, d_down = (up, down) if j == 0 else (d_up + up, d_down + down)
-        d_up_ref[0] = d_up
-        d_down_ref[0] = d_down
+    x = flat(x_rows_ref[...])
 
     @pl.when(step < early)
     def _():
-        form(both_ref)
+        d_up_ref[0] = dot(x, flat(both_ref[...]), over)
 
     @pl.when(step >= early)
     def _():
-        form(late_both_ref)
+        d_up_ref[0] = dot(x, flat(late_both_ref[...]), over)
+
+    d_down_ref[0] = dot(flat(inner_ref[...]), flat(og_rows_ref[...]), over)
 
 
 def on_device(
@@ -934,9 +982,9 @@
     def mixture_of_experts(*refs):
         take = taker(refs)
         nh, mt, hid, sc, pb, ms, tb, og_mine, og, up, down = take(11)
-        out_part, inr, gb, grad_hidden_ref, branch_ref, small_ref, mt_group, xd, gb_all = take(9)
+        out_part, inr, gb, grad_hidden_ref, branch_ref, small_ref, mt_group, xd, ogd, gb_all = take(10)
         nh_all, mt_all, gg, gg_all, back_part, mt_own, x_sc, og_sc, og_in, up_in, down_in = take(11)
-        og_sems, up_sems, own_sems = take(3)
+        og_sems, up_sems, own_sems, own_sem = take(4)
         dp, ex = Grid(*group), Grid(*plane)
         mine = pl.ds(pl.multiple_of(ex.me * SLOT_STRIDE, SLOT_STRIDE), SLOT_STRIDE)
         nh_all[ex.me] = nh[...]
@@ -951,6 +999,9 @@
             fetch(s, lambda copy: copy.start())
         greet(dp.all() + ex.all())
         mts = begin(gather(ex, mt, mt_all, take(4)))
+        og_passed, og_end = pass_slices(dp, ogd, take(2))
+        for i in range(n_expert):
+            og_passed(i, og.at[i])
         passed, end = pass_slices(dp, xd, take(2))
 
         def keep(i, block):
@@ -998,7 +1049,10 @@
 
         lax.fori_loop(0, slots, one, 0)
         run(mgs)
-        gbs = begin(gather(dp, gb.at[pl.ds(0, early)], gb_all, take(4)))
+        gb_early = gb.at[pl.ds(0, early)]
+        keep_gb = pltpu.make_async_copy(gb_early, gb_all.at[dp.me], own_sem)
+        keep_gb.start()
+        gbs = begin(gather(dp, gb_early, gb_all, take(4)))
         sum_rows_back(slots, n_expert, mine, mt_all, out_part, back_part, og_sc, x_sc)
 
         def store(total):
@@ -1009,11 +1063,13 @@
         run(ggs)
         route_backward(ranks, n_expert, shard, hid, nh, sc, pb, ms, tb, og_mine, grad_hidden_ref, gg_all, grad_hidden_ref, branch_ref, small_ref)
         run(gbs)
+        keep_gb.wait()
         end(range(n_expert), nh)
+        og_end(range(n_expert), og.at[0])
         for i in range(n_expert):
             keep(i, nh).wait()
 
-    out_part, inner, grad_both, grad_hidden, grad_branch, small, meta_group, norm_slices, both_all = call(
+    out_part, inner, grad_both, grad_hidden, grad_branch, small, meta_group, norm_slices, og_slices, both_all = call(
         mixture_of_experts,
         "mixture_of_experts",
         [
@@ -1024,6 +1080,7 @@
             ((tokens, width), BF16),
             ((ranks, used + 8, shard), F32),
             ((ranks, n_expert, 2, SLOT_STRIDE, tokens), F32),
+            ((ranks, n_expert, tokens, shard), BF16),
             ((ranks, n_expert, tokens, shard), BF16),
             ((ranks, early, rows, double), BF16),
         ],
@@ -1055,9 +1112,10 @@
             dma((2,)),
             dma((2, deep)),
             dma((n_expert,)),
+            dma(()),
         ]
         + line_sems(*plane[1:])
-        + [dma((n_expert, ranks))] * 2
+        + [dma((n_expert, ranks))] * 4
         + line_sems(*plane[1:])
         + line_sems(*group[1:]) * 2
         + exchange_sems(n_expert)
@@ -1066,58 +1124,81 @@
         cid=1,
         us=115,
         in_specs=[VMEM] * 8 + [ANY] * 3,
-        out_specs=[VMEM] * 7 + [ANY] * 2,
+        out_specs=[VMEM] * 7 + [ANY] * 3,
     )
 
     sum_rows = 16 * n_expert
     part_rows = shard // n_expert
     o_block, w_block, s_block = (part_rows, width), (part_rows, ranks * heads.cols), (16, shard)
 
+    halves_of = ranks * heads.cols // 2
+    summed = lambda block: total_sems(*plane[1:]) + total_slots(*plane[1:], block)
+
     def backward(*refs):
         take = taker(refs)
-        br, sm, at, qkv, wo, ms, cs, sn, xc, sc, gn, w, terms, og, gb, inr = take(16)
-        mix, gx_all, do_all, dw_all, su_all, ogd, gb_all, inr_all = take(8)
-        br_all, sm_all, gr, gr_all, do, dw, su, gx = take(8)
+        br, sm, at, qkv, wo, ms, cs, sn, xc, sc, gn, w, terms, mt, og, xd, ogd, gb, inr = take(19)
+        mix, gx_all, do_all, dw_all, su_all, x_rows, og_rows, gb_all, inr_all = take(9)
+        br_all, sm_all, gr, gr_all, do, dw, su, gx, x_in, og_in, in_sems, own_sems = take(12)
         dp, ex = Grid(*group), Grid(*plane)
+
+        def fetch(j, do_):
+            p, slot = (dp.me + j) % ranks, j % 2
+            do_(pltpu.make_async_copy(xd.at[p], x_in.at[slot], in_sems.at[0, slot]))
+            do_(pltpu.make_async_copy(og.at[:, dp.me] if j == 0 else ogd.at[p], og_in.at[slot], in_sems.at[1, slot]))
+
+        fetch(0, lambda copy: copy.start())
+        keeps = [
+            pltpu.make_async_copy(inr, inr_all.at[dp.me], own_sems.at[0]),
+            pltpu.make_async_copy(gb.at[pl.ds(early, slots - early)], gb_all.at[dp.me], own_sems.at[1]),
+        ]
+        for copy in keeps:
+            copy.start()
         br_all[dp.me] = br[...]
-        greet(dp.all() + ex.near())
-
-        def store(total):
-            mix[...] = total
+        greet(dp.all() + ex.all())
+
+        def store(value):
+            mix[...] = value
 
         brs = begin(gather(dp, br, br_all, take(4)))
         sms = begin(exchange(dp, sm, sm_all, take(2)))
         outs = begin(reduce(ex, lambda i: terms.at[i], store, take(4), take(3)))
+        for j in range(ranks):
+            if j + 1 < ranks:
+                fetch(j + 1, lambda copy: copy.start())
+            fetch(j, lambda copy: copy.wait())
+            group_rows(ranks, n_expert, slots, (dp.me + j) % ranks, x_in.at[j % 2], og_in.at[j % 2], mt, x_rows, og_rows)
         run(brs)
-        passed, end = pass_slices(dp, ogd, take(2))
-        for i in range(n_expert // 3):
-            passed(i, og.at[i])
+        inrs = begin(gather(dp, inr, inr_all, take(4)))
         advance(outs, 2)
         attention_backward(ranks, heads, tokens, br_all, at, qkv, wo, ms, cs, sn, gr, do)
         gr_all[dp.me] = gr[...]
         grs = begin(gather(dp, gr, gr_all, take(4)))
-        dos = begin(reduce_gather(ex, lambda i: do.at[i], do_all, take(), take(8), take(3)))
+        dos = begin(total(ex, lambda i: do.at[i], lambda i: do_all.at[i], take(4), take(4)))
         advance(outs, 2)
         run(sms)
         run(grs)
-        for i in range(n_expert // 3, n_expert):
-            passed(i, og.at[i])
-        inrs = begin(gather(dp, inr, inr_all, take(4)))
         gbs = begin(gather(dp, gb.at[pl.ds(early, slots - early)], gb_all, take(4)))
         advance(outs, 2)
         projection_backward(ranks, heads, shard, xc, sc, gn, gr_all, w, sm_all, gx, dw, su)
         gxs = begin(exchange(dp, gx, gx_all, take(2)))
-        dws = begin(reduce_gather(ex, lambda i: dw.at[i], dw_all, take(), take(8), take(3)))
-        sus = begin(reduce_gather(ex, lambda i: su.at[pl.ds(pl.multiple_of(i * 16, 16), 16)], su_all, take(), take(8), take(3)))
+        dws = []
+        for i in range(2):
+            cols = pl.ds(i * halves_of, halves_of)
+            block = lambda ref, cols=cols: lambda i: ref.at[i, :, cols]
+            dws.append(begin(total(ex, block(dw), block(dw_all), take(4), take(4))))
+        rows_of = lambda i: pl.ds(pl.multiple_of(i * 16, 16), 16)
+        sus = begin(total(ex, lambda i: su.at[rows_of(i)], lambda i: su_all.at[i], take(4), take(4)))
         run(outs)
-        run(dos, dws, sus)
+        run(dos)
+        run(*dws, sus)
         run(gxs)
         run(inrs)
         run(gbs)
-        end(range(n_expert), og.at[0])
-
-    summed = lambda block: [pltpu.VMEM(block, BF16)] + line_sems(*plane[1:]) * 2 + sum_slots(*plane[1:], block)
-    mixture, grad_x, d_o, d_w, sums, og_slices, both_late, inner_all = call(
+        for copy in keeps:
+            copy.wait()
+
+    row_block = (n_expert, slots * SLOT_ROWS, shard)
+    mixture, grad_x, d_o, d_w, sums, x_rows, og_rows, both_late, inner_all = call(
         backward,
         "backward",
         [
@@ -1126,7 +1207,8 @@
             ((n_expert,) + o_block, BF16),
             ((n_expert,) + w_block, BF16),
             ((n_expert,) + s_block, BF16),
-            ((ranks, n_expert, tokens, shard), BF16),
+            ((ranks,) + row_block, BF16),
+            ((ranks,) + row_block, BF16),
             ((ranks, slots - early, rows, double), BF16),
             ((ranks, slots, rows, hidden), BF16),
         ],
@@ -1144,7 +1226,10 @@
             gains,
             weights,
             out_part,
+            meta_group,
             og_all,
+            norm_slices,
+            og_slices,
             grad_both,
             inner,
         ),
@@ -1157,22 +1242,25 @@
             pltpu.VMEM((n_expert,) + w_block, BF16),
             pltpu.VMEM((sum_rows, shard), BF16),
             pltpu.VMEM((ranks, tokens, shard), F32),
+            pltpu.VMEM((2, n_expert, tokens, shard), BF16),
+            pltpu.VMEM((2, n_expert, tokens, shard), BF16),
+            dma((2, 2)),
+            dma((2,)),
         ]
         + line_sems(*group[1:])
         + exchange_sems(ranks)
         + line_sems(*plane[1:])
         + sum_slots(*plane[1:], (tokens, width))
-        + [pltpu.SemaphoreType.DMA((n_expert, ranks))] * 2
+        + line_sems(*group[1:]) * 2
+        + summed(o_block)
         + line_sems(*group[1:])
-        + summed(o_block)
-        + line_sems(*group[1:]) * 2
         + exchange_sems(ranks)
-        + summed(w_block)
+        + summed((part_rows, halves_of)) * 2
         + summed(s_block),
         cid=2,
-        us=130,
-        in_specs=[VMEM] * 13 + [ANY] * 3,
-        out_specs=[VMEM] * 5 + [ANY] * 3,
+        us=125,
+        in_specs=[VMEM] * 14 + [ANY] * 5,
+        out_specs=[VMEM] * 7 + [ANY] * 2,
     )
 
     held = pl.Buffered(deep)
@@ -1193,26 +1281,21 @@
         ((shard, KEY_VALUE_HEADS * HEAD_DIMENSION), F32),
         ((shard, width), F32),
         ((router_weight.shape[1], shard), F32),
-        ((1, shard), F32),
-        ((1, shard), F32),
+        ((shard,), F32),
+        ((shard,), F32),
     ]
     d_up, d_down, output, grad_inputs, d_q, d_k, d_v, d_o, d_router, gain_one, gain_two = call(
         functools.partial(finish, ranks, n_expert, slots, early, heads, tokens),
         "finish",
         outs,
-        (og_all, norm_slices, og_slices, meta_group, grad_both, both_all, both_late, inner, inner_all) + ins,
-        [pltpu.VMEM((ranks, n_expert, slots * SLOT_ROWS, shard), BF16)] * 2
-        + [pltpu.VMEM((2, n_expert, tokens, shard), BF16)] * 2
-        + [pltpu.SemaphoreType.DMA((2, 2))],
-        us=20,
+        (x_rows, og_rows, both_all, both_late, inner_all) + ins,
+        us=15,
         grid=(slots,),
-        in_specs=[ANY] * 3
-        + [
-            fixed(meta_group.shape),
-            moving((rows, double)),
+        in_specs=[
+            pl.BlockSpec((ranks, n_expert, SLOT_ROWS, shard), lambda s: (0, 0, s, 0)),
+            pl.BlockSpec((ranks, n_expert, SLOT_ROWS, shard), lambda s: (0, 0, s, 0)),
             gathered((rows, double), lambda s: jnp.minimum(s, early - 1)),
             gathered((rows, double), lambda s: jnp.maximum(s - early, 0)),
-            moving((rows, hidden)),
             gathered((rows, hidden), lambda s: s),
         ]
         + [fixed(array.shape) for array in ins],
@@ -1221,12 +1304,12 @@
     return (
         output,
         grad_inputs,
-        gain_one.reshape(shard),
+        gain_one,
         d_q,
         d_k,
         d_v,
         d_o,
-        gain_two.reshape(shard),
+        gain_two,
         d_router.T,
         d_up,
         d_down,

time: 371 us -> 398 us (1.073)
  Pallas kernels: 366 us -> 395 us
    pallas_call x4, Pallas kernels: 366 us -> 395 us  [call(): pl.pallas_call(body, out_shape=[jax.ShapeDtypeStruct(shape, dtype) for sh...]
where the time goes in v5:
time: 398 us
  Pallas kernels  395 us (99%)
    pallas_call x4, Pallas kernels, call(): pl.pallas_call(body, out_shape=[jax.ShapeDtypeStruct(shape, dtype) for sh...  395 us

profile of v5, /device:TPU:0, one launch (start us, length us, event | category | flops | bytes accessed | tf_op | source)
XLA Modules:
  0.0 397.6 jit_solution(4229322324196126985)
XLA Ops:
  0.6 0.7 stack.9
  1.3 0.7 stack.10
  2.0 0.6 maximum_convert_fusion.refs_5_.refs_10_
  2.6 64.4 %forward.1 = (bf16[4,384,640]{2,1,0:T(8,128)(2,1)}, f32[4,16,384]{2,1,0:T(8,128)}, bf16[8,4,128,384]{3,2,1,0:T(8,128)(2,1)}, bf16[4,128,640]{2,1,0:T(8,128)(2,1)...) custom-call(bf16[128,1536]{1,0:T(8,128)(2,1)} %x_ref.1, ...), custom_call_target="tpu_custom_call" | custom-call | bytes 210000000 | tf_op jit(solution)/shard_map/forward/pallas_call | solution.py:441
  67.0 127.8 %mixture_of_experts.1 = (bf16[8,128,1536]{2,1,0:T(8,128)(2,1)}, bf16[5,256,512]{2,1,0:T(8,128)(2,1)}, bf16[5,256,1024]{2,1,0:T(8,128)(2,1)}, f32[128,1536]{1,0:T...) custom-call(bf16[4,128,384]{2,1,0:T(8,128)(2,1)} %get-tuple-element., ...), custom_call_target="tpu_custom_call" | custom-call | bytes 345000000 | tf_op jit(solution)/shard_map/mixture_of_experts/pallas_call | solution.py:441
  194.7 180.9 %backward.1 = (f32[128,1536]{1,0:T(8,128)}, f32[4,128,384]{2,1,0:T(8,128)}, bf16[8,48,1536]{2,1,0:T(8,128)(2,1)}, bf16[8,48,2560]{2,1,0:T(8,128)(2,1)}, bf16[8,1...) custom-call(bf16[128,1536]{1,0:T(8,128)(2,1)} %get-tuple-element.62., ...), custom_call_target="tpu_custom_call" | custom-call | bytes 375000000 | tf_op jit(solution)/shard_map/backward/pallas_call | solution.py:441
  375.6 21.8 %finish.1 = (f32[5,384,1024]{2,1,0:T(8,128)}, f32[5,512,384]{2,1,0:T(8,128)}, bf16[128,1536]{1,0:T(8,128)(2,1)}, f32[128,1536]{1,0:T(8,128)}, f32[384,1536]{1,0:...) custom-call(bf16[4,8,160,384]{3,2,1,0:T(8,128)(2,1)} %get-tuple-elem, ...), custom_call_target="tpu_custom_call" | custom-call | bytes 45000000 | tf_op jit(solution)/shard_map/finish/pallas_call | solution.py:441

commit v6 on v5

--- a/solution.py
+++ b/solution.py
@@ -98,6 +98,25 @@
         return self.ref.at[(i,) + self.rest]
 
 
+class Ring:
+    def __init__(self, stage, out, sems):
+        self.stage, self.out, self.sems = stage, out, sems
+
+    def copy(self, i):
+        return pltpu.make_async_copy(self.stage.at[i % 2], self.out.at[i], self.sems.at[i % 2])
+
+    def free(self, i):
+        @pl.when(i >= 2)
+        def _():
+            self.copy(i - 2).wait()
+
+        return self.stage.at[i % 2]
+
+    def end(self, count):
+        for i in range(max(count - 2, 0), count):
+            self.copy(i).wait()
+
+
 def begin(step):
     next(step)
     return step
@@ -106,6 +125,20 @@
 def advance(step, count):
     for _ in range(count):
         next(step)
+
+
+def run_behind(*steps):
+    steps, turn = list(steps), 0
+    while steps:
+        left = []
+        for lag, step in steps:
+            try:
+                if turn >= lag:
+                    next(step)
+                left.append((lag, step))
+            except StopIteration:
+                pass
+        steps, turn = left, turn + 1
 
 
 def run(*steps):
@@ -213,9 +246,10 @@
     ]
 
 
-def reduce(g, part, finish, sems, slots):
+def reduce(g, part, finish, sems, slots, sent=None):
     send_a, recv_a, send_b, recv_b = sems
     land_a, out_a, land_b = slots
+    sent = sent or part
     A, B = g.A, g.B
     row = lambda way, k: g.a + k if way == 0 else g.a - k
     rows = [(way, k) for k in range(A - 1, 0, -1) for way in (0, 1)] + [(0, 0)]
@@ -223,7 +257,7 @@
 
     def across(a, r):
         to = (g.b + r) % B
-        return remote(part(g.at(a, to)), land_b.at[a, r - 1], send_b.at[0, a, r], recv_b.at[0, a, r], g.dev(g.a, to))
+        return remote(sent(g.at(a, to)), land_b.at[a, r - 1], send_b.at[0, a, r], recv_b.at[0, a, r], g.dev(g.a, to))
 
     def landing(way, k):
         return land_a.at[A if k == 0 and way == 1 else row(way, k)]
@@ -301,86 +335,19 @@
                 along(way, k).wait_send()
 
 
-def total_sems(A, B):
-    dma = pltpu.SemaphoreType.DMA
-    return [dma((2, A, B)), dma((2, A)), dma((2, A)), dma((2, A, B))]
-
-
-def total_slots(A, B, block, dtype=BF16):
-    return [
-        pltpu.VMEM(block, dtype),
-        pltpu.VMEM((A, B - 1) + block, dtype),
-        pltpu.VMEM((A - 1,) + block, dtype),
-        pltpu.VMEM((A - 1,) + block, dtype),
-    ]
-
-
-def total(g, part, out, sems, slots):
-    first, second, third, fourth = sems
-    kept, land_b, out_a, land_a = slots
-    A, B = g.A, g.B
-    here = g.here()
-    row = lambda k: (g.a + k) % A
-    col = lambda r: (g.b + r) % B
-
-    def terms(a, r):
-        return remote(part(g.at(a, col(r))), land_b.at[a, r - 1], first.at[0, a, r], first.at[1, a, r], g.dev(g.a, col(r)))
-
-    def sums(k):
-        return remote(out_a.at[k - 1], land_a.at[k - 1], second.at[0, k], second.at[1, k], g.dev(row(k), g.b))
-
-    def rows(k):
-        return remote(kept, out(g.me), third.at[0, k], third.at[1, k], g.dev(row(k), g.b))
-
-    def cols(a, r, src):
-        return remote(src, out(g.at(a, g.b)), fourth.at[0, a, r], fourth.at[1, a, r], g.dev(g.a, col(r)))
-
-    def near(a):
-        value = part(g.at(a, g.b))[...].astype(F32)
-        for r in range(1, B):
-            terms(a, r).wait_recv()
-            value = value + land_b[a, r - 1].astype(F32)
-        return value
-
-    for k in [*range(1, A), 0]:
-        for r in range(1, B):
-            terms(row(k), r).start()
-    yield
-    for k in range(1, A):
-        out_a[k - 1] = near(row(k)).astype(BF16)
-        sums(k).start()
-        yield
-    value = near(g.a)
-    for k in range(1, A):
-        sums(k).wait_recv()
-        value = value + land_a[k - 1].astype(F32)
-    kept[...] = value.astype(BF16)
-    out(g.me)[...] = kept[...]
-    for r in range(1, B):
-        cols(g.a, r, kept).start()
-    for k in range(1, A):
-        rows(k).start()
-    yield
-    for k in range(1, A):
-        a = (g.a + A - k) % A
-        mine = out(g.at(a, g.b))
-        remote(mine, mine, third.at[0, k], third.at[1, k], here).wait_recv()
-        for r in range(1, B):
-            cols(a, r, mine).start()
-        yield
-    for k in [0, *range(1, A)]:
-        a = (g.a + A - k) % A
-        for r in range(1, B):
-            mine = out(g.at(a, (g.b + B - r) % B))
-            remote(mine, mine, fourth.at[0, a, r], fourth.at[1, a, r], here).wait_recv()
-        yield
-    for k in range(A):
-        for r in range(1, B):
-            terms(row(k), r).wait_send()
-            cols(row(k), r, kept).wait_send()
-        if k:
-            sums(k).wait_send()
-            rows(k).wait_send()
+def total_scratch(A, B, block):
+    return [pltpu.VMEM(block, BF16)] + line_sems(A, B) * 2 + sum_slots(A, B, block)
+
+
+def total(g, part, out, take):
+    kept, sems, slots = take(), take(8), take(3)
+
+    def finish(value):
+        kept[...] = value.astype(kept.dtype)
+
+    yield from reduce(g, part, finish, sems[:4], slots)
+    out.at[g.me][...] = kept[...]
+    yield from gather(g, kept, out, sems[4:])
 
 
 def exchange_sems(n):
@@ -644,7 +611,7 @@
     lax.fori_loop(0, n_expert, one, 0)
 
 
-def expert_slot(n_expert, tokens, s, mine, meta_ref, up_ref, down_ref, gate_grad_ref, inner_ref, both_ref, x_sc, og_sc):
+def expert_slot(n_expert, tokens, s, mine, meta_ref, up_ref, down_ref, gate_grad_ref, inner_ring, both_ring, x_sc, og_sc):
     width = x_sc.shape[2]
     hidden = down_ref.shape[0]
     place_of = pl.ds(pl.multiple_of(s * SLOT_ROWS, SLOT_ROWS), SLOT_ROWS)
@@ -655,7 +622,8 @@
     gate, up = both[:, :hidden], both[:, hidden:]
     squash = jax.nn.sigmoid(gate)
     inner = (gate * squash * up).astype(BF16)
-    inner_ref[s] = inner
+    inner_ring.free(s)[...] = inner
+    inner_ring.copy(s).start()
     produced = dot(inner, down_ref[...]).astype(BF16)
     masks, gates = [], []
     for q in range(n_expert):
@@ -674,17 +642,20 @@
     grad_both = jnp.concatenate(
         [grad_inner * up * squash * (1.0 + gate * (1.0 - squash)), grad_inner * (gate * squash)], axis=1
     ).astype(BF16)
-    both_ref[s] = grad_both
+    both_ring.free(s)[...] = grad_both
+    both_ring.copy(s).start()
     x_sc[:, place_of, :] = dot(grad_both, up_ref[...], ((1,), (1,))).astype(BF16).reshape(n_expert, SLOT_ROWS, width)
 
 
-def sum_rows_back(slots, n_expert, mine, meta_ref, out_ref, back_ref, eo_sc, gx_sc):
+def sum_rows_back(slots, n_expert, mine, meta_ref, out_ring, back_ring, eo_sc, gx_sc):
     def one(q, carry):
         pick = row_picks(slots, meta_ref[q, 0, mine, :])
         high, low = halves(pick * row_shares(slots, meta_ref[q, 1, mine, :]))
         over = ((0,), (0,))
-        back_ref[q] = dot(pick.astype(BF16), gx_sc[q], over).astype(BF16)
-        out_ref[q] = (dot(high, eo_sc[q], over) + dot(low, eo_sc[q], over)).astype(BF16)
+        back_ring.free(q)[...] = dot(pick.astype(BF16), gx_sc[q], over).astype(BF16)
+        back_ring.copy(q).start()
+        out_ring.free(q)[...] = (dot(high, eo_sc[q], over) + dot(low, eo_sc[q], over)).astype(BF16)
+        out_ring.copy(q).start()
         return carry
 
     lax.fori_loop(0, n_expert, one, 0)
@@ -715,8 +686,8 @@
     for i in range(ranks):
         here = slice(i * shard, (i + 1) * shard)
         grad_router = dot(high, norm_ref[i], over) + dot(low, norm_ref[i], over)
-        small_ref[i, :used, :] = grad_router[:used]
-        small_ref[i, used:, :] = jnp.broadcast_to(grad_gain[:, here], (8, shard))
+        small_ref[i, :used, :] = grad_router[:used].astype(BF16)
+        small_ref[i, used:, :] = jnp.broadcast_to(grad_gain[:, here], (16, shard)).astype(BF16)
 
 
 def store_blocks(ref, cols, values):
@@ -765,30 +736,30 @@
         total = term if total is None else total + term
         store_blocks(d_w_ref, slice(i * heads.cols, (i + 1) * heads.cols), dot(norm_input, grads, ((0,), (0,))).astype(BF16))
     grad_x_ref[...] = total.reshape(grad_x_ref.shape)
-    small = small_ref[0]
+    small = small_ref[0].astype(F32)
     for i in range(1, ranks):
-        small = small + small_ref[i]
+        small = small + small_ref[i].astype(F32)
     gain_grad = jnp.sum(total * normed, axis=0, keepdims=True)
-    used = small.shape[0] - 8
+    used = small.shape[0] - 16
     sums_ref[...] = jnp.zeros_like(sums_ref)
     sums_ref[:used, :] = small[:used].astype(BF16)
-    second = lax.broadcasted_iota(jnp.int32, (8, shard), 0)
-    sums_ref[used : used + 8, :] = jnp.where(second == 0, small[used:], jnp.where(second == 1, gain_grad, 0.0)).astype(BF16)
-
-
-def group_rows(ranks, n_expert, slots, at, x, og, meta_ref, x_rows, og_rows):
+    second = lax.broadcasted_iota(jnp.int32, (16, shard), 0)
+    sums_ref[used : used + 16, :] = jnp.where(second == 0, small[used:], jnp.where(second == 1, gain_grad, 0.0)).astype(BF16)
+
+
+def group_rows(n_expert, slots, at, x, og, meta_ref, x_rows, og_rows):
     def one(q, carry):
         pick = row_picks(slots, meta_ref[at, q, 0])
         share = jnp.sum(pick * row_shares(slots, meta_ref[at, q, 1]), axis=1, keepdims=True)
         pick = pick.astype(BF16)
-        x_rows[at, q] = dot(pick, x[q]).astype(BF16)
-        og_rows[at, q] = (share * (RESIDUAL_SCALE * dot(pick, og[q]))).astype(BF16)
+        x_rows[q] = dot(pick, x[q]).astype(BF16)
+        og_rows[q] = (share * (RESIDUAL_SCALE * dot(pick, og[q]))).astype(BF16)
         return carry
 
     lax.fori_loop(0, n_expert, one, 0)
 
 
-def finish(ranks, n_expert, slots, early, heads, tokens, x_rows_ref, og_rows_ref, both_ref, late_both_ref, inner_ref, grad_ref, x_ref, misc_ref, grad_hidden_ref, hidden_ref, mixture_ref, d_w_ref, d_o_ref, sums_ref, d_up_ref, d_down_ref, output_ref, grad_inputs_ref, q_ref, k_ref, v_ref, o_ref, router_ref, gain_one_ref, gain_two_ref):
+def finish(ranks, n_expert, slots, heads, tokens, x_rows_ref, og_rows_ref, both_ref, inner_ref, grad_ref, x_ref, misc_ref, grad_hidden_ref, hidden_ref, mixture_ref, d_w_ref, d_o_ref, sums_ref, d_up_ref, d_down_ref, output_ref, grad_inputs_ref, q_ref, k_ref, v_ref, o_ref, router_ref, gain_one_ref, gain_two_ref):
     step = pl.program_id(0)
 
     @pl.when(step == 0)
@@ -815,16 +786,7 @@
 
     flat = lambda value: value.reshape(-1, value.shape[-1])
     over = ((0,), (0,))
-    x = flat(x_rows_ref[...])
-
-    @pl.when(step < early)
-    def _():
-        d_up_ref[0] = dot(x, flat(both_ref[...]), over)
-
-    @pl.when(step >= early)
-    def _():
-        d_up_ref[0] = dot(x, flat(late_both_ref[...]), over)
-
+    d_up_ref[0] = dot(flat(x_rows_ref[...]), flat(both_ref[...]), over)
     d_down_ref[0] = dot(flat(inner_ref[...]), flat(og_rows_ref[...]), over)
 
 
@@ -977,15 +939,18 @@
     moving = lambda shape: pl.BlockSpec((1,) + shape, lambda s: (s,) + (0,) * len(shape))
     rows = n_expert * SLOT_ROWS
     deep = 2 if ranks * rows <= 1024 else 1
-    early = slots * 3 // 5
 
     def mixture_of_experts(*refs):
         take = taker(refs)
-        nh, mt, hid, sc, pb, ms, tb, og_mine, og, up, down = take(11)
-        out_part, inr, gb, grad_hidden_ref, branch_ref, small_ref, mt_group, xd, ogd, gb_all = take(10)
-        nh_all, mt_all, gg, gg_all, back_part, mt_own, x_sc, og_sc, og_in, up_in, down_in = take(11)
-        og_sems, up_sems, own_sems, own_sem = take(4)
+        nh, mt, og, up, down = take(5)
+        gg, mt_group, out_part, back_part, inr, gb, xd, ogd = take(8)
+        nh_all, mt_all, mt_own, x_sc, og_sc, og_in, up_in, down_in = take(8)
+        stages, ring_sems, og_sems, up_sems, own_sems = take(4), take(), take(), take(), take()
         dp, ex = Grid(*group), Grid(*plane)
+        out_ring, back_ring, inner_ring, both_ring = (
+            Ring(stage, out, ring_sems.at[i])
+            for i, (stage, out) in enumerate(zip(stages, (out_part, back_part, inr.at[dp.me], gb.at[dp.me])))
+        )
         mine = pl.ds(pl.multiple_of(ex.me * SLOT_STRIDE, SLOT_STRIDE), SLOT_STRIDE)
         nh_all[ex.me] = nh[...]
         mt_all[ex.me] = mt[...]
@@ -997,7 +962,7 @@
 
         for s in range(deep):
             fetch(s, lambda copy: copy.start())
-        greet(dp.all() + ex.all())
+        greet(dp.all() + ex.near())
         mts = begin(gather(ex, mt, mt_all, take(4)))
         og_passed, og_end = pass_slices(dp, ogd, take(2))
         for i in range(n_expert):
@@ -1039,7 +1004,9 @@
 
         def one(s, carry):
             fetch(s, lambda copy: copy.wait())
-            expert_slot(n_expert, tokens, s, mine, mt_all, up_in.at[s % deep], down_in.at[s % deep], gg, inr, gb, x_sc, og_sc)
+            expert_slot(
+                n_expert, tokens, s, mine, mt_all, up_in.at[s % deep], down_in.at[s % deep], gg, inner_ring, both_ring, x_sc, og_sc
+            )
 
             @pl.when(s + deep < slots)
             def _():
@@ -1049,82 +1016,56 @@
 
         lax.fori_loop(0, slots, one, 0)
         run(mgs)
-        gb_early = gb.at[pl.ds(0, early)]
-        keep_gb = pltpu.make_async_copy(gb_early, gb_all.at[dp.me], own_sem)
-        keep_gb.start()
-        gbs = begin(gather(dp, gb_early, gb_all, take(4)))
-        sum_rows_back(slots, n_expert, mine, mt_all, out_part, back_part, og_sc, x_sc)
-
-        def store(total):
-            grad_hidden_ref[...] = total
-
-        ggs = begin(exchange(ex, gg, gg_all, take(2)))
-        run(reduce(ex, lambda i: back_part.at[i], store, take(4), take(3)))
-        run(ggs)
-        route_backward(ranks, n_expert, shard, hid, nh, sc, pb, ms, tb, og_mine, grad_hidden_ref, gg_all, grad_hidden_ref, branch_ref, small_ref)
-        run(gbs)
-        keep_gb.wait()
+        sum_rows_back(slots, n_expert, mine, mt_all, out_ring, back_ring, og_sc, x_sc)
+        inner_ring.end(slots)
+        both_ring.end(slots)
+        out_ring.end(n_expert)
+        back_ring.end(n_expert)
         end(range(n_expert), nh)
         og_end(range(n_expert), og.at[0])
         for i in range(n_expert):
             keep(i, nh).wait()
 
-    out_part, inner, grad_both, grad_hidden, grad_branch, small, meta_group, norm_slices, og_slices, both_all = call(
+    gate_grad, meta_group, out_part, back_part, inner, grad_both, norm_slices, og_slices = call(
         mixture_of_experts,
         "mixture_of_experts",
         [
+            ((n_expert, SLOT_STRIDE, tokens), F32),
+            ((ranks, n_expert, 2, SLOT_STRIDE, tokens), F32),
             ((n_expert, tokens, width), BF16),
-            ((slots, rows, hidden), BF16),
-            ((slots, rows, double), BF16),
-            ((tokens, width), F32),
-            ((tokens, width), BF16),
-            ((ranks, used + 8, shard), F32),
-            ((ranks, n_expert, 2, SLOT_STRIDE, tokens), F32),
+            ((n_expert, tokens, width), BF16),
+            ((ranks, slots, rows, hidden), BF16),
+            ((ranks, slots, rows, double), BF16),
             ((ranks, n_expert, tokens, shard), BF16),
             ((ranks, n_expert, tokens, shard), BF16),
-            ((ranks, early, rows, double), BF16),
         ],
-        (
-            norm_hidden,
-            meta,
-            hidden_rows,
-            scale_two,
-            probs,
-            misc_all,
-            router,
-            out_grad,
-            og_all,
-            expert_gate_up,
-            expert_down,
-        ),
+        (norm_hidden, meta, og_all, expert_gate_up, expert_down),
         [
             pltpu.VMEM((n_expert, ranks, tokens, shard), BF16),
             pltpu.VMEM((n_expert, 2, used, tokens), F32),
-            pltpu.VMEM((n_expert, SLOT_STRIDE, tokens), F32),
-            pltpu.VMEM((n_expert, SLOT_STRIDE, tokens), F32),
-            pltpu.VMEM((n_expert, tokens, width), BF16),
             pltpu.VMEM((n_expert, 2, SLOT_STRIDE, tokens), F32),
             pltpu.VMEM((n_expert, slots * SLOT_ROWS, width), BF16),
             pltpu.VMEM((n_expert, slots * SLOT_ROWS, width), BF16),
             pltpu.VMEM((2, ranks, tokens, shard), BF16),
             pltpu.VMEM((deep, width, double), BF16),
             pltpu.VMEM((deep, hidden, width), BF16),
+            pltpu.VMEM((2, tokens, width), BF16),
+            pltpu.VMEM((2, tokens, width), BF16),
+            pltpu.VMEM((2, rows, hidden), BF16),
+            pltpu.VMEM((2, rows, double), BF16),
+            dma((4, 2)),
             dma((2,)),
             dma((2, deep)),
             dma((n_expert,)),
-            dma(()),
         ]
         + line_sems(*plane[1:])
         + [dma((n_expert, ranks))] * 4
         + line_sems(*plane[1:])
-        + line_sems(*group[1:]) * 2
-        + exchange_sems(n_expert)
-        + line_sems(*plane[1:])
-        + sum_slots(*plane[1:], (tokens, width)),
+        + line_sems(*group[1:]),
         cid=1,
-        us=115,
-        in_specs=[VMEM] * 8 + [ANY] * 3,
-        out_specs=[VMEM] * 7 + [ANY] * 3,
+        us=80,
+        in_specs=[VMEM] * 2 + [ANY] * 3,
+        out_specs=[VMEM] * 2 + [ANY] * 6,
     )
 
     sum_rows = 16 * n_expert
@@ -1132,76 +1073,117 @@
     o_block, w_block, s_block = (part_rows, width), (part_rows, ranks * heads.cols), (16, shard)
 
     halves_of = ranks * heads.cols // 2
-    summed = lambda block: total_sems(*plane[1:]) + total_slots(*plane[1:], block)
+    summed = lambda block: total_scratch(*plane[1:], block)
+
+    lead = max(slots // 5, 1)
 
     def backward(*refs):
         take = taker(refs)
-        br, sm, at, qkv, wo, ms, cs, sn, xc, sc, gn, w, terms, mt, og, xd, ogd, gb, inr = take(19)
-        mix, gx_all, do_all, dw_all, su_all, x_rows, og_rows, gb_all, inr_all = take(9)
-        br_all, sm_all, gr, gr_all, do, dw, su, gx, x_in, og_in, in_sems, own_sems = take(12)
+        hid, nh, sc2, pb, ms, tb, og_mine, gg, cs, sn, sc, gn, mt = take(13)
+        brought, (og, xd, ogd, _, _, terms, back_terms) = take(5), take(7)
+        grad_hidden_ref, mix, gx_all, do_all, dw_all, su_all, x_rows, og_rows, gb_all, inr_all = take(10)
+        places, bring_sems = take(5), take()
+        wo, qkv, at, xc, w = places
+        out_in, back_in, term_sems = take(3)
+        gg_all, sm, br_all, sm_all, gr_all, do, dw, su, gx, x_in, og_in, x_out, og_out, in_sems, out_sems = take(15)
         dp, ex = Grid(*group), Grid(*plane)
+        brings = [pltpu.make_async_copy(*pair, bring_sems.at[i]) for i, pair in enumerate(zip(brought, places))]
+        holds = [
+            pltpu.make_async_copy(back_terms, back_in, term_sems.at[0]),
+            pltpu.make_async_copy(terms, out_in, term_sems.at[1]),
+        ]
 
         def fetch(j, do_):
-            p, slot = (dp.me + j) % ranks, j % 2
+            p, slot = (dp.me + j) % ranks, j % deep
             do_(pltpu.make_async_copy(xd.at[p], x_in.at[slot], in_sems.at[0, slot]))
             do_(pltpu.make_async_copy(og.at[:, dp.me] if j == 0 else ogd.at[p], og_in.at[slot], in_sems.at[1, slot]))
 
-        fetch(0, lambda copy: copy.start())
-        keeps = [
-            pltpu.make_async_copy(inr, inr_all.at[dp.me], own_sems.at[0]),
-            pltpu.make_async_copy(gb.at[pl.ds(early, slots - early)], gb_all.at[dp.me], own_sems.at[1]),
-        ]
-        for copy in keeps:
+        for copy in holds + brings:
             copy.start()
-        br_all[dp.me] = br[...]
+        for j in range(deep):
+            fetch(j, lambda copy: copy.start())
         greet(dp.all() + ex.all())
 
-        def store(value):
-            mix[...] = value
-
-        brs = begin(gather(dp, br, br_all, take(4)))
+        def store(to):
+            def finish_(value):
+                to[...] = value
+
+            return finish_
+
+        ggs = begin(exchange(ex, gg, gg_all, take(2)))
+        backs = begin(reduce(ex, lambda i: back_in.at[i], store(grad_hidden_ref), take(4), take(3), lambda i: back_terms.at[i]))
+        outs = begin(reduce(ex, lambda i: out_in.at[i], store(mix), take(4), take(3), lambda i: terms.at[i]))
+        inrs = begin(gather(dp, inr_all.at[dp.me], inr_all, take(4)))
+        share = lambda start, count: begin(
+            gather(dp, gb_all.at[dp.me, pl.ds(start, count)], Part(gb_all, pl.ds(start, count)), take(4))
+        )
+        gbs = [share(0, lead)]
+        for copy in holds:
+            copy.wait()
+
+        def out_copies(j):
+            p, slot = (dp.me + j) % ranks, j % deep
+            return [
+                pltpu.make_async_copy(x_out.at[slot], x_rows.at[p], out_sems.at[0, slot]),
+                pltpu.make_async_copy(og_out.at[slot], og_rows.at[p], out_sems.at[1, slot]),
+            ]
+
+        def build(j):
+            fetch(j, lambda copy: copy.wait())
+            if j >= deep:
+                for copy in out_copies(j - deep):
+                    copy.wait()
+            p, slot = (dp.me + j) % ranks, j % deep
+            group_rows(n_expert, slots, p, x_in.at[slot], og_in.at[slot], mt, x_out.at[slot], og_out.at[slot])
+            for copy in out_copies(j):
+                copy.start()
+            if j + deep < ranks:
+                fetch(j + deep, lambda copy: copy.start())
+
+        for j in range(ranks):
+            build(j)
+            if j < 2 * (plane[1] - 1):
+                advance(backs, 1)
+        for j in range(ranks - deep, ranks):
+            for copy in out_copies(j):
+                copy.wait()
+        run(backs)
+        run(ggs)
+        route_backward(ranks, n_expert, shard, hid, nh, sc2, pb, ms, tb, og_mine, grad_hidden_ref, gg_all, grad_hidden_ref, br_all.at[dp.me], sm)
+        brs = begin(gather(dp, br_all.at[dp.me], br_all, take(4)))
         sms = begin(exchange(dp, sm, sm_all, take(2)))
-        outs = begin(reduce(ex, lambda i: terms.at[i], store, take(4), take(3)))
-        for j in range(ranks):
-            if j + 1 < ranks:
-                fetch(j + 1, lambda copy: copy.start())
-            fetch(j, lambda copy: copy.wait())
-            group_rows(ranks, n_expert, slots, (dp.me + j) % ranks, x_in.at[j % 2], og_in.at[j % 2], mt, x_rows, og_rows)
+        for copy in brings:
+            copy.wait()
+        advance(outs, 2)
         run(brs)
-        inrs = begin(gather(dp, inr, inr_all, take(4)))
         advance(outs, 2)
-        attention_backward(ranks, heads, tokens, br_all, at, qkv, wo, ms, cs, sn, gr, do)
-        gr_all[dp.me] = gr[...]
-        grs = begin(gather(dp, gr, gr_all, take(4)))
-        dos = begin(total(ex, lambda i: do.at[i], lambda i: do_all.at[i], take(4), take(4)))
+        attention_backward(ranks, heads, tokens, br_all, at, qkv, wo, ms, cs, sn, gr_all.at[dp.me], do)
+        grs = begin(gather(dp, gr_all.at[dp.me], gr_all, take(4)))
+        dos = begin(total(ex, lambda i: do.at[i], do_all, take))
         advance(outs, 2)
         run(sms)
+        advance(dos, 2 * plane[1])
         run(grs)
-        gbs = begin(gather(dp, gb.at[pl.ds(early, slots - early)], gb_all, take(4)))
-        advance(outs, 2)
+        gbs.append(share(lead, slots - lead))
         projection_backward(ranks, heads, shard, xc, sc, gn, gr_all, w, sm_all, gx, dw, su)
         gxs = begin(exchange(dp, gx, gx_all, take(2)))
         dws = []
         for i in range(2):
             cols = pl.ds(i * halves_of, halves_of)
-            block = lambda ref, cols=cols: lambda i: ref.at[i, :, cols]
-            dws.append(begin(total(ex, block(dw), block(dw_all), take(4), take(4))))
+            part = Part(dw, slice(None), cols)
+            dws.append(begin(total(ex, part.__getitem__, Part(dw_all, slice(None), cols), take)))
         rows_of = lambda i: pl.ds(pl.multiple_of(i * 16, 16), 16)
-        sus = begin(total(ex, lambda i: su.at[rows_of(i)], lambda i: su_all.at[i], take(4), take(4)))
-        run(outs)
-        run(dos)
-        run(*dws, sus)
+        sus = begin(total(ex, lambda i: su.at[rows_of(i)], su_all, take))
+        run_behind((0, dos), (0, outs), (1, sus), (1, dws[0]), (6, dws[1]))
         run(gxs)
-        run(inrs)
-        run(gbs)
-        for copy in keeps:
-            copy.wait()
+        run(inrs, *gbs)
 
     row_block = (n_expert, slots * SLOT_ROWS, shard)
-    mixture, grad_x, d_o, d_w, sums, x_rows, og_rows, both_late, inner_all = call(
+    grad_hidden, mixture, grad_x, d_o, d_w, sums, x_rows, og_rows, both_all, inner_all = call(
         backward,
         "backward",
         [
+            ((tokens, width), F32),
             ((tokens, width), F32),
             ((ranks, tokens, shard), F32),
             ((n_expert,) + o_block, BF16),
@@ -1209,58 +1191,77 @@
             ((n_expert,) + s_block, BF16),
             ((ranks,) + row_block, BF16),
             ((ranks,) + row_block, BF16),
-            ((ranks, slots - early, rows, double), BF16),
+            ((ranks, slots, rows, double), BF16),
             ((ranks, slots, rows, hidden), BF16),
         ],
         (
-            grad_branch,
-            small,
-            att,
-            qkv,
-            o_weight,
+            hidden_rows,
+            norm_hidden,
+            scale_two,
+            probs,
             misc_all,
+            router,
+            out_grad,
+            gate_grad,
             cosine,
             sine,
-            x_cols,
             scale_one.reshape(ranks * tokens, 128),
             gains,
+            meta_group,
+            o_weight,
+            qkv,
+            att,
+            x_cols,
             weights,
-            out_part,
-            meta_group,
             og_all,
             norm_slices,
             og_slices,
             grad_both,
             inner,
+            out_part,
+            back_part,
         ),
         [
+            pltpu.VMEM(o_weight.shape, BF16),
+            pltpu.VMEM(qkv.shape, BF16),
+            pltpu.VMEM(att.shape, BF16),
+            pltpu.VMEM(x_cols.shape, BF16),
+            pltpu.VMEM(weights.shape, BF16),
+            dma((5,)),
+            pltpu.VMEM((n_expert, tokens, width), BF16),
+            pltpu.VMEM((n_expert, tokens, width), BF16),
+            dma((2,)),
+            pltpu.VMEM((n_expert, SLOT_STRIDE, tokens), F32),
+            pltpu.VMEM((ranks, used + 16, shard), BF16),
             pltpu.VMEM((ranks, tokens, width), BF16),
-            pltpu.VMEM((ranks, used + 8, shard), F32),
-            pltpu.VMEM((ranks, tokens, heads.cols), BF16),
+            pltpu.VMEM((ranks, used + 16, shard), BF16),
             pltpu.VMEM((ranks, ranks, tokens, heads.cols), BF16),
             pltpu.VMEM((n_expert,) + o_block, BF16),
             pltpu.VMEM((n_expert,) + w_block, BF16),
             pltpu.VMEM((sum_rows, shard), BF16),
             pltpu.VMEM((ranks, tokens, shard), F32),
-            pltpu.VMEM((2, n_expert, tokens, shard), BF16),
-            pltpu.VMEM((2, n_expert, tokens, shard), BF16),
-            dma((2, 2)),
-            dma((2,)),
+            pltpu.VMEM((deep, n_expert, tokens, shard), BF16),
+            pltpu.VMEM((deep, n_expert, tokens, shard), BF16),
+            pltpu.VMEM((deep,) + row_block, BF16),
+            pltpu.VMEM((deep,) + row_block, BF16),
+            dma((2, deep)),
+            dma((2, deep)),
         ]
+        + exchange_sems(n_expert)
+        + (line_sems(*plane[1:]) + sum_slots(*plane[1:], (tokens, width))) * 2
+        + line_sems(*group[1:]) * 3
+        + exchange_sems(ranks)
         + line_sems(*group[1:])
-        + exchange_sems(ranks)
-        + line_sems(*plane[1:])
-        + sum_slots(*plane[1:], (tokens, width))
-        + line_sems(*group[1:]) * 2
         + summed(o_block)
         + line_sems(*group[1:])
         + exchange_sems(ranks)
         + summed((part_rows, halves_of)) * 2
         + summed(s_block),
         cid=2,
-        us=125,
-        in_specs=[VMEM] * 14 + [ANY] * 5,
-        out_specs=[VMEM] * 7 + [ANY] * 2,
+        us=165,
+        in_specs=[VMEM] * 13 + [ANY] * 12,
+        out_specs=[VMEM] * 6 + [ANY] * 4,
+        input_output_aliases={21: 8, 22: 9},
     )
 
     held = pl.Buffered(deep)
@@ -1285,17 +1286,16 @@
         ((shard,), F32),
     ]
     d_up, d_down, output, grad_inputs, d_q, d_k, d_v, d_o, d_router, gain_one, gain_two = call(
-        functools.partial(finish, ranks, n_expert, slots, early, heads, tokens),
+        functools.partial(finish, ranks, n_expert, slots, heads, tokens),
         "finish",
         outs,
-        (x_rows, og_rows, both_all, both_late, inner_all) + ins,
+        (x_rows, og_rows, both_all, inner_all) + ins,
         us=15,
         grid=(slots,),
         in_specs=[
             pl.BlockSpec((ranks, n_expert, SLOT_ROWS, shard), lambda s: (0, 0, s, 0)),
             pl.BlockSpec((ranks, n_expert, SLOT_ROWS, shard), lambda s: (0, 0, s, 0)),
-            gathered((rows, double), lambda s: jnp.minimum(s, early - 1)),
-            gathered((rows, double), lambda s: jnp.maximum(s - early, 0)),
+            gathered((rows, double), lambda s: s),
             gathered((rows, hidden), lambda s: s),
         ]
         + [fixed(array.shape) for array in ins],

time: 398 us -> 351 us (0.88)
  Pallas kernels: 395 us -> 346 us
    pallas_call x4, Pallas kernels: 395 us -> 346 us  [call(): pl.pallas_call(body, out_shape=[jax.ShapeDtypeStruct(shape, dtype) for sh...]
where the time goes in v6:
time: 351 us; the launch traced here: 349 us
  Pallas kernels  346 us (99%)
    pallas_call x4, Pallas kernels, call(): pl.pallas_call(body, out_shape=[jax.ShapeDtypeStruct(shape, dtype) for sh...  346 us

profile of v6, /device:TPU:0, one launch (start us, length us, event | category | flops | bytes accessed | tf_op | source)
XLA Modules:
  0.0 349.2 jit_solution(17979779814519111839)
XLA Ops:
  0.6 0.7 stack.9
  1.3 0.7 stack.10
  2.0 0.6 maximum_convert_fusion.refs_5_.refs_11_
  2.6 64.3 %forward.1 = (bf16[4,384,640]{2,1,0:T(8,128)(2,1)}, f32[4,16,384]{2,1,0:T(8,128)}, bf16[8,4,128,384]{3,2,1,0:T(8,128)(2,1)}, bf16[4,128,640]{2,1,0:T(8,128)(2,1)...) custom-call(bf16[128,1536]{1,0:T(8,128)(2,1)} %x_ref.1, ...), custom_call_target="tpu_custom_call" | custom-call | bytes 210000000 | tf_op jit(solution)/shard_map/forward/pallas_call | solution.py:408
  67.0 81.7 %mixture_of_experts.1 = (f32[8,8,128]{2,1,0:T(8,128)}, f32[4,8,2,8,128]{4,3,2,1,0:T(8,128)}, bf16[8,128,1536]{2,1,0:T(8,128)(2,1)}, bf16[8,128,1536]{2,1,0:T(8,1...) custom-call(bf16[4,128,384]{2,1,0:T(8,128)(2,1)} %get-tuple-element., ...), custom_call_target="tpu_custom_call" | custom-call | bytes 240000000 | tf_op jit(solution)/shard_map/mixture_of_experts/pallas_call | solution.py:408
  148.7 180.5 %backward.1 = (f32[128,1536]{1,0:T(8,128)}, f32[128,1536]{1,0:T(8,128)}, f32[4,128,384]{2,1,0:T(8,128)}, bf16[8,48,1536]{2,1,0:T(8,128)(2,1)}, bf16[8,48,2560]{2...) custom-call(f32[128,1536]{1,0:T(8,128)} %get-tuple-element.53.refs_0, ...), custom_call_target="tpu_custom_call", output_to_operand_aliasing={{8}: (21, {}), {9}: (22, {})} | custom-call | bytes 495000000 | tf_op jit(solution)/shard_map/backward/pallas_call | solution.py:408
  329.2 19.8 %finish.1 = (f32[5,384,1024]{2,1,0:T(8,128)}, f32[5,512,384]{2,1,0:T(8,128)}, bf16[128,1536]{1,0:T(8,128)(2,1)}, f32[128,1536]{1,0:T(8,128)}, f32[384,1536]{1,0:...) custom-call(bf16[4,8,160,384]{3,2,1,0:T(8,128)(2,1)} %get-tuple-elem, ...), custom_call_target="tpu_custom_call" | custom-call | bytes 45000000 | tf_op jit(solution)/shard_map/finish/pallas_call | solution.py:408

commit v7 on v6

--- a/solution.py
+++ b/solution.py
@@ -30,14 +30,13 @@
 
 
 class Grid:
-    def __init__(self, axis, A, B, step_a=None, step_b=1):
+    def __init__(self, axis, A, B):
         self.axis, self.A, self.B = axis, A, B
-        self.step_a, self.step_b = B if step_a is None else step_a, step_b
         self.me = lax.axis_index(axis)
-        self.a, self.b = self.me // self.step_a % A, self.me // self.step_b % B
+        self.a, self.b = self.me // B, self.me % B
 
     def at(self, a, b):
-        return a * self.step_a + b * self.step_b
+        return a * self.B + b
 
     def dev(self, a, b):
         return {self.axis: self.at(a, b)}
@@ -159,7 +158,7 @@
     return [dma((2, A)), dma((2, A)), dma((2, A, B)), dma((2, A, B))]
 
 
-def gather(g, own, out, sems, arrived=lambda i, block: None):
+def gather(g, own, out, sems, arrived=lambda i, block: None, near_first=False, started=False):
     send_a, recv_a, send_b, recv_b = sems
     A, B = g.A, g.B
     row = lambda way, k: g.a - k if way == 0 else g.a + k
@@ -183,18 +182,34 @@
             def _():
                 do(remote(src, out.at[i], send_b.at[way, a, j], recv_b.at[way, a, j + 1], device))
 
+    def from_b(way, k, j):
+        for w in (0, 1):
+            i = g.at(row(way, k), col(w, j))
+
+            @pl.when(g.behind("a", way, k) & g.behind("b", w, j))
+            def _():
+                a = row(way, k)
+                remote(out.at[i], out.at[i], send_b.at[w, a, j], recv_b.at[w, a, j], g.here()).wait_recv()
+                along_b(w, j, a, i, out.at[i], start)
+                arrived(i, out.at[i])
+
     def start(copy):
         copy.start()
 
     def sent(copy):
         copy.wait_send()
 
-    for way in (0, 1):
-        along_a(way, 0, own, start)
-    for way in (0, 1):
-        along_b(way, 0, g.a, g.me, own, start)
-    arrived(g.me, own)
+    if not started:
+        for way in (0, 1):
+            along_a(way, 0, own, start)
+        for way in (0, 1):
+            along_b(way, 0, g.a, g.me, own, start)
+        arrived(g.me, own)
     yield
+    if near_first:
+        for j in range(1, B):
+            from_b(0, 0, j)
+        yield
     for k in range(1, A):
         for way in (0, 1):
             i = g.at(row(way, k), g.b)
@@ -209,17 +224,8 @@
 
             yield
     for j in range(1, B):
-        for way, k in rows:
-            for w in (0, 1):
-                i = g.at(row(way, k), col(w, j))
-
-                @pl.when(g.behind("a", way, k) & g.behind("b", w, j))
-                def _():
-                    a = row(way, k)
-                    remote(out.at[i], out.at[i], send_b.at[w, a, j], recv_b.at[w, a, j], g.here()).wait_recv()
-                    along_b(w, j, a, i, out.at[i], start)
-                    arrived(i, out.at[i])
-
+        for way, k in rows[1:] if near_first else rows:
+            from_b(way, k, j)
             yield
     for way, k in rows:
         for w in (0, 1) if k == 0 else (way,):
@@ -246,7 +252,12 @@
     ]
 
 
-def reduce(g, part, finish, sems, slots, sent=None):
+def across(g, part, sems, slots, a, r):
+    to = (g.b + r) % g.B
+    return remote(part(g.at(a, to)), slots[2].at[a, r - 1], sems[2].at[0, a, r], sems[3].at[0, a, r], g.dev(g.a, to))
+
+
+def reduce(g, part, finish, sems, slots, sent=None, started=False):
     send_a, recv_a, send_b, recv_b = sems
     land_a, out_a, land_b = slots
     sent = sent or part
@@ -255,10 +266,6 @@
     rows = [(way, k) for k in range(A - 1, 0, -1) for way in (0, 1)] + [(0, 0)]
     here = g.here()
 
-    def across(a, r):
-        to = (g.b + r) % B
-        return remote(sent(g.at(a, to)), land_b.at[a, r - 1], send_b.at[0, a, r], recv_b.at[0, a, r], g.dev(g.a, to))
-
     def landing(way, k):
         return land_a.at[A if k == 0 and way == 1 else row(way, k)]
 
@@ -271,12 +278,12 @@
     def landed(way, k):
         remote(landing(way, k), landing(way, k), send_a.at[way, k], recv_a.at[way, k], here).wait_recv()
 
-    for way, k in rows:
+    for way, k in [] if started else rows:
 
         @pl.when(g.ahead("a", way, k))
         def _():
             for r in range(1, B):
-                across(row(way, k), r).start()
+                across(g, sent, sems, slots, row(way, k), r).start()
 
     yield
     for way, k in rows:
@@ -330,7 +337,7 @@
         @pl.when(g.ahead("a", way, k))
         def _():
             for r in range(1, B):
-                across(row(way, k), r).wait_send()
+                across(g, sent, sems, slots, row(way, k), r).wait_send()
             if k > 0:
                 along(way, k).wait_send()
 
@@ -508,30 +515,23 @@
     return jnp.concatenate([misc_ref[i, which : which + 1, :] for i in range(ranks)], axis=1)
 
 
-def attention_forward(ranks, heads, length, x_ref, w_ref, o_ref, misc_ref, cos_ref, sin_ref, part_ref, qkv_ref, att_ref, scale_ref):
+def attention_forward(ranks, heads, length, b, x_ref, w_ref, o_ref, misc_ref, cos_ref, sin_ref, part_ref, qkv_ref, att_ref, scale_ref):
     width = x_ref.shape[2]
-    gain = gain_row(misc_ref, ranks, 0)
-    weights = w_ref[...].reshape(width, heads.cols)
-
-    def one(b, carry):
-        x = x_ref[b].astype(F32)
-        scale = norm_scale(x)
-        scale_ref[b] = jnp.broadcast_to(scale, (length, 128))
-        normed = (x * scale * gain).astype(BF16)
-        qkv_ref[b] = rotary(dot(normed, weights), cos_ref[...], sin_ref[...]).astype(BF16)
-        qkv = qkv_ref[b]
-        allowed = allowed_pairs(misc_ref[b, 8:9, :length])
-        allowed = jnp.concatenate([allowed] * heads.group, axis=0)
-        outs = []
-        for kv in range(heads.kv):
-            probs = attention_weights(heads.stack(qkv, kv), heads.key(qkv, kv), allowed).astype(BF16)
-            mixed = dot(probs, heads.value(qkv, kv)).astype(BF16)
-            outs += [mixed[i * length : (i + 1) * length] for i in range(heads.group)]
-        att_ref[b] = jnp.concatenate(outs, axis=1)
-        part_ref[b] = dot(att_ref[b], o_ref[...]).astype(BF16)
-        return carry
-
-    lax.fori_loop(0, ranks, one, 0)
+    x = x_ref[b].astype(F32)
+    scale = norm_scale(x)
+    scale_ref[b] = jnp.broadcast_to(scale, (length, 128))
+    normed = (x * scale * gain_row(misc_ref, ranks, 0)).astype(BF16)
+    qkv_ref[b] = rotary(dot(normed, w_ref[...].reshape(width, heads.cols)), cos_ref[...], sin_ref[...]).astype(BF16)
+    qkv = qkv_ref[b]
+    allowed = allowed_pairs(misc_ref[b, 8:9, :length])
+    allowed = jnp.concatenate([allowed] * heads.group, axis=0)
+    outs = []
+    for kv in range(heads.kv):
+        probs = attention_weights(heads.stack(qkv, kv), heads.key(qkv, kv), allowed).astype(BF16)
+        mixed = dot(probs, heads.value(qkv, kv)).astype(BF16)
+        outs += [mixed[i * length : (i + 1) * length] for i in range(heads.group)]
+    att_ref[b] = jnp.concatenate(outs, axis=1)
+    part_ref[b] = dot(att_ref[b], o_ref[...]).astype(BF16)
 
 
 def column_experts(n_expert, slots, axis):
@@ -696,45 +696,48 @@
         ref[i, :, cols] = values[i * rows : (i + 1) * rows]
 
 
-def attention_backward(ranks, heads, length, branch_ref, att_ref, qkv_ref, o_ref, misc_ref, cos_ref, sin_ref, grad_ref, d_o_ref):
-    d_o = dot(att_ref[...].reshape(ranks * length, heads.q_cols), branch_ref[...].reshape(ranks * length, -1), ((0,), (0,)))
-    store_blocks(d_o_ref, slice(None), d_o.astype(BF16))
-
-    def one(b, carry):
-        grad_att = dot(branch_ref[b], o_ref[...], ((1,), (1,))).astype(BF16)
-        att, qkv = att_ref[b], qkv_ref[b]
-        allowed = allowed_pairs(misc_ref[b, 8:9, :length])
-        allowed = jnp.concatenate([allowed] * heads.group, axis=0)
-        d_q, d_k, d_v = [], [], []
-        for kv in range(heads.kv):
-            queries, keys = heads.stack(qkv, kv), heads.key(qkv, kv)
-            soft = attention_weights(queries, keys, allowed)
-            grads = heads.stack(grad_att, kv)
-            d_v.append(dot(soft.astype(BF16), grads, ((0,), (0,))))
-            delta = jnp.sum(grads.astype(F32) * heads.stack(att, kv).astype(F32), axis=1, keepdims=True)
-            inner = dot(grads, heads.value(qkv, kv), ((1,), (1,)))
-            d_scores = (soft * (inner - delta) * SCORE_SCALE).astype(BF16)
-            rows = dot(d_scores, keys)
-            d_q += [rows[i * length : (i + 1) * length] for i in range(heads.group)]
-            d_k.append(dot(d_scores, queries, ((0,), (0,))))
-        spare = heads.cols - heads.q_cols - 2 * heads.kv_cols
-        fill = [jnp.zeros((length, spare), F32)] if spare else []
-        grads = jnp.concatenate(d_q + d_k + d_v + fill, axis=1)
-        grad_ref[b] = rotary(grads, cos_ref[...], sin_ref[...], back=True).astype(BF16)
-        return carry
-
-    lax.fori_loop(0, ranks, one, 0)
-
-
-def projection_backward(ranks, heads, shard, x_ref, scale_ref, gain_ref, grad_ref, w_ref, small_ref, grad_x_ref, d_w_ref, sums_ref):
+def attention_backward(heads, length, b, branch_ref, att_ref, qkv_ref, o_ref, misc_ref, cos_ref, sin_ref, grad_ref):
+    grad_att = dot(branch_ref[b], o_ref[...], ((1,), (1,))).astype(BF16)
+    att, qkv = att_ref[b], qkv_ref[b]
+    allowed = allowed_pairs(misc_ref[b, 8:9, :length])
+    allowed = jnp.concatenate([allowed] * heads.group, axis=0)
+    d_q, d_k, d_v = [], [], []
+    for kv in range(heads.kv):
+        queries, keys = heads.stack(qkv, kv), heads.key(qkv, kv)
+        soft = attention_weights(queries, keys, allowed)
+        grads = heads.stack(grad_att, kv)
+        d_v.append(dot(soft.astype(BF16), grads, ((0,), (0,))))
+        delta = jnp.sum(grads.astype(F32) * heads.stack(att, kv).astype(F32), axis=1, keepdims=True)
+        inner = dot(grads, heads.value(qkv, kv), ((1,), (1,)))
+        d_scores = (soft * (inner - delta) * SCORE_SCALE).astype(BF16)
+        rows = dot(d_scores, keys)
+        d_q += [rows[i * length : (i + 1) * length] for i in range(heads.group)]
+        d_k.append(dot(d_scores, queries, ((0,), (0,))))
+    spare = heads.cols - heads.q_cols - 2 * heads.kv_cols
+    fill = [jnp.zeros((length, spare), F32)] if spare else []
+    grads = jnp.concatenate(d_q + d_k + d_v + fill, axis=1)
+    grad_ref[b] = rotary(grads, cos_ref[...], sin_ref[...], back=True).astype(BF16)
+
+
+def output_weight_backward(heads, branch_ref, att_ref, d_o_ref):
+    branch = branch_ref[...].reshape(-1, branch_ref.shape[-1])
+    store_blocks(d_o_ref, slice(None), dot(att_ref[...].reshape(-1, heads.q_cols), branch, ((0,), (0,))).astype(BF16))
+
+
+def projection_products(ranks, heads, x_ref, scale_ref, gain_ref, grad_ref, d_w_ref, done):
+    norm_input = (x_ref[...].astype(F32) * scale_ref[:, 0:1] * gain_ref[0:1, :]).astype(BF16)
+    for i in range(ranks):
+        grads = grad_ref[i].reshape(-1, heads.cols)
+        store_blocks(d_w_ref, slice(i * heads.cols, (i + 1) * heads.cols), dot(norm_input, grads, ((0,), (0,))).astype(BF16))
+        done(i)
+
+
+def projection_backward(ranks, heads, shard, x_ref, scale_ref, grad_ref, w_ref, small_ref, grad_x_ref, sums_ref):
     normed = x_ref[...].astype(F32) * scale_ref[:, 0:1]
-    norm_input = (normed * gain_ref[0:1, :]).astype(BF16)
     total = None
     for i in range(ranks):
-        grads = grad_ref[i].reshape(-1, heads.cols)
-        term = dot(grads, w_ref[i], ((1,), (1,)))
+        term = dot(grad_ref[i].reshape(-1, heads.cols), w_ref[i], ((1,), (1,)))
         total = term if total is None else total + term
-        store_blocks(d_w_ref, slice(i * heads.cols, (i + 1) * heads.cols), dot(norm_input, grads, ((0,), (0,))).astype(BF16))
     grad_x_ref[...] = total.reshape(grad_x_ref.shape)
     small = small_ref[0].astype(F32)
     for i in range(1, ranks):
@@ -857,12 +860,31 @@
 
         advance(ogs, 2 * (plane[1] - 1))
         run(ws)
-        attention_forward(ranks, heads, tokens, x_all, w_all, wo, ms_all, cs, sn, part, qkv, att, scale_one)
 
         def store(total):
             branch[...] = total
 
-        run(reduce(dp, lambda i: part.at[i], store, take(4), take(3)))
+        dp_sems, dp_slots = take(4), take(3)
+        sums = begin(reduce(dp, lambda i: part.at[i], store, dp_sems, dp_slots, started=True))
+
+        def one(t, carry):
+            a, r = (dp.a + 1 + t // 2) % dp.A, 1 + t % 2
+
+            @pl.when(t == 2 * (dp.A - 1))
+            def _():
+                advance(sums, 2 * (dp.A - 1))
+
+            b = dp.at(a, (dp.b + r) % 2)
+            attention_forward(ranks, heads, tokens, b, x_all, w_all, wo, ms_all, cs, sn, part, qkv, att, scale_one)
+
+            @pl.when(r < 2)
+            def _():
+                across(dp, lambda i: part.at[i], dp_sems, dp_slots, a, 1).start()
+
+            return carry
+
+        lax.fori_loop(0, ranks, one, 0)
+        run(sums)
         route_forward(ranks, n_expert, slots, x, branch, ms_all, rt_all, routes_ref, blocks_ref, hidden_ref, norm, scale_two, probs, meta, table)
         run(ogs)
         keep.wait()
@@ -930,7 +952,7 @@
         + line_sems(*group[1:])
         + sum_slots(*group[1:], (tokens, width)),
         cid=0,
-        us=70,
+        us=60,
         in_specs=[VMEM] * 12 + [pl.BlockSpec(memory_space=pltpu.SMEM)],
         out_specs=[VMEM] * 2 + [ANY] + [VMEM] * 10,
     )
@@ -1022,9 +1044,9 @@
         out_ring.end(n_expert)
         back_ring.end(n_expert)
         end(range(n_expert), nh)
-        og_end(range(n_expert), og.at[0])
         for i in range(n_expert):
             keep(i, nh).wait()
+        og_end(range(n_expert), og.at[0])
 
     gate_grad, meta_group, out_part, back_part, inner, grad_both, norm_slices, og_slices = call(
         mixture_of_experts,
@@ -1063,7 +1085,7 @@
         + line_sems(*plane[1:])
         + line_sems(*group[1:]),
         cid=1,
-        us=80,
+        us=75,
         in_specs=[VMEM] * 2 + [ANY] * 3,
         out_specs=[VMEM] * 2 + [ANY] * 6,
     )
@@ -1072,7 +1094,7 @@
     part_rows = shard // n_expert
     o_block, w_block, s_block = (part_rows, width), (part_rows, ranks * heads.cols), (16, shard)
 
-    halves_of = ranks * heads.cols // 2
+    half = ranks * heads.cols // 2
     summed = lambda block: total_scratch(*plane[1:], block)
 
     lead = max(slots // 5, 1)
@@ -1104,15 +1126,15 @@
             fetch(j, lambda copy: copy.start())
         greet(dp.all() + ex.all())
 
-        def store(to):
-            def finish_(value):
+        def token_sum(to, kept, sent):
+            def store(value):
                 to[...] = value
 
-            return finish_
+            return begin(reduce(ex, lambda i: kept.at[i], store, take(4), take(3), lambda i: sent.at[i]))
 
         ggs = begin(exchange(ex, gg, gg_all, take(2)))
-        backs = begin(reduce(ex, lambda i: back_in.at[i], store(grad_hidden_ref), take(4), take(3), lambda i: back_terms.at[i]))
-        outs = begin(reduce(ex, lambda i: out_in.at[i], store(mix), take(4), take(3), lambda i: terms.at[i]))
+        backs = token_sum(grad_hidden_ref, back_in, back_terms)
+        outs = token_sum(mix, out_in, terms)
         inrs = begin(gather(dp, inr_all.at[dp.me], inr_all, take(4)))
         share = lambda start, count: begin(
             gather(dp, gb_all.at[dp.me, pl.ds(start, count)], Part(gb_all, pl.ds(start, count)), take(4))
@@ -1150,31 +1172,52 @@
         run(backs)
         run(ggs)
         route_backward(ranks, n_expert, shard, hid, nh, sc2, pb, ms, tb, og_mine, grad_hidden_ref, gg_all, grad_hidden_ref, br_all.at[dp.me], sm)
-        brs = begin(gather(dp, br_all.at[dp.me], br_all, take(4)))
+        brs = begin(gather(dp, br_all.at[dp.me], br_all, take(4), near_first=True))
         sms = begin(exchange(dp, sm, sm_all, take(2)))
         for copy in brings:
             copy.wait()
         advance(outs, 2)
-        run(brs)
-        advance(outs, 2)
-        attention_backward(ranks, heads, tokens, br_all, at, qkv, wo, ms, cs, sn, gr_all.at[dp.me], do)
-        grs = begin(gather(dp, gr_all.at[dp.me], gr_all, take(4)))
+        gr_sems = take(4)
+        share_gr = lambda p, started: gather(
+            dp, gr_all.at[dp.me, p], Part(gr_all, p), [sems.at[p] for sems in gr_sems], started=started
+        )
+
+        def one(t, carry):
+            @pl.when(t == 1)
+            def _():
+                advance(brs, 1)
+
+            @pl.when(t == 2)
+            def _():
+                run(brs)
+
+            p = dp.at((dp.a + t // 2) % dp.A, (dp.b + t % 2) % 2)
+            attention_backward(heads, tokens, p, br_all, at, qkv, wo, ms, cs, sn, gr_all.at[dp.me])
+            begin(share_gr(p, False))
+            return carry
+
+        lax.fori_loop(0, ranks, one, 0)
+        output_weight_backward(heads, br_all, at, do)
         dos = begin(total(ex, lambda i: do.at[i], do_all, take))
         advance(outs, 2)
         run(sms)
-        advance(dos, 2 * plane[1])
-        run(grs)
+        advance(dos, 2)
+        run(*[share_gr(p, True) for p in range(ranks)])
         gbs.append(share(lead, slots - lead))
-        projection_backward(ranks, heads, shard, xc, sc, gn, gr_all, w, sm_all, gx, dw, su)
+        dws = []
+
+        def done(i):
+            if (i + 1) % (ranks // 2) == 0:
+                cols = pl.ds(len(dws) * half, half)
+                part = Part(dw, slice(None), cols)
+                dws.append(begin(total(ex, part.__getitem__, Part(dw_all, slice(None), cols), take)))
+
+        projection_products(ranks, heads, xc, sc, gn, gr_all, dw, done)
+        projection_backward(ranks, heads, shard, xc, sc, gr_all, w, sm_all, gx, su)
         gxs = begin(exchange(dp, gx, gx_all, take(2)))
-        dws = []
-        for i in range(2):
-            cols = pl.ds(i * halves_of, halves_of)
-            part = Part(dw, slice(None), cols)
-            dws.append(begin(total(ex, part.__getitem__, Part(dw_all, slice(None), cols), take)))
         rows_of = lambda i: pl.ds(pl.multiple_of(i * 16, 16), 16)
         sus = begin(total(ex, lambda i: su.at[rows_of(i)], su_all, take))
-        run_behind((0, dos), (0, outs), (1, sus), (1, dws[0]), (6, dws[1]))
+        run_behind((0, dos), (0, outs), (0, dws[0]), (2, sus), (5, dws[1]))
         run(gxs)
         run(inrs, *gbs)
 
@@ -1251,11 +1294,11 @@
         + (line_sems(*plane[1:]) + sum_slots(*plane[1:], (tokens, width))) * 2
         + line_sems(*group[1:]) * 3
         + exchange_sems(ranks)
-        + line_sems(*group[1:])
+        + [dma((ranks,) + sems.shape) for sems in line_sems(*group[1:])]
         + summed(o_block)
         + line_sems(*group[1:])
+        + summed((part_rows, half)) * 2
         + exchange_sems(ranks)
-        + summed((part_rows, halves_of)) * 2
         + summed(s_block),
         cid=2,
         us=165,

time: 351 us -> 330 us (0.940)
  Pallas kernels: 346 us -> 327 us
    pallas_call x4, Pallas kernels: 346 us -> 327 us  [call(): pl.pallas_call(body, out_shape=[jax.ShapeDtypeStruct(shape, dtype) for sh...]
where the time goes in v7:
time: 330 us
  Pallas kernels  327 us (99%)
    pallas_call x4, Pallas kernels, call(): pl.pallas_call(body, out_shape=[jax.ShapeDtypeStruct(shape, dtype) for sh...  327 us

profile of v7, /device:TPU:0, one launch (start us, length us, event | category | flops | bytes accessed | tf_op | source)
XLA Modules:
  0.0 330.1 jit_solution(12153115811863084807)
XLA Ops:
  0.6 0.7 stack.9
  1.3 0.7 stack.10
  2.0 0.6 maximum_convert_fusion.refs_5_.refs_11_
  2.6 60.4 %forward.1 = (bf16[4,384,640]{2,1,0:T(8,128)(2,1)}, f32[4,16,384]{2,1,0:T(8,128)}, bf16[8,4,128,384]{3,2,1,0:T(8,128)(2,1)}, bf16[4,128,640]{2,1,0:T(8,128)(2,1)...) custom-call(bf16[128,1536]{1,0:T(8,128)(2,1)} %x_ref.1, ...), custom_call_target="tpu_custom_call" | custom-call | bytes 180000000 | tf_op jit(solution)/shard_map/forward/pallas_call | solution.py:415
  63.0 80.8 %mixture_of_experts.1 = (f32[8,8,128]{2,1,0:T(8,128)}, f32[4,8,2,8,128]{4,3,2,1,0:T(8,128)}, bf16[8,128,1536]{2,1,0:T(8,128)(2,1)}, bf16[8,128,1536]{2,1,0:T(8,1...) custom-call(bf16[4,128,384]{2,1,0:T(8,128)(2,1)} %get-tuple-element., ...), custom_call_target="tpu_custom_call" | custom-call | bytes 225000000 | tf_op jit(solution)/shard_map/mixture_of_experts/pallas_call | solution.py:415
  143.9 166.2 %backward.1 = (f32[128,1536]{1,0:T(8,128)}, f32[128,1536]{1,0:T(8,128)}, f32[4,128,384]{2,1,0:T(8,128)}, bf16[8,48,1536]{2,1,0:T(8,128)(2,1)}, bf16[8,48,2560]{2...) custom-call(f32[128,1536]{1,0:T(8,128)} %get-tuple-element.53.refs_0, ...), custom_call_target="tpu_custom_call", output_to_operand_aliasing={{8}: (21, {}), {9}: (22, {})} | custom-call | bytes 495000000 | tf_op jit(solution)/shard_map/backward/pallas_call | solution.py:415
  310.1 19.8 %finish.1 = (f32[5,384,1024]{2,1,0:T(8,128)}, f32[5,512,384]{2,1,0:T(8,128)}, bf16[128,1536]{1,0:T(8,128)(2,1)}, f32[128,1536]{1,0:T(8,128)}, f32[384,1536]{1,0:...) custom-call(bf16[4,8,160,384]{3,2,1,0:T(8,128)(2,1)} %get-tuple-elem, ...), custom_call_target="tpu_custom_call" | custom-call | bytes 45000000 | tf_op jit(solution)/shard_map/finish/pallas_call | solution.py:415

commit v8 on v7

--- a/solution.py
+++ b/solution.py
@@ -600,15 +600,16 @@
     )
 
 
-def pick_rows(slots, n_expert, mine, meta_ref, block, to_sc):
-    def one(q, carry):
+def pick_rows(slots, count, sequence, mine, meta_ref, block, to_sc):
+    def one(t, carry):
+        q = sequence(t)
         pick = row_picks(slots, meta_ref[q, 0, mine, :]).astype(BF16)
         ranks, _, shard = block(q).shape
         for i in range(ranks):
             to_sc[q, :, i * shard : (i + 1) * shard] = dot(pick, block(q)[i]).astype(BF16)
         return carry
 
-    lax.fori_loop(0, n_expert, one, 0)
+    lax.fori_loop(0, count, one, 0)
 
 
 def expert_slot(n_expert, tokens, s, mine, meta_ref, up_ref, down_ref, gate_grad_ref, inner_ring, both_ring, x_sc, og_sc):
@@ -762,11 +763,26 @@
     lax.fori_loop(0, n_expert, one, 0)
 
 
-def finish(ranks, n_expert, slots, heads, tokens, x_rows_ref, og_rows_ref, both_ref, inner_ref, grad_ref, x_ref, misc_ref, grad_hidden_ref, hidden_ref, mixture_ref, d_w_ref, d_o_ref, sums_ref, d_up_ref, d_down_ref, output_ref, grad_inputs_ref, q_ref, k_ref, v_ref, o_ref, router_ref, gain_one_ref, gain_two_ref):
+def finish(ranks, n_expert, slots, heads, x_rows_ref, og_rows_ref, both_ref, inner_ref, *refs):
     step = pl.program_id(0)
+    take = taker(refs)
+    sources, d_up_ref, d_down_ref, targets = take(9), take(), take(), take(6)
+    router_ref, gain_one_ref, gain_two_ref = take(3)
+    places, stages, in_sems, out_sems = take(9), take(6), take(), take()
+    grad_ref, x_ref, misc_ref, grad_hidden_ref, hidden_ref, mixture_ref, d_w_ref, d_o_ref, sums_ref = places
+    output_ref, grad_inputs_ref, q_ref, k_ref, v_ref, o_ref = stages
+    ins = [pltpu.make_async_copy(*pair, in_sems.at[i]) for i, pair in enumerate(zip(sources, places))]
+    outs = [pltpu.make_async_copy(*pair, out_sems.at[i]) for i, pair in enumerate(zip(stages, targets))]
 
     @pl.when(step == 0)
     def _():
+        for copy in ins:
+            copy.start()
+
+    @pl.when(step == min(1, slots - 1))
+    def _():
+        for copy in ins:
+            copy.wait()
         output_ref[...] = (hidden_ref[...] + RESIDUAL_SCALE * mixture_ref[...]).astype(BF16)
         gain = gain_row(misc_ref, ranks, 0)
         grad = jnp.concatenate([grad_ref[i] for i in range(ranks)], axis=1)
@@ -786,11 +802,18 @@
             here = slice(i * heads.kv_cols, (i + 1) * heads.kv_cols)
             k_ref[:, here] = d_w_ref[:, start + first : start + second].astype(F32)
             v_ref[:, here] = d_w_ref[:, start + second : start + second + heads.kv_cols].astype(F32)
+        for copy in outs:
+            copy.start()
 
     flat = lambda value: value.reshape(-1, value.shape[-1])
     over = ((0,), (0,))
     d_up_ref[0] = dot(flat(x_rows_ref[...]), flat(both_ref[...]), over)
     d_down_ref[0] = dot(flat(inner_ref[...]), flat(og_rows_ref[...]), over)
+
+    @pl.when(step == slots - 1)
+    def _():
+        for copy in outs:
+            copy.wait()
 
 
 def on_device(
@@ -820,12 +843,11 @@
     used = n_expert * SLOT_STRIDE
     cosine, sine = rope_tables(tokens, heads)
 
-    gains = jnp.stack([norm1_gain, norm2_gain]).astype(F32)
     dma = pltpu.SemaphoreType.DMA
 
     def forward(*refs):
         take = taker(refs)
-        x, wq, wk, wv, rt, gn, sg, og, wo, cs, sn, routes_ref, blocks_ref = take(13)
+        x, wq, wk, wv, rt, gain_one, gain_two, sg, og, wo, cs, sn, routes_ref, blocks_ref = take(14)
         w, ms_all, og_all, qkv, att, scale_one, xc, hidden_ref, norm, scale_two, probs, meta, table = take(13)
         x_all, w_all, rt_all, ms, og_own, part, branch, own_sem = take(8)
         dp, ex = Grid(*group), Grid(*plane)
@@ -838,7 +860,8 @@
                 w[i, :, at:] = jnp.zeros((shard, heads.cols - at), BF16)
             og_own[i] = og[:, i * shard : (i + 1) * shard]
         ms[...] = jnp.zeros_like(ms)
-        ms[0:2, :] = gn[...]
+        ms[0, :] = gain_one[...].astype(F32)
+        ms[1, :] = gain_two[...].astype(F32)
         ms[8:9, :tokens] = sg[...].astype(F32)
         x_all[dp.me] = x[...]
         rt_all[dp.me] = rt[...]
@@ -927,7 +950,8 @@
             k_weight,
             value_matrix,
             router_weight.T,
-            gains,
+            norm1_gain,
+            norm2_gain,
             segment_ids,
             out_grad,
             o_weight,
@@ -953,7 +977,7 @@
         + sum_slots(*group[1:], (tokens, width)),
         cid=0,
         us=60,
-        in_specs=[VMEM] * 12 + [pl.BlockSpec(memory_space=pltpu.SMEM)],
+        in_specs=[VMEM] * 13 + [pl.BlockSpec(memory_space=pltpu.SMEM)],
         out_specs=[VMEM] * 2 + [ANY] + [VMEM] * 10,
     )
 
@@ -1021,8 +1045,14 @@
         mt_own[...] = mt_all[:, :, mine, :]
         mt_group[dp.me] = mt_own[...]
         mgs = begin(gather(dp, mt_own, mt_group, take(4)))
+        advance(nhs, 2 * (ex.A - 1))
+        block = lambda q: nh_all.at[q]
+        pick_rows(slots, ex.A, lambda t: ex.at(t, ex.b), mine, mt_all, block, x_sc)
         run(nhs)
-        pick_rows(slots, n_expert, mine, mt_all, lambda q: nh_all.at[q], x_sc)
+        others = ex.B - 1
+        pick_rows(
+            slots, ex.A * others, lambda t: ex.at(t // others, (ex.b + 1 + t % others) % ex.B), mine, mt_all, block, x_sc
+        )
 
         def one(s, carry):
             fetch(s, lambda copy: copy.wait())
@@ -1101,7 +1131,7 @@
 
     def backward(*refs):
         take = taker(refs)
-        hid, nh, sc2, pb, ms, tb, og_mine, gg, cs, sn, sc, gn, mt = take(13)
+        hid, nh, sc2, pb, ms, tb, og_mine, gg, cs, sn, sc, mt = take(12)
         brought, (og, xd, ogd, _, _, terms, back_terms) = take(5), take(7)
         grad_hidden_ref, mix, gx_all, do_all, dw_all, su_all, x_rows, og_rows, gb_all, inr_all = take(10)
         places, bring_sems = take(5), take()
@@ -1199,7 +1229,7 @@
         lax.fori_loop(0, ranks, one, 0)
         output_weight_backward(heads, br_all, at, do)
         dos = begin(total(ex, lambda i: do.at[i], do_all, take))
-        advance(outs, 2)
+        advance(outs, 4)
         run(sms)
         advance(dos, 2)
         run(*[share_gr(p, True) for p in range(ranks)])
@@ -1212,7 +1242,7 @@
                 part = Part(dw, slice(None), cols)
                 dws.append(begin(total(ex, part.__getitem__, Part(dw_all, slice(None), cols), take)))
 
-        projection_products(ranks, heads, xc, sc, gn, gr_all, dw, done)
+        projection_products(ranks, heads, xc, sc, ms.at[dp.me], gr_all, dw, done)
         projection_backward(ranks, heads, shard, xc, sc, gr_all, w, sm_all, gx, su)
         gxs = begin(exchange(dp, gx, gx_all, take(2)))
         rows_of = lambda i: pl.ds(pl.multiple_of(i * 16, 16), 16)
@@ -1249,7 +1279,6 @@
             cosine,
             sine,
             scale_one.reshape(ranks * tokens, 128),
-            gains,
             meta_group,
             o_weight,
             qkv,
@@ -1302,9 +1331,9 @@
         + summed(s_block),
         cid=2,
         us=165,
-        in_specs=[VMEM] * 13 + [ANY] * 12,
+        in_specs=[VMEM] * 12 + [ANY] * 12,
         out_specs=[VMEM] * 6 + [ANY] * 4,
-        input_output_aliases={21: 8, 22: 9},
+        input_output_aliases={20: 8, 21: 9},
     )
 
     held = pl.Buffered(deep)
@@ -1329,10 +1358,13 @@
         ((shard,), F32),
     ]
     d_up, d_down, output, grad_inputs, d_q, d_k, d_v, d_o, d_router, gain_one, gain_two = call(
-        functools.partial(finish, ranks, n_expert, slots, heads, tokens),
+        functools.partial(finish, ranks, n_expert, slots, heads),
         "finish",
         outs,
         (x_rows, og_rows, both_all, inner_all) + ins,
+        [pltpu.VMEM(array.shape, array.dtype) for array in ins]
+        + [pltpu.VMEM(*out) for out in outs[2:8]]
+        + [dma((9,)), dma((6,))],
         us=15,
         grid=(slots,),
         in_specs=[
@@ -1341,8 +1373,10 @@
             gathered((rows, double), lambda s: s),
             gathered((rows, hidden), lambda s: s),
         ]
-        + [fixed(array.shape) for array in ins],
-        out_specs=[moving((shard, double)), moving((hidden, shard))] + [fixed(shape) for shape, _ in outs[2:]],
+        + [ANY] * 9,
+        out_specs=[moving((shard, double)), moving((hidden, shard))]
+        + [ANY] * 6
+        + [fixed(shape) for shape, _ in outs[8:]],
     )
     return (
         output,

time: 330 us -> 326 us (0.988)
  no operation moved by 1% of the time
where the time goes in v8:
time: 326 us
  Pallas kernels  325 us (100%)
    pallas_call x4, Pallas kernels, call(): pl.pallas_call(body, out_shape=[jax.ShapeDtypeStruct(shape, dtype) for sh...  325 us

profile of v8, /device:TPU:0, one launch (start us, length us, event | category | flops | bytes accessed | tf_op | source)
XLA Modules:
  0.0 325.6 jit_solution(3138575742158025212)
XLA Ops:
  0.6 60.4 %forward.1 = (bf16[4,384,640]{2,1,0:T(8,128)(2,1)}, f32[4,16,384]{2,1,0:T(8,128)}, bf16[8,4,128,384]{3,2,1,0:T(8,128)(2,1)}, bf16[4,128,640]{2,1,0:T(8,128)(2,1)...) custom-call(bf16[128,1536]{1,0:T(8,128)(2,1)} %refs_1_.3, ...), custom_call_target="tpu_custom_call" | custom-call | bytes 180000000 | tf_op jit(solution)/shard_map/forward/pallas_call | solution.py:415
  61.1 79.6 %mixture_of_experts.1 = (f32[8,8,128]{2,1,0:T(8,128)}, f32[4,8,2,8,128]{4,3,2,1,0:T(8,128)}, bf16[8,128,1536]{2,1,0:T(8,128)(2,1)}, bf16[8,128,1536]{2,1,0:T(8,1...) custom-call(bf16[4,128,384]{2,1,0:T(8,128)(2,1)} %get-tuple-element., ...), custom_call_target="tpu_custom_call" | custom-call | bytes 225000000 | tf_op jit(solution)/shard_map/mixture_of_experts/pallas_call | solution.py:415
  140.7 166.4 %backward.1 = (f32[128,1536]{1,0:T(8,128)}, f32[128,1536]{1,0:T(8,128)}, f32[4,128,384]{2,1,0:T(8,128)}, bf16[8,48,1536]{2,1,0:T(8,128)(2,1)}, bf16[8,48,2560]{2...) custom-call(f32[128,1536]{1,0:T(8,128)} %get-tuple-element.53.refs_0, ...), custom_call_target="tpu_custom_call", output_to_operand_aliasing={{8}: (20, {}), {9}: (21, {})} | custom-call | bytes 495000000 | tf_op jit(solution)/shard_map/backward/pallas_call | solution.py:415
  307.1 18.3 %finish.1 = (f32[5,384,1024]{2,1,0:T(8,128)}, f32[5,512,384]{2,1,0:T(8,128)}, bf16[128,1536]{1,0:T(8,128)(2,1)}, f32[128,1536]{1,0:T(8,128)}, f32[384,1536]{1,0:...) custom-call(bf16[4,8,160,384]{3,2,1,0:T(8,128)(2,1)} %get-tuple-elem, ...), custom_call_target="tpu_custom_call" | custom-call | bytes 45000000 | tf_op jit(solution)/shard_map/finish/pallas_call | solution.py:415
